TPU v7x, 32 devices: a whole 2x2x4 slice. The times are simulated.
32 devices in a mesh: row: 4 (over x, core), col: 8 (over z, y).
Axes of the slice: x: 2, y: 2, z: 4, core: 2. Of those that a mesh axis runs over, the one named last changes fastest.
Arguments:
- moment_x: float32 [496, 496], P('row', 'col'), may hold values from -8 to 8
- zinv: float32 [496, 496], P('row', 'col'), may hold values from -8 to 8
- positions: int32 [1024, 16], P(('row', 'col')), may hold values from 0 to 495
- entry_count: int32 [1024], P(('row', 'col')), may hold values from 1 to 8
Outputs:
- schur: float32 [1024, 1024], P('row', 'col')
All inputs are finite; a program needn't handle non-finite values.
Results may differ from a plain program's by a relative error of at most 0.0003.
Values sent between devices are 32-bit elements; how exact they have to be, the bound alone decides.
No kernel may reach another device: no remote copies, remote signals or barrier semaphores. Data moves between devices by JAX's collectives and lax.ppermute only.
A program may use at most 64 MiB of HBM per device.

v0:
```python
import jax
import jax.numpy as jnp
from jax import lax
from jax.sharding import PartitionSpec as P


def spread(value, axis, source):
    kept = jnp.where(lax.axis_index(axis) == source, value, 0).astype(value.dtype)
    return lax.psum(kept, axis)


def schur_rows(moment_x, zinv, row_positions, row_counts, col_positions, col_counts, group_rows):
    slot_count = row_positions.shape[1] // 2
    order_size = moment_x.shape[0]
    slot_iota = jnp.arange(slot_count, dtype=jnp.int32)
    whole_iota = jnp.arange(order_size, dtype=jnp.int32)
    col_left = col_positions[:, :slot_count].T.reshape(-1)
    col_right = col_positions[:, slot_count:].T.reshape(-1)
    col_alive = (slot_iota[:, None] < col_counts[None, :]).astype(jnp.float32).reshape(-1)
    pick_left = jnp.where(whole_iota[:, None] == col_left[None, :], col_alive[None, :], 0.0)
    pick_right = (whole_iota[:, None] == col_right[None, :]).astype(jnp.float32)
    ncols = col_positions.shape[0]
    nrows = row_positions.shape[0]

    def one_group(packed):
        grp_positions, grp_counts = packed
        grp_left = grp_positions[:, :slot_count].reshape(-1)
        grp_right = grp_positions[:, slot_count:].reshape(-1)
        grp_alive = (slot_iota[None, :] < grp_counts[:, None]).astype(jnp.float32).reshape(-1)
        x_rows = jnp.take(moment_x, grp_right, axis=0)
        w_rows = jnp.take(zinv, grp_left, axis=0)
        x_picked = jnp.dot(
            x_rows, pick_left, preferred_element_type=jnp.float32, precision=lax.Precision.HIGHEST
        )
        w_picked = jnp.dot(
            w_rows, pick_right, preferred_element_type=jnp.float32, precision=lax.Precision.HIGHEST
        )
        terms = x_picked * w_picked * grp_alive[:, None]
        return jnp.sum(terms.reshape(group_rows, slot_count, slot_count, ncols), axis=(1, 2))

    grouped = (
        row_positions.reshape(nrows // group_rows, group_rows, 2 * slot_count),
        row_counts.reshape(nrows // group_rows, group_rows),
    )
    return lax.map(one_group, grouped).reshape(nrows, ncols)


def collect(pieces):
    wide = (
        lax.all_gather(pieces[0], "col", axis=1, tiled=True),
        lax.all_gather(pieces[1], "col", axis=1, tiled=True),
    )
    return (
        lax.all_gather(wide[0], "row", axis=0, tiled=True),
        lax.all_gather(wide[1], "row", axis=0, tiled=True),
    )


def shards(moment_x, zinv, positions, entry_count):
    full_x, full_w = collect((moment_x, zinv))
    row_positions, row_counts = (
        lax.all_gather(positions, "col", axis=0, tiled=True),
        lax.all_gather(entry_count, "col", axis=0, tiled=True),
    )
    col_devices = lax.axis_size("col")
    share_ratio = col_devices // lax.axis_size("row")
    col_index = lax.axis_index("col")
    piece_size = row_counts.shape[0] // share_ratio
    offset_rows = col_index % share_ratio * piece_size
    piece_positions = lax.dynamic_slice_in_dim(row_positions, offset_rows, piece_size, 0)
    piece_counts = lax.dynamic_slice_in_dim(row_counts, offset_rows, piece_size, 0)
    col_positions, col_counts = (
        spread(piece_positions, "row", col_index // share_ratio),
        spread(piece_counts, "row", col_index // share_ratio),
    )
    group_rows = min(64, row_counts.shape[0])
    return schur_rows(
        full_x, full_w, row_positions, row_counts, col_positions, col_counts, group_rows
    )


def solution(mesh):
    return jax.shard_map(
        shards,
        mesh=mesh,
        in_specs=(P("row", "col"), P("row", "col"), P(("row", "col"), None), P(("row", "col"))),
        out_specs=P("row", "col"),
        check_vma=False,
    )
```

profile of v0, /device:TPU:0, one launch (start us, length us, event | category | flops | bytes accessed | tf_op | source)
XLA Modules:
  0.0 191.0 jit_solution(2002128787792000203)
XLA Ops:
  0.0 32.5 %all-gather = s32[8,32,16]{1,2,0:T(8,128)S(1)} all-gather(s32[1,32,16]{1,2,0:T(8,128)} %bitcast.49), channel_id=1, replica_groups=mesh['row'=4,'col'=8] {'col'}, dimensions={0}, use_global_device_ids=true | all-gather | bytes 18432 | tf_op jit(solution)/shard_map/all_gather | solution.py:62
  32.6 0.1 reshape.91
  32.7 1.3 dynamic-slice
  34.7 0.9 dynamic-update-slice
  35.6 10.8 %all-reduce = s32[256]{0:T(256)S(1)} all-reduce(s32[256]{0:T(256)S(1)} %dynamic-update-slice), channel_id=1, replica_groups=mesh['row'=4,'col'=8] {'col'}, use_global_device_ids=true, to_apply=%add | all-reduce | flops 256 | bytes 2048
  46.4 0.1 broadcast_select_fusion
  46.4 5.0 %all-reduce.1 = (s32[128,16]{0,1:T(8,128)S(1)}, s32[128]{0:T(128)S(1)}) all-reduce(s32[128,16]{0,1:T(8,128)S(1)} %dynamic-slice_select_fusion, s32[128]{0:T(128)S(1)} %broadcast_select_fusion), channel_id=1, replica_groups=mesh['row'=4,'col'=8] {'row'}, use_global_device_ids=true, to_apply=%region_0.1 | all-reduce | flops 2176 | bytes 17408 | tf_op jit(solution)/shard_map/psum | solution.py:9
  51.5 0.1 reshape.65
  51.6 0.1 copy.17
  51.7 31.1 %all-gather.1 = f32[8,62,124]{2,1,0:T(8,128)S(1)} all-gather(f32[1,62,124]{2,1,0:T(8,128)} %bitcast.47), channel_id=1, replica_groups=mesh['row'=4,'col'=8] {'col'}, dimensions={0}, use_global_device_ids=true | all-gather | bytes 276768 | tf_op jit(solution)/shard_map/all_gather | solution.py:50
  82.8 9.1 %all-gather.2 = f32[4,124,496]{1,2,0:T(8,128)S(1)} all-gather(f32[1,124,496]{1,2,0:T(8,128)S(1)} %bitcast.44), channel_id=1, replica_groups=mesh['row'=4,'col'=8] {'row'}, dimensions={0}, use_global_device_ids=true | all-gather | bytes 1230080 | tf_op jit(solution)/shard_map/all_gather | solution.py:54
  91.9 0.4 copy.13
  92.2 0.1 reshape.95
  92.4 0.3 copy-done
  92.6 30.7 %all-gather.3 = f32[8,62,124]{2,1,0:T(8,128)S(1)} all-gather(f32[1,62,124]{2,1,0:T(8,128)S(1)} %bitcast.48), channel_id=1, replica_groups=mesh['row'=4,'col'=8] {'col'}, dimensions={0}, use_global_device_ids=true | all-gather | bytes 276768 | tf_op jit(solution)/shard_map/all_gather | solution.py:51
  123.4 9.6 %all-gather.4 = f32[4,124,496]{1,2,0:T(8,128)S(1)} all-gather(f32[1,124,496]{1,2,0:T(8,128)S(1)} %bitcast.45), channel_id=1, replica_groups=mesh['row'=4,'col'=8] {'row'}, dimensions={0}, use_global_device_ids=true | all-gather | bytes 1230080 | tf_op jit(solution)/shard_map/all_gather | solution.py:55
  133.0 0.4 copy.14
  133.4 0.1 reshape.99
  133.5 56.9 %while.11 = (s32[]{:T(128)}, f32[4,64,128]{2,1,0:T(8,128)S(1)}, s32[4,64,16]{2,1,0:T(8,128)S(1)}, f32[496,496]{1,0:T(8,128)S(1)}, f32[496,496]{1,0:T(8,128)S(1)}...) while((s32[]{:T(128)}, f32[4,64,128]{2,1,0:T(8,128)S(1)}, ...), condition=%wide.region_4.6_spmd.clone, body=%wide.region_2.5_spmd.clone.sunk | while | flops 6245240832 | bytes 10464113 | solution.py:45
  133.6 0.1 reshape.122
  133.7 1.6 gather_fusion
  135.4 5.0 %fusion.41 = f32[512,1024]{1,0:T(8,128)} fusion(f32[512,496]{1,0:T(8,128)S(1)} %gather_fusion, s32[1024]{0:T(1024)S(1)} %get-tuple-element.208, pred[512]{0:T(512)(128)(4,1)S(1)} %compare_and_fusion.4), kind=kOutput, calls=%fused_computation.6.clone.1 | convolution fusion | flops 3121831936 | bytes 3117568 | tf_op jit(solution)/shard_map/while/body/eval_jaxpr/dot_general | solution.py:35
  140.4 0.1 reshape.123
  140.5 1.6 gather_fusion.1
  142.2 0.1 reshape.124
  142.3 5.4 %bitcast_reduce_fusion.2 = f32[64,128]{1,0:T(8,128)S(1)} fusion(f32[512,1024]{1,0:T(8,128)} %fusion.41, f32[512,496]{1,0:T(8,128)S(1)} %gather_fusion.1, f32[512]{0:T(512)S(1)} %reshape.124, f32[1024]{0:T(1024)S(1)} %get-tuple-element.207, s32[1024]{0:T(1024)S(1)} %get-tuple-element.206, pred[512]{0:T(512)(128)(4,1)S(1)} %compare_and_fusion.5), kind=kOutput, calls=%fused_computation.5.clone.1 | convolution fusion | flops 3123396608 | bytes 3156480 | tf_op jit(solution)/shard_map/while/body/eval_jaxpr/dot_general | solution.py:32
  147.8 0.1 reshape.122
  147.9 1.6 gather_fusion
  149.6 5.0 %fusion.41 = f32[512,1024]{1,0:T(8,128)} fusion(f32[512,496]{1,0:T(8,128)S(1)} %gather_fusion, s32[1024]{0:T(1024)S(1)} %get-tuple-element.208, pred[512]{0:T(512)(128)(4,1)S(1)} %compare_and_fusion.4), kind=kOutput, calls=%fused_computation.6.clone.1 | convolution fusion | flops 3121831936 | bytes 3117568 | tf_op jit(solution)/shard_map/while/body/eval_jaxpr/dot_general | solution.py:35
  154.6 0.1 reshape.123
  154.7 1.6 gather_fusion.1
  156.5 0.1 reshape.124
  156.6 5.4 %bitcast_reduce_fusion.2 = f32[64,128]{1,0:T(8,128)S(1)} fusion(f32[512,1024]{1,0:T(8,128)} %fusion.41, f32[512,496]{1,0:T(8,128)S(1)} %gather_fusion.1, f32[512]{0:T(512)S(1)} %reshape.124, f32[1024]{0:T(1024)S(1)} %get-tuple-element.207, s32[1024]{0:T(1024)S(1)} %get-tuple-element.206, pred[512]{0:T(512)(128)(4,1)S(1)} %compare_and_fusion.5), kind=kOutput, calls=%fused_computation.5.clone.1 | convolution fusion | flops 3123396608 | bytes 3156480 | tf_op jit(solution)/shard_map/while/body/eval_jaxpr/dot_general | solution.py:32
  162.0 0.1 reshape.122
  162.2 1.6 gather_fusion
  163.8 5.0 %fusion.41 = f32[512,1024]{1,0:T(8,128)} fusion(f32[512,496]{1,0:T(8,128)S(1)} %gather_fusion, s32[1024]{0:T(1024)S(1)} %get-tuple-element.208, pred[512]{0:T(512)(128)(4,1)S(1)} %compare_and_fusion.4), kind=kOutput, calls=%fused_computation.6.clone.1 | convolution fusion | flops 3121831936 | bytes 3117568 | tf_op jit(solution)/shard_map/while/body/eval_jaxpr/dot_general | solution.py:35
  168.8 0.1 reshape.123
  168.9 1.6 gather_fusion.1
  170.7 0.1 reshape.124
  170.8 5.4 %bitcast_reduce_fusion.2 = f32[64,128]{1,0:T(8,128)S(1)} fusion(f32[512,1024]{1,0:T(8,128)} %fusion.41, f32[512,496]{1,0:T(8,128)S(1)} %gather_fusion.1, f32[512]{0:T(512)S(1)} %reshape.124, f32[1024]{0:T(1024)S(1)} %get-tuple-element.207, s32[1024]{0:T(1024)S(1)} %get-tuple-element.206, pred[512]{0:T(512)(128)(4,1)S(1)} %compare_and_fusion.5), kind=kOutput, calls=%fused_computation.5.clone.1 | convolution fusion | flops 3123396608 | bytes 3156480 | tf_op jit(solution)/shard_map/while/body/eval_jaxpr/dot_general | solution.py:32
  176.3 0.1 reshape.122
  176.4 1.6 gather_fusion
  178.0 5.0 %fusion.41 = f32[512,1024]{1,0:T(8,128)} fusion(f32[512,496]{1,0:T(8,128)S(1)} %gather_fusion, s32[1024]{0:T(1024)S(1)} %get-tuple-element.208, pred[512]{0:T(512)(128)(4,1)S(1)} %compare_and_fusion.4), kind=kOutput, calls=%fused_computation.6.clone.1 | convolution fusion | flops 3121831936 | bytes 3117568 | tf_op jit(solution)/shard_map/while/body/eval_jaxpr/dot_general | solution.py:35
  183.1 0.1 reshape.123
  183.2 1.6 gather_fusion.1
  184.9 0.1 reshape.124
  185.0 5.4 %bitcast_reduce_fusion.2 = f32[64,128]{1,0:T(8,128)S(1)} fusion(f32[512,1024]{1,0:T(8,128)} %fusion.41, f32[512,496]{1,0:T(8,128)S(1)} %gather_fusion.1, f32[512]{0:T(512)S(1)} %reshape.124, f32[1024]{0:T(1024)S(1)} %get-tuple-element.207, s32[1024]{0:T(1024)S(1)} %get-tuple-element.206, pred[512]{0:T(512)(128)(4,1)S(1)} %compare_and_fusion.5), kind=kOutput, calls=%fused_computation.5.clone.1 | convolution fusion | flops 3123396608 | bytes 3156480 | tf_op jit(solution)/shard_map/while/body/eval_jaxpr/dot_general | solution.py:32
  190.4 0.6 copy-done.1
  (54 shorter events, 0.9 us)
Async XLA Ops:
  91.9 0.8 copy-start
  190.4 0.7 copy-start.1
where the time goes:
time: 191 us
  blocking collectives  129 us (68%)
  matrix products  41.5 us (22%)
  local copies, waits for them, and re-layouts  18.8 us (10%)
    all_gather x1, blocking collectives, shards(): lax.all_gather(positions, 'col', axis=0, tiled=True)  32.5 us
    all_gather x1, blocking collectives, collect(): lax.all_gather(pieces[0], 'col', axis=1, tiled=True)  31.1 us
    all_gather x1, blocking collectives, collect(): lax.all_gather(pieces[1], 'col', axis=1, tiled=True)  30.7 us
    dot_general x4, matrix products, one_group(): jnp.dot(x_rows, pick_left, preferred_element_type=jnp.float32, precision=...  21.4 us
    dot_general x4, matrix products, one_group(): jnp.dot(w_rows, pick_right, preferred_element_type=jnp.float32, precision...  20.1 us
    unnamed x1, blocking collectives  10.8 us
    all_gather x1, blocking collectives, collect(): lax.all_gather(wide[1], 'row', axis=0, tiled=True)  9.63 us
    all_gather x1, blocking collectives, collect(): lax.all_gather(wide[0], 'row', axis=0, tiled=True)  9.1 us

commit v1 on v0

v1 whole, which is shorter than its diff:
```python
import functools
import jax
import jax.numpy as jnp
from jax import lax
from jax.experimental import pallas as pl
from jax.experimental.pallas import tpu as pltpu
from jax.sharding import PartitionSpec as P

LANES = 128
F32, BF16, I32 = jnp.float32, jnp.bfloat16, jnp.int32


class Plan:
    def __init__(self, rows, cols, x_shape, pos_shape):
        self.rows, self.cols = rows, cols
        self.mb, self.nb = x_shape
        self.order = self.mb * rows
        self.halves = self.mb // self.nb
        self.slot = 1 << self.nb.bit_length()
        self.depth = cols * self.slot
        self.dead = self.slot - 1
        self.local, self.slots = pos_shape[0], pos_shape[1] // 2
        self.per_tile = LANES // self.local
        self.ni = self.local * cols
        self.nj = self.local * rows
        self.x_at, self.z_at, self.p_at = 0, self.slot, 2 * self.slot
        self.payload = 2 * self.slot + 2 * self.slots
        row_bits = [b for b in range(rows.bit_length() - 1)]
        col_bits = [b for b in range(cols.bit_length() - 1)]
        self.steps = [("row", b) for b in row_bits[1:]]
        self.steps += [("col", b) for b in col_bits]
        self.steps += [("row", 0)]

    def place(self, row_xor, col_xor):
        out = 0
        for n, (axis, bit) in enumerate(self.steps):
            value = row_xor if axis == "row" else col_xor
            out = out | (((value >> bit) & 1) << n)
        return out


def pack_kernel(plan, x_ref, z_ref, pos_ref, cnt_ref, out_ref):
    nb, slot = plan.nb, plan.slot
    out_ref[...] = jnp.zeros_like(out_ref)
    zt = z_ref[...].T
    for h in range(plan.halves):
        out_ref[0:nb, h * slot : h * slot + nb] = x_ref[h * nb : (h + 1) * nb, :]
        out_ref[slot : slot + nb, h * slot : h * slot + nb] = zt[:, h * nb : (h + 1) * nb]
    spots = pos_ref[...].astype(F32).T
    code = spots
    for t in range(1, plan.cols):
        code = code + jnp.where(spots >= float(t * nb), float(slot - nb), 0.0)
    k = lax.broadcasted_iota(I32, code.shape, 0) % plan.slots
    code = jnp.where(k < cnt_ref[...], code, float(plan.dead))
    wide = jnp.concatenate([code] * plan.per_tile, axis=1)
    me = lax.axis_index("row") * plan.cols + lax.axis_index("col")
    mine = lax.broadcasted_iota(I32, wide.shape, 1) // plan.local == me % plan.per_tile
    out_ref[plan.p_at :, :] = jnp.where(mine, wide, 0.0)


def main_kernel(plan, g_ref, out_ref, xj, zj, pick, ivec, acc, idx, sem):
    slot, halves, cols, rows = plan.slot, plan.halves, plan.cols, plan.rows
    slots, tiles = plan.slots, plan.ni // LANES
    me_r, me_c = lax.axis_index("row"), lax.axis_index("col")
    chunk = pl.program_id(0)
    group_of = me_c // plan.per_tile

    def codes(row, group):
        at = row ^ me_r
        total = None
        for e in range(plan.per_tile):
            cx = (group ^ group_of) * plan.per_tile + e
            part = g_ref[plan.place(at, cx), plan.p_at :, :]
            total = part if total is None else total + part
        return total.astype(I32)

    for t in range(tiles):
        ivec[t] = codes(me_r, t)
    copy = pltpu.make_async_copy(ivec, idx, sem)
    copy.start()

    tile_at = me_c * (plan.nj // LANES) + chunk
    jcode = codes(tile_at // (cols // plan.per_tile), tile_at % (cols // plan.per_tile))
    depth_iota = lax.broadcasted_iota(I32, (plan.depth, LANES), 0)
    lane = lax.broadcasted_iota(I32, (slot, LANES), 1)
    per_group = LANES // slot

    def block(row, col, at):
        return g_ref[plan.place(row ^ me_r, col ^ me_c), at : at + slot, :]

    def split(v):
        hi = v.astype(BF16)
        lo = (v - hi.astype(F32)).astype(BF16)
        return hi, lo

    def select(left, out):
        hi, lo = split(left)
        both = jnp.concatenate([hi, lo], axis=0)
        res = jnp.dot(both, pick[...], preferred_element_type=F32)
        res = res[:slot] + res[slot:]
        for l in range(slots):
            out[pl.ds(l, slot, stride=slots), :] = res[:, l * LANES : (l + 1) * LANES]

    for l in range(slots):
        at = jcode[l : l + 1, :]
        pick[:, l * LANES : (l + 1) * LANES] = jnp.where(depth_iota == at, 1.0, 0.0).astype(BF16)
    for r in range(rows):
        for h in range(halves):
            parts = []
            for g in range(cols // per_group):
                part = None
                for e in range(per_group):
                    v = block(r, g * per_group + e, plan.x_at)
                    if e != h:
                        v = pltpu.roll(v, ((e - h) * slot) % LANES, 1)
                    part = v if part is None else jnp.where(lane // slot == e, v, part)
                parts.append(part)
            u = r * halves + h
            select(jnp.concatenate(parts, axis=1), xj.at[pl.ds(u * slot * slots, slot * slots), :])
    for l in range(slots):
        at = jcode[slots + l : slots + l + 1, :]
        pick[:, l * LANES : (l + 1) * LANES] = jnp.where(depth_iota == at, 1.0, 0.0).astype(BF16)
    wide = halves * slot
    for c in range(cols):
        parts = []
        for g in range(rows * wide // LANES):
            part = None
            for e in range(LANES // wide):
                v = block(g * (LANES // wide) + e, c, plan.z_at)
                if e:
                    v = pltpu.roll(v, e * wide, 1)
                part = v if part is None else jnp.where(lane // wide == e, v, part)
            parts.append(part)
        select(jnp.concatenate(parts, axis=1), zj.at[pl.ds(c * slot * slots, slot * slots), :])

    copy.wait()

    def eight(n, _):
        tile, base = n // (LANES // 8), (n % (LANES // 8)) * 8
        for s in range(8):
            total = None
            for k in range(slots):
                q = pl.multiple_of(idx[tile, slots + k, base + s] * slots, slots)
                p = pl.multiple_of(idx[tile, k, base + s] * slots, slots)
                term = xj[pl.ds(q, slots), :] * zj[pl.ds(p, slots), :]
                total = term if total is None else total + term
            acc[s * slots : (s + 1) * slots, :] = total
        out = None
        for l in range(slots):
            v = acc[pl.ds(l, 8, stride=slots), :]
            out = v if out is None else out + v
        out_ref[pl.ds(pl.multiple_of(n * 8, 8), 8), :] = out
        return 0

    lax.fori_loop(0, plan.ni // 8, eight, 0)


def gather(plan, v):
    for axis, bit in plan.steps:
        size = plan.rows if axis == "row" else plan.cols
        other = lax.ppermute(v, axis, [(d, d ^ (1 << bit)) for d in range(size)])
        v = jnp.concatenate([v, other], axis=0)
    return v


def shards(rows, cols, moment_x, zinv, positions, entry_count):
    plan = Plan(rows, cols, moment_x.shape, positions.shape)
    packed = pl.pallas_call(
        functools.partial(pack_kernel, plan),
        out_shape=jax.ShapeDtypeStruct((plan.payload, LANES), F32),
        name="pack",
    )(moment_x, zinv, positions, entry_count.reshape(1, -1))
    whole = gather(plan, packed[None])
    return pl.pallas_call(
        functools.partial(main_kernel, plan),
        grid=(plan.nj // LANES,),
        in_specs=[pl.BlockSpec(memory_space=pltpu.VMEM)],
        out_specs=pl.BlockSpec((plan.ni, LANES), lambda c: (0, c)),
        out_shape=jax.ShapeDtypeStruct((plan.ni, plan.nj), F32),
        scratch_shapes=[
            pltpu.VMEM((plan.depth * plan.slots, LANES), F32),
            pltpu.VMEM((plan.depth * plan.slots, LANES), F32),
            pltpu.VMEM((plan.depth, plan.slots * LANES), BF16),
            pltpu.VMEM((plan.ni // LANES, 2 * plan.slots, LANES), I32),
            pltpu.VMEM((8 * plan.slots, LANES), F32),
            pltpu.SMEM((plan.ni // LANES, 2 * plan.slots, LANES), I32),
            pltpu.SemaphoreType.DMA,
        ],
        name="schur",
    )(whole)


def solution(mesh):
    return jax.shard_map(
        functools.partial(shards, mesh.shape["row"], mesh.shape["col"]),
        mesh=mesh,
        in_specs=(P("row", "col"), P("row", "col"), P(("row", "col"), None), P(("row", "col"))),
        out_specs=P("row", "col"),
        check_vma=False,
    )
```

time: 191 us -> 71.6 us (0.37)
  blocking collectives: 129 us -> 0 us
  matrix products: 41.5 us -> 0 us
  waiting for transfers between devices: 0 us -> 34.8 us
  Pallas kernels: 0 us -> 16.1 us
  local copies, waits for them, and re-layouts: 18.8 us -> 6.86 us
  starting transfers between devices: 0 us -> 10.5 us
  other arithmetic: 0.55 us -> 2.73 us
    all_gather x5 -> x0, blocking collectives: 113 us -> none  [the longest x1 32.5 us: shards(): lax.all_gather(positions, 'col', axis=0, tiled=True)]
    dot_general x8 -> x0, matrix products: 41.5 us -> none  [the longest x4 21.4 us: one_group(): jnp.dot(x_rows, pick_left, preferred_element_type=jnp.float32, precision=...]
    ppermute x0 -> x5, waiting for transfers between devices: none -> 34.8 us  [gather(): other = lax.ppermute(v, axis, [(d, d ^ 1 << bit) for d in range(size)])]
    pallas_call x0 -> x2, Pallas kernels: none -> 16.1 us  [the longest x1 14.4 us: shards(): pl.pallas_call(functools.partial(main_kernel, plan), grid=(plan.nj // LAN...]
    gather x8 -> x0, local copies, waits for them, and re-layouts: 13 us -> none  [the longest x4 6.48 us: one_group(): x_rows = jnp.take(moment_x, grp_right, axis=0)]
    unnamed x1 -> x0, blocking collectives: 10.8 us -> none
    ppermute x0 -> x5, starting transfers between devices: none -> 10.5 us  [gather(): other = lax.ppermute(v, axis, [(d, d ^ 1 << bit) for d in range(size)])]
    psum x1 -> x0, blocking collectives: 5.04 us -> none  [spread(): return lax.psum(kept, axis)]
  transfers between devices with their start and end apart: 0 -> 5, of which waited for: 0 -> 5; matrix products, arithmetic and copies ran while one was open for 0% -> 1% of each run, Pallas kernels for 0% -> 0%
where the time goes in v1:
time: 71.6 us; the launch traced here: 71.1 us
  waiting for transfers between devices  34.8 us (49%)
  Pallas kernels  16.1 us (22%)
  starting transfers between devices  10.5 us (15%)
  local copies, waits for them, and re-layouts  6.86 us (10%)
  other arithmetic  2.73 us (4%)
    ppermute x5, waiting for transfers between devices, gather(): other = lax.ppermute(v, axis, [(d, d ^ 1 << bit) for d in range(size)])  34.8 us
    pallas_call x1, Pallas kernels, shards(): pl.pallas_call(functools.partial(main_kernel, plan), grid=(plan.nj // LAN...  14.4 us
    ppermute x5, starting transfers between devices, gather(): other = lax.ppermute(v, axis, [(d, d ^ 1 << bit) for d in range(size)])  10.5 us
    unnamed x9, local copies, waits for them, and re-layouts  6.71 us
    concatenate x3, other arithmetic, gather(): v = jnp.concatenate([v, other], axis=0)  2.73 us
    pallas_call x1, Pallas kernels, shards(): pl.pallas_call(functools.partial(pack_kernel, plan), out_shape=jax.ShapeD...  1.67 us
  transfers between devices with their start and end apart: 5, of which 5 were waited for; matrix products, arithmetic and copies ran while one was open for 1% of the time, Pallas kernels for 0%

profile of v1, /device:TPU:0, one launch (start us, length us, event | category | flops | bytes accessed | tf_op | source)
XLA Modules:
  0.0 71.1 jit_solution(4343769451218954138)
XLA Ops:
  0.0 1.5 %copy.5.x_ref = f32[124,62]{1,0:T(8,128)} copy(f32[124,62]{0,1:T(8,128)} %param.4) | data formatting | bytes 61504 | tf_op args[0]
  1.5 1.5 %copy.6.z_ref = f32[124,62]{1,0:T(8,128)} copy(f32[124,62]{0,1:T(8,128)} %param.5) | data formatting | bytes 61504 | tf_op args[1]
  3.0 1.4 %copy.7.pos_ref = s32[32,16]{1,0:T(8,128)} copy(s32[32,16]{0,1:T(8,128)} %param.6) | data formatting | bytes 4096 | tf_op args[2]
  4.3 1.7 %pack.1 = f32[144,128]{1,0:T(8,128)} custom-call(f32[124,62]{1,0:T(8,128)} %copy.5.x_ref, f32[124,62]{1,0:T(8,128)} %copy.6.z_ref, s32[32,16]{1,0:T(8,128)} %copy.7.pos_ref, s32[1,32]{1,0:T(1,128)} %bitcast.8), custom_call_target="tpu_custom_call" | custom-call | tf_op jit(solution)/shard_map/pack/pallas_call | solution.py:168
  6.0 3.0 %collective-permute-start = (f32[1,144,128]{2,1,0:T(8,128)}, f32[1,144,128]{2,1,0:T(8,128)S(1)}, u32[]{:S(2)}, u32[]{:S(2)}) collective-permute-start(f32[1,144,128]{2,1,0:T(8,128)} %bitcast.4), channel_id=1, source_target_pairs={{0,16},{8,24},{16,0},{24,8},{1,17},{9,25},{17,1},{25,9},{2,18},{10... | collective-permute-start | bytes 221192 | tf_op jit(solution)/shard_map/ppermute | solution.py:161
  9.0 2.5 %collective-permute-done = f32[1,144,128]{2,1,0:T(8,128)S(1)} collective-permute-done((f32[1,144,128]{2,1,0:T(8,128)}, f32[1,144,128]{2,1,0:T(8,128)S(1)}, u32[]{:S(2)}, u32[]{:S(2)}) %collective-permute-start) | collective-permute-done | bytes 73760 | tf_op jit(solution)/shard_map/ppermute | solution.py:161
  11.5 0.9 %pad_maximum_fusion.2 = f32[2,144,128]{2,1,0:T(8,128)S(1)} fusion(f32[1,144,128]{2,1,0:T(8,128)S(1)} %collective-permute-done, f32[1,144,128]{2,1,0:T(8,128)} %bitcast.5), kind=kLoop, calls=%fused_computation.2 | loop fusion | flops 36864 | bytes 294912 | tf_op jit(solution)/shard_map/concatenate | solution.py:162
  12.4 2.1 %collective-permute-start.1 = (f32[2,144,128]{2,1,0:T(8,128)S(1)}, f32[2,144,128]{2,1,0:T(8,128)S(1)}, u32[]{:S(2)}, u32[]{:S(2)}) collective-permute-start(f32[2,144,128]{2,1,0:T(8,128)S(1)} %pad_maximum_fusion.2), channel_id=1, source_target_pairs={{0,1},{1,0},{2,3},{3,2},{4,5},{5,4},{6,7},{7,6},{8,9},{9,8},{10,11... | collective-permute-start | bytes 442376 | tf_op jit(solution)/shard_map/ppermute | solution.py:161
  14.5 3.1 %collective-permute-done.1 = f32[2,144,128]{2,1,0:T(8,128)S(1)} collective-permute-done((f32[2,144,128]{2,1,0:T(8,128)S(1)}, f32[2,144,128]{2,1,0:T(8,128)S(1)}, u32[]{:S(2)}, u32[]{:S(2)}) %collective-permute-start.1) | collective-permute-done | bytes 147488 | tf_op jit(solution)/shard_map/ppermute | solution.py:161
  17.7 0.9 %pad_maximum_fusion.1 = f32[4,144,128]{2,1,0:T(8,128)S(1)} fusion(f32[2,144,128]{2,1,0:T(8,128)S(1)} %collective-permute-done.1, f32[1,144,128]{2,1,0:T(8,128)S(1)} %collective-permute-done, f32[1,144,128]{2,1,0:T(8,128)} %bitcast.6), kind=kLoop, calls=%fused_computation.1 | loop fusion | flops 147456 | bytes 589824 | tf_op jit(solution)/shard_map/concatenate | solution.py:162
  18.6 2.1 %collective-permute-start.2 = (f32[4,144,128]{2,1,0:T(8,128)S(1)}, f32[4,144,128]{2,1,0:T(8,128)S(1)}, u32[]{:S(2)}, u32[]{:S(2)}) collective-permute-start(f32[4,144,128]{2,1,0:T(8,128)S(1)} %pad_maximum_fusion.1), channel_id=1, source_target_pairs={{0,2},{1,3},{2,0},{3,1},{4,6},{5,7},{6,4},{7,5},{8,10},{9,11},{10,... | collective-permute-start | bytes 884744 | tf_op jit(solution)/shard_map/ppermute | solution.py:161
  20.7 4.7 %collective-permute-done.2 = f32[4,144,128]{2,1,0:T(8,128)S(1)} collective-permute-done((f32[4,144,128]{2,1,0:T(8,128)S(1)}, f32[4,144,128]{2,1,0:T(8,128)S(1)}, u32[]{:S(2)}, u32[]{:S(2)}) %collective-permute-start.2) | collective-permute-done | bytes 294944 | tf_op jit(solution)/shard_map/ppermute | solution.py:161
  25.4 0.9 %pad_maximum_fusion = f32[8,144,128]{2,1,0:T(8,128)S(1)} fusion(f32[4,144,128]{2,1,0:T(8,128)S(1)} %collective-permute-done.2, f32[2,144,128]{2,1,0:T(8,128)S(1)} %collective-permute-done.1, f32[1,144,128]{2,1,0:T(8,128)S(1)} %collective-permute-done, f32[1,144,128]{2,1,0:T(8,128)} %bitcast.7), kind=kLoop, calls=%fused_computation | loop fusion | flops 442368 | bytes 1179648 | tf_op jit(solution)/shard_map/concatenate | solution.py:162
  26.4 3.2 %collective-permute-start.3 = (f32[8,144,128]{2,1,0:T(8,128)S(1)}, f32[8,144,128]{2,1,0:T(8,128)S(1)}, u32[]{:S(2)}, u32[]{:S(2)}) collective-permute-start(f32[8,144,128]{2,1,0:T(8,128)S(1)} %pad_maximum_fusion), channel_id=1, source_target_pairs={{0,4},{1,5},{2,6},{3,7},{4,0},{5,1},{6,2},{7,3},{8,12},{9,13},{10,... | collective-permute-start | bytes 1769480 | tf_op jit(solution)/shard_map/ppermute | solution.py:161
  29.6 0.9 %constant_dynamic-update-slice_fusion.4 = (f32[16,144,128]{2,1,0:T(8,128)S(1)}, f32[32,144,128]{2,1,0:T(8,128)S(1)}) fusion(f32[144,128]{1,0:T(8,128)} %pack.1), kind=kLoop, calls=%fused_computation.7 | loop fusion | bytes 221184
  30.6 21.6 %collective-permute-done.3 = f32[8,144,128]{2,1,0:T(8,128)S(1)} collective-permute-done((f32[8,144,128]{2,1,0:T(8,128)S(1)}, f32[8,144,128]{2,1,0:T(8,128)S(1)}, u32[]{:S(2)}, u32[]{:S(2)}) %collective-permute-start.3) | collective-permute-done | bytes 589856 | tf_op jit(solution)/shard_map/ppermute | solution.py:161
  52.2 0.1 constant_dynamic-update-slice_fusion
  52.2 0.1 collective-permute-start.4
  52.3 2.8 %collective-permute-done.4 = f32[16,144,128]{2,1,0:T(8,128)S(1)} collective-permute-done((f32[16,144,128]{2,1,0:T(8,128)S(1)}, f32[16,144,128]{2,1,0:T(8,128)S(1)}, u32[]{:S(2)}, u32[]{:S(2)}) %collective-permute-start.4) | collective-permute-done | bytes 1179680 | tf_op jit(solution)/shard_map/ppermute | solution.py:161
  55.1 0.1 constant_dynamic-update-slice_fusion.5.g_ref
  55.2 0.0 copy-start
  55.2 1.4 %copy-done = f32[32,144,128]{2,1,0:T(8,128)} copy-done((f32[32,144,128]{2,1,0:T(8,128)}, f32[32,144,128]{2,1,0:T(8,128)S(1)}, u32[]{:S(2)}) %copy-start) | copy-done | bytes 2359320
  56.6 14.4 %schur.1 = f32[256,128]{1,0:T(8,128)} custom-call(f32[32,144,128]{2,1,0:T(8,128)} %copy-done), custom_call_target="tpu_custom_call" | custom-call | tf_op jit(solution)/shard_map/schur/pallas_call | solution.py:174
  (3 shorter events, 0.1 us)
Async XLA Ops:
  6.0 5.5 %collective-permute-start = (f32[1,144,128]{2,1,0:T(8,128)}, f32[1,144,128]{2,1,0:T(8,128)S(1)}, u32[]{:S(2)}, u32[]{:S(2)}) collective-permute-start(f32[1,144,128]{2,1,0:T(8,128)} %bitcast.4), channel_id=1, source_target_pairs={{0,16},{8,24},{16,0},{24,8},{1,17},{9,25},{17,1},{25,9},{2,18},{10... | collective-permute-start | bytes 221192 | tf_op jit(solution)/shard_map/ppermute | solution.py:161
  12.4 5.2 %collective-permute-start.1 = (f32[2,144,128]{2,1,0:T(8,128)S(1)}, f32[2,144,128]{2,1,0:T(8,128)S(1)}, u32[]{:S(2)}, u32[]{:S(2)}) collective-permute-start(f32[2,144,128]{2,1,0:T(8,128)S(1)} %pad_maximum_fusion.2), channel_id=1, source_target_pairs={{0,1},{1,0},{2,3},{3,2},{4,5},{5,4},{6,7},{7,6},{8,9},{9,8},{10,11... | collective-permute-start | bytes 442376 | tf_op jit(solution)/shard_map/ppermute | solution.py:161
  18.6 6.9 %collective-permute-start.2 = (f32[4,144,128]{2,1,0:T(8,128)S(1)}, f32[4,144,128]{2,1,0:T(8,128)S(1)}, u32[]{:S(2)}, u32[]{:S(2)}) collective-permute-start(f32[4,144,128]{2,1,0:T(8,128)S(1)} %pad_maximum_fusion.1), channel_id=1, source_target_pairs={{0,2},{1,3},{2,0},{3,1},{4,6},{5,7},{6,4},{7,5},{8,10},{9,11},{10,... | collective-permute-start | bytes 884744 | tf_op jit(solution)/shard_map/ppermute | solution.py:161
  26.4 25.8 %collective-permute-start.3 = (f32[8,144,128]{2,1,0:T(8,128)S(1)}, f32[8,144,128]{2,1,0:T(8,128)S(1)}, u32[]{:S(2)}, u32[]{:S(2)}) collective-permute-start(f32[8,144,128]{2,1,0:T(8,128)S(1)} %pad_maximum_fusion), channel_id=1, source_target_pairs={{0,4},{1,5},{2,6},{3,7},{4,0},{5,1},{6,2},{7,3},{8,12},{9,13},{10,... | collective-permute-start | bytes 1769480 | tf_op jit(solution)/shard_map/ppermute | solution.py:161
  52.2 2.9 %collective-permute-start.4 = (f32[16,144,128]{2,1,0:T(8,128)S(1)}, f32[16,144,128]{2,1,0:T(8,128)S(1)}, u32[]{:S(2)}, u32[]{:S(2)}) collective-permute-start(f32[16,144,128]{2,1,0:T(8,128)S(1)} %get-tuple-element.5), channel_id=1, source_target_pairs={{0,8},{8,0},{16,24},{24,16},{1,9},{9,1},{17,25},{25,17},{2,10},{10... | collective-permute-start | bytes 3538952 | tf_op jit(solution)/shard_map/ppermute | solution.py:161
  55.2 1.4 %copy-start = (f32[32,144,128]{2,1,0:T(8,128)}, f32[32,144,128]{2,1,0:T(8,128)S(1)}, u32[]{:S(2)}) copy-start(f32[32,144,128]{2,1,0:T(8,128)S(1)} %constant_dynamic-update-slice_fusion.5.g_ref) | copy-start | bytes 7077892

commit v2 on v1

v2 whole, which is shorter than its diff:
```python
import functools
import itertools
import jax
import jax.numpy as jnp
from jax import lax
from jax.experimental import pallas as pl
from jax.experimental.pallas import tpu as pltpu
from jax.sharding import PartitionSpec as P

LANES = 128
F32, BF16, I32 = jnp.float32, jnp.bfloat16, jnp.int32
EXTRA = 8


class Plan:
    def __init__(self, rows, cols, x_shape, pos_shape):
        self.rows, self.cols = rows, cols
        self.mb, self.nb = x_shape
        self.halves = self.mb // self.nb
        self.slot = 1 << self.nb.bit_length()
        self.wide = self.halves * self.slot
        self.depth = cols * self.slot
        self.dead = self.slot - 1
        self.local, self.slots = pos_shape[0], pos_shape[1] // 2
        self.fold = LANES // self.local
        self.folded = 2 * self.slots // self.fold
        self.ni = self.local * cols
        self.nj = self.local * rows
        self.payload = self.slot + EXTRA
        row_bits, col_bits = rows.bit_length() - 1, cols.bit_length() - 1
        y_bits = col_bits // 2
        self.far = [(0, k << y_bits) for k in range(1 << (col_bits - y_bits))]
        self.near = [(i << 1, k) for i in range(1 << (row_bits - 1)) for k in range(1 << y_bits)]


def pack_kernel(plan, x_ref, z_ref, pos_ref, cnt_ref, out_ref):
    nb, slot, wide = plan.nb, plan.slot, plan.wide
    me_r, me_c = lax.axis_index("row"), lax.axis_index("col")
    out_ref[...] = jnp.zeros_like(out_ref)
    a = lax.broadcasted_iota(I32, (nb, plan.mb), 0) + me_c * nb
    b = lax.broadcasted_iota(I32, (nb, plan.mb), 1) + me_r * plan.mb
    z = z_ref[...]
    mixed = jnp.where(a <= b, x_ref[...], z)
    diag = jnp.sum(jnp.where(a == b, z, 0.0), axis=0, keepdims=True)
    at = slot + plan.folded
    for h in range(plan.halves):
        out_ref[0:nb, h * slot : h * slot + nb] = mixed[:, h * nb : (h + 1) * nb]
        out_ref[at : at + 1, h * slot : h * slot + nb] = diag[:, h * nb : (h + 1) * nb]
    spots = pos_ref[...].astype(F32)
    code = spots
    for t in range(1, plan.cols):
        code = code + jnp.where(spots >= float(t * nb), float(slot - nb), 0.0)
    k = lax.broadcasted_iota(I32, code.shape, 0) % plan.slots
    code = jnp.where(k < cnt_ref[...], code, float(plan.dead))
    for g in range(plan.fold):
        piece = code[g * plan.folded : (g + 1) * plan.folded, :]
        out_ref[slot : slot + plan.folded, g * plan.local : (g + 1) * plan.local] = piece


def main_kernel(plan, n_in, *refs):
    ins, out_ref = refs[:n_in], refs[n_in]
    misc, mat, left, xj, zj, pick, ivec, acc, idx, sem = refs[n_in + 1 :]
    slot, cols, rows = plan.slot, plan.cols, plan.rows
    slots, tiles, depth = plan.slots, plan.ni // LANES, plan.depth
    me_r, me_c = lax.axis_index("row"), lax.axis_index("col")
    chunk = pl.program_id(0)
    per = LANES // plan.wide
    if per > 1:
        mat[...] = jnp.zeros_like(mat)
    near = [(core ^ i, k) for core in (0, 1) for i, k in plan.near]
    for ref, (ri, ci) in zip(ins, near):
        for n, (rf, cf) in enumerate(plan.far):
            r, c = me_r ^ (ri ^ rf), me_c ^ (ci ^ cf)
            misc[r * cols + c] = ref[n, slot:, :]
            v = ref[n, 0:slot, :]
            span = pl.ds(pl.multiple_of(c * slot, slot), slot)
            if per == 1:
                mat[r, span, :] = v
            else:
                mat[r // per, span, :] += pltpu.roll(v, (r % per) * plan.wide, 1)

    lane = lax.broadcasted_iota(I32, (plan.folded, LANES), 1) // plan.local

    def codes(first):
        got = [misc[first + e][0 : plan.folded] for e in range(plan.fold)]
        quads = []
        for g in range(plan.fold):
            quad = None
            for e in range(plan.fold):
                v = got[e]
                if e != g:
                    v = pltpu.roll(v, ((e - g) * plan.local) % LANES, 1)
                quad = v if quad is None else jnp.where(lane == e, v, quad)
            quads.append(quad)
        return jnp.concatenate(quads, axis=0).astype(I32)

    for t in range(tiles):
        ivec[t] = codes(me_r * cols + t * plan.fold) * slots
    copy = pltpu.make_async_copy(ivec, idx, sem)
    copy.start()
    jcode = codes(me_c * rows + chunk * plan.fold)

    depth_iota = lax.broadcasted_iota(I32, (depth, LANES), 0)
    n_tile = depth // LANES
    ra = lax.broadcasted_iota(I32, (LANES, LANES), 0)
    rb = lax.broadcasted_iota(I32, (LANES, LANES), 1)

    def tile(i, j):
        return mat[j, i * LANES : (i + 1) * LANES, :]

    def put(i, j, v):
        hi = v.astype(BF16)
        lo = (v - hi.astype(F32)).astype(BF16)
        left[i * LANES : (i + 1) * LANES, j * LANES : (j + 1) * LANES] = hi
        left[depth + i * LANES : depth + (i + 1) * LANES, j * LANES : (j + 1) * LANES] = lo

    def select(base, out):
        for l in range(slots):
            at = jcode[base + l : base + l + 1, :]
            pick[:, l * LANES : (l + 1) * LANES] = jnp.where(depth_iota == at, 1.0, 0.0).astype(BF16)
        for m in range(slots // 2):
            res = jnp.dot(left[...], pick[:, m * 256 : (m + 1) * 256], preferred_element_type=F32)
            res = res[:depth] + res[depth:]
            for l in range(2):
                out[pl.ds(2 * m + l, depth, stride=slots), :] = res[:, l * LANES : (l + 1) * LANES]

    for i in range(n_tile):
        for j in range(i, n_tile):
            v = tile(i, j)
            if i == j:
                put(i, i, jnp.where(ra <= rb, v, v.T))
            else:
                put(i, j, v)
                put(j, i, v.T)
    select(0, xj)
    per_tile = LANES // slot
    for i in range(n_tile):
        for j in range(i, n_tile):
            v = tile(j, i)
            if i == j:
                diag = None
                for c in range(i * per_tile, (i + 1) * per_tile):
                    r = c // plan.halves
                    row = misc[r * cols + c][plan.folded : plan.folded + 1]
                    if per > 1 and r % per:
                        row = pltpu.roll(row, (r % per) * plan.wide, 1)
                    diag = row if diag is None else diag + row
                put(i, i, jnp.where(ra > rb, v, jnp.where(ra == rb, diag, v.T)))
            else:
                put(j, i, v)
                put(i, j, v.T)
    select(slots, zj)
    copy.wait()

    def eight(n, _):
        tile_at, base = n // (LANES // 8), (n % (LANES // 8)) * 8
        for s in range(8):
            total = None
            for k in range(slots):
                q = pl.multiple_of(idx[tile_at, slots + k, base + s], slots)
                p = pl.multiple_of(idx[tile_at, k, base + s], slots)
                term = xj[pl.ds(q, slots), :] * zj[pl.ds(p, slots), :]
                total = term if total is None else total + term
            acc[s * slots : (s + 1) * slots, :] = total
        out = None
        for l in range(slots):
            v = acc[pl.ds(l, 8, stride=slots), :]
            out = v if out is None else out + v
        out_ref[pl.ds(pl.multiple_of(n * 8, 8), 8), :] = out
        return 0

    lax.fori_loop(0, plan.ni // 8, eight, 0)


def send(plan, v, row_xor, col_xor):
    size = plan.cols
    pairs = []
    for r, c in itertools.product(range(plan.rows), range(plan.cols)):
        pairs.append((r * size + c, (r ^ row_xor) * size + (c ^ col_xor)))
    return lax.ppermute(v, ("row", "col"), pairs)


def gather(plan, v):
    line = [v if k == (0, 0) else send(plan, v, *k) for k in plan.far]
    stack = jnp.stack(line)
    stacks = [stack if k == (0, 0) else send(plan, stack, *k) for k in plan.near]
    return stacks + [send(plan, s, 1, 0) for s in stacks]


def schur_call(plan, stacks):
    n_tile = plan.depth // LANES
    return pl.pallas_call(
        functools.partial(main_kernel, plan, len(stacks)),
        grid=(plan.nj // LANES,),
        in_specs=[pl.BlockSpec(memory_space=pltpu.VMEM)] * len(stacks),
        out_specs=pl.BlockSpec((plan.ni, LANES), lambda c: (0, c)),
        out_shape=jax.ShapeDtypeStruct((plan.ni, plan.nj), F32),
        scratch_shapes=[
            pltpu.VMEM((plan.rows * plan.cols, EXTRA, LANES), F32),
            pltpu.VMEM((n_tile, plan.depth, LANES), F32),
            pltpu.VMEM((2 * plan.depth, plan.depth), BF16),
            pltpu.VMEM((plan.depth * plan.slots, LANES), F32),
            pltpu.VMEM((plan.depth * plan.slots, LANES), F32),
            pltpu.VMEM((plan.depth, plan.slots * LANES), BF16),
            pltpu.VMEM((plan.ni // LANES, 2 * plan.slots, LANES), I32),
            pltpu.VMEM((8 * plan.slots, LANES), F32),
            pltpu.SMEM((plan.ni // LANES, 2 * plan.slots, LANES), I32),
            pltpu.SemaphoreType.DMA,
        ],
        compiler_params=pltpu.CompilerParams(vmem_limit_bytes=24 << 20),
        name="schur",
    )(*stacks)


def shards(rows, cols, moment_x, zinv, positions, entry_count):
    plan = Plan(rows, cols, moment_x.shape, positions.shape)
    packed = pl.pallas_call(
        functools.partial(pack_kernel, plan),
        out_shape=jax.ShapeDtypeStruct((plan.payload, LANES), F32),
        compiler_params=pltpu.CompilerParams(vmem_limit_bytes=4 << 20),
        name="pack",
    )(moment_x.T, zinv.T, positions.T, entry_count.reshape(1, -1))
    return schur_call(plan, gather(plan, packed))


def solution(mesh):
    return jax.shard_map(
        functools.partial(shards, mesh.shape["row"], mesh.shape["col"]),
        mesh=mesh,
        in_specs=(P("row", "col"), P("row", "col"), P(("row", "col"), None), P(("row", "col"))),
        out_specs=P("row", "col"),
        check_vma=False,
    )
```

time: 71.6 us -> 35.2 us (0.49)
  waiting for transfers between devices: 34.8 us -> 10.1 us
  Pallas kernels: 16.1 us -> 12.1 us
  local copies, waits for them, and re-layouts: 6.86 us -> 2.87 us
  other arithmetic: 2.73 us -> 0.01 us
    ppermute x5 -> x10, waiting for transfers between devices: 34.8 us -> 10.1 us  [send(): return lax.ppermute(v, ('row', 'col'), pairs)]
    unnamed x9 -> x8, local copies, waits for them, and re-layouts: 6.71 us -> 2.87 us
    concatenate x3 -> x0, other arithmetic: 2.73 us -> none  [gather(): v = jnp.concatenate([v, other], axis=0)]
    pallas_call x1, Pallas kernels: 14.4 us -> 12 us  [schur_call(): pl.pallas_call(functools.partial(main_kernel, plan, len(stacks)), grid=(p...]
    pallas_call x1, Pallas kernels: 1.67 us -> 0.1 us  [shards(): pl.pallas_call(functools.partial(pack_kernel, plan), out_shape=jax.ShapeD...]
    ppermute x5 -> x10, starting transfers between devices: 10.5 us -> 9.83 us  [send(): return lax.ppermute(v, ('row', 'col'), pairs)]
  transfers between devices with their start and end apart: 5 -> 10, of which waited for: 5 -> 6; matrix products, arithmetic and copies ran while one was open for 1% -> 0% of each run, Pallas kernels for 0% -> 0%
where the time goes in v2:
time: 35.2 us; the launch traced here: 34.9 us
  Pallas kernels  12.1 us (34%)
  waiting for transfers between devices  10.1 us (29%)
  starting transfers between devices  9.83 us (28%)
  local copies, waits for them, and re-layouts  2.87 us (8%)
    pallas_call x1, Pallas kernels, schur_call(): pl.pallas_call(functools.partial(main_kernel, plan, len(stacks)), grid=(p...  12 us
    ppermute x10, waiting for transfers between devices, send(): return lax.ppermute(v, ('row', 'col'), pairs)  10.1 us
    ppermute x10, starting transfers between devices, send(): return lax.ppermute(v, ('row', 'col'), pairs)  9.83 us
    unnamed x8, local copies, waits for them, and re-layouts  2.87 us
  transfers between devices with their start and end apart: 10, of which 6 were waited for; matrix products, arithmetic and copies ran while one was open for 0% of the time, Pallas kernels for 0%

profile of v2, /device:TPU:0, one launch (start us, length us, event | category | flops | bytes accessed | tf_op | source)
XLA Modules:
  0.0 34.9 jit_solution(12323527940862333361)
XLA Ops:
  0.0 0.0 copy-start.3
  0.0 0.7 %copy-done.3 = s32[32]{0:T(128)S(1)} copy-done((s32[32]{0:T(128)S(1)}, s32[32]{0:T(128)}, u32[]{:S(2)}) %copy-start.3) | copy-done | bytes 152
  0.7 0.0 copy-start
  0.7 0.8 %copy-done = f32[124,62]{0,1:T(8,128)S(1)} copy-done((f32[124,62]{0,1:T(8,128)S(1)}, f32[124,62]{0,1:T(8,128)}, u32[]{:S(2)}) %copy-start) | copy-done | bytes 30776
  1.4 0.0 copy-start.1
  1.4 0.8 %copy-done.1 = f32[124,62]{0,1:T(8,128)S(1)} copy-done((f32[124,62]{0,1:T(8,128)S(1)}, f32[124,62]{0,1:T(8,128)}, u32[]{:S(2)}) %copy-start.1) | copy-done | bytes 30776
  2.2 0.0 copy-start.2
  2.2 0.7 %copy-done.2 = s32[32,16]{0,1:T(8,128)S(1)} copy-done((s32[32,16]{0,1:T(8,128)S(1)}, s32[32,16]{0,1:T(8,128)}, u32[]{:S(2)}) %copy-start.2) | copy-done | bytes 2072
  2.9 0.1 pack.1
  3.0 5.1 %collective-permute-start.2 = (f32[72,128]{1,0:T(8,128)S(1)}, f32[72,128]{1,0:T(8,128)S(1)}, u32[]{:S(2)}, u32[]{:S(2)}) collective-permute-start(f32[72,128]{1,0:T(8,128)S(1)} %pack.1), channel_id=1, source_target_pairs={{0,6},{1,7},{2,4},{3,5},{4,2},{5,3},{6,0},{7,1},{8,14},{9,15},{10,... | collective-permute-start | bytes 110600 | tf_op jit(solution)/shard_map/ppermute | solution.py:180
  8.1 0.0 collective-permute-start.1
  8.1 0.6 %collective-permute-start = (f32[72,128]{1,0:T(8,128)S(1)}, f32[72,128]{1,0:T(8,128)S(1)}, u32[]{:S(2)}, u32[]{:S(2)}) collective-permute-start(f32[72,128]{1,0:T(8,128)S(1)} %pack.1), channel_id=1, source_target_pairs={{0,2},{1,3},{2,0},{3,1},{4,6},{5,7},{6,4},{7,5},{8,10},{9,11},{10,... | collective-permute-start | bytes 110600 | tf_op jit(solution)/shard_map/ppermute | solution.py:180
  8.7 1.3 %collective-permute-done.2 = f32[72,128]{1,0:T(8,128)S(1)} collective-permute-done((f32[72,128]{1,0:T(8,128)S(1)}, f32[72,128]{1,0:T(8,128)S(1)}, u32[]{:S(2)}, u32[]{:S(2)}) %collective-permute-start.2) | collective-permute-done | bytes 36896 | tf_op jit(solution)/shard_map/ppermute | solution.py:180
  10.0 2.9 %collective-permute-done.1 = f32[72,128]{1,0:T(8,128)S(1)} collective-permute-done((f32[72,128]{1,0:T(8,128)S(1)}, f32[72,128]{1,0:T(8,128)S(1)}, u32[]{:S(2)}, u32[]{:S(2)}) %collective-permute-start.1) | collective-permute-done | bytes 36896 | tf_op jit(solution)/shard_map/ppermute | solution.py:180
  12.9 0.0 collective-permute-done
  13.0 2.5 %collective-permute-start.5 = (f32[4,72,128]{2,1,0:T(8,128)S(1)}, f32[4,72,128]{2,1,0:T(8,128)S(1)}, u32[]{:S(2)}, u32[]{:S(2)}) collective-permute-start(f32[4,72,128]{2,1,0:T(8,128)S(1)} %pad_maximum_fusion.refs_0_), channel_id=1, source_target_pairs={{0,17},{1,16},{2,19},{3,18},{4,21},{5,20},{6,23},{7,22},{8,25},{9,... | collective-permute-start | bytes 442376 | tf_op jit(solution)/shard_map/ppermute | solution.py:180
  15.5 0.5 %collective-permute-start.4 = (f32[4,72,128]{2,1,0:T(8,128)S(1)}, f32[4,72,128]{2,1,0:T(8,128)S(1)}, u32[]{:S(2)}, u32[]{:S(2)}) collective-permute-start(f32[4,72,128]{2,1,0:T(8,128)S(1)} %pad_maximum_fusion.refs_0_), channel_id=1, source_target_pairs={{0,16},{1,17},{2,18},{3,19},{4,20},{5,21},{6,22},{7,23},{8,24},{9,... | collective-permute-start | bytes 442376 | tf_op jit(solution)/shard_map/ppermute | solution.py:180
  16.0 0.5 %collective-permute-start.3 = (f32[4,72,128]{2,1,0:T(8,128)S(1)}, f32[4,72,128]{2,1,0:T(8,128)S(1)}, u32[]{:S(2)}, u32[]{:S(2)}) collective-permute-start(f32[4,72,128]{2,1,0:T(8,128)S(1)} %pad_maximum_fusion.refs_0_), channel_id=1, source_target_pairs={{0,1},{1,0},{2,3},{3,2},{4,5},{5,4},{6,7},{7,6},{8,9},{9,8},{10,11... | collective-permute-start | bytes 442376 | tf_op jit(solution)/shard_map/ppermute | solution.py:180
  16.5 0.0 collective-permute-start.6
  16.5 3.1 %collective-permute-done.5.refs_3_ = f32[4,72,128]{2,1,0:T(8,128)S(1)} collective-permute-done((f32[4,72,128]{2,1,0:T(8,128)S(1)}, f32[4,72,128]{2,1,0:T(8,128)S(1)}, u32[]{:S(2)}, u32[]{:S(2)}) %collective-permute-start.5) | collective-permute-done | bytes 147488 | tf_op jit(solution)/shard_map/ppermute | solution.py:180
  19.7 0.0 collective-permute-start.9
  19.7 1.7 %collective-permute-done.4.refs_2_ = f32[4,72,128]{2,1,0:T(8,128)S(1)} collective-permute-done((f32[4,72,128]{2,1,0:T(8,128)S(1)}, f32[4,72,128]{2,1,0:T(8,128)S(1)}, u32[]{:S(2)}, u32[]{:S(2)}) %collective-permute-start.4) | collective-permute-done | bytes 147488 | tf_op jit(solution)/shard_map/ppermute | solution.py:180
  21.3 0.0 collective-permute-start.8
  21.3 0.0 collective-permute-done.3.refs_1_
  21.4 0.5 %collective-permute-start.7 = (f32[4,72,128]{2,1,0:T(8,128)S(1)}, f32[4,72,128]{2,1,0:T(8,128)S(1)}, u32[]{:S(2)}, u32[]{:S(2)}) collective-permute-start(f32[4,72,128]{2,1,0:T(8,128)S(1)} %collective-permute-done.3.refs_1_), channel_id=1, source_target_pairs={{0,8},{1,9},{2,10},{3,11},{4,12},{5,13},{6,14},{7,15},{8,0},{9,1},... | collective-permute-start | bytes 442376 | tf_op jit(solution)/shard_map/ppermute | solution.py:180
  21.9 0.0 collective-permute-done.6.refs_4_
  21.9 0.0 collective-permute-done.9.refs_7_
  21.9 0.9 %collective-permute-done.8.refs_6_ = f32[4,72,128]{2,1,0:T(8,128)S(1)} collective-permute-done((f32[4,72,128]{2,1,0:T(8,128)S(1)}, f32[4,72,128]{2,1,0:T(8,128)S(1)}, u32[]{:S(2)}, u32[]{:S(2)}) %collective-permute-start.8) | collective-permute-done | bytes 147488 | tf_op jit(solution)/shard_map/ppermute | solution.py:180
  22.7 0.2 collective-permute-done.7.refs_5_
  22.9 12.0 %schur.1 = f32[256,128]{1,0:T(8,128)} custom-call(f32[4,72,128]{2,1,0:T(8,128)S(1)} %pad_maximum_fusion.refs_0_, f32[4,72,128]{2,1,0:T(8,128)S(1)} %collective-permute-done.3.refs_1_, f32[4,72,128]{2,1,0:T(8,128)S(1)} %collective-permute-done.4.refs_2_, f32[4,72,128]{2,1,0:T(8,128)S(1)} %collective-permute-done.5.refs_3_, ...), custom_call_target="tpu_custom_call" | custom-call | tf_op jit(solution)/shard_map/schur/pallas_call | solution.py:192
  (1 shorter events, 0.0 us)
Async XLA Ops:
  0.0 0.7 %copy-start.3 = (s32[32]{0:T(128)S(1)}, s32[32]{0:T(128)}, u32[]{:S(2)}) copy-start(s32[32]{0:T(128)} %param.7) | copy-start | bytes 388
  0.7 0.8 %copy-start = (f32[124,62]{0,1:T(8,128)S(1)}, f32[124,62]{0,1:T(8,128)}, u32[]{:S(2)}) copy-start(f32[124,62]{0,1:T(8,128)} %param.4) | copy-start | bytes 92260
  1.4 0.8 %copy-start.1 = (f32[124,62]{0,1:T(8,128)S(1)}, f32[124,62]{0,1:T(8,128)}, u32[]{:S(2)}) copy-start(f32[124,62]{0,1:T(8,128)} %param.5) | copy-start | bytes 92260
  2.2 0.7 %copy-start.2 = (s32[32,16]{0,1:T(8,128)S(1)}, s32[32,16]{0,1:T(8,128)}, u32[]{:S(2)}) copy-start(s32[32,16]{0,1:T(8,128)} %param.6) | copy-start | bytes 6148
  3.0 7.1 %collective-permute-start.2 = (f32[72,128]{1,0:T(8,128)S(1)}, f32[72,128]{1,0:T(8,128)S(1)}, u32[]{:S(2)}, u32[]{:S(2)}) collective-permute-start(f32[72,128]{1,0:T(8,128)S(1)} %pack.1), channel_id=1, source_target_pairs={{0,6},{1,7},{2,4},{3,5},{4,2},{5,3},{6,0},{7,1},{8,14},{9,15},{10,... | collective-permute-start | bytes 110600 | tf_op jit(solution)/shard_map/ppermute | solution.py:180
  8.1 4.9 %collective-permute-start.1 = (f32[72,128]{1,0:T(8,128)S(1)}, f32[72,128]{1,0:T(8,128)S(1)}, u32[]{:S(2)}, u32[]{:S(2)}) collective-permute-start(f32[72,128]{1,0:T(8,128)S(1)} %pack.1), channel_id=1, source_target_pairs={{0,4},{1,5},{2,6},{3,7},{4,0},{5,1},{6,2},{7,3},{8,12},{9,13},{10,... | collective-permute-start | bytes 110600 | tf_op jit(solution)/shard_map/ppermute | solution.py:180
  8.1 4.9 %collective-permute-start = (f32[72,128]{1,0:T(8,128)S(1)}, f32[72,128]{1,0:T(8,128)S(1)}, u32[]{:S(2)}, u32[]{:S(2)}) collective-permute-start(f32[72,128]{1,0:T(8,128)S(1)} %pack.1), channel_id=1, source_target_pairs={{0,2},{1,3},{2,0},{3,1},{4,6},{5,7},{6,4},{7,5},{8,10},{9,11},{10,... | collective-permute-start | bytes 110600 | tf_op jit(solution)/shard_map/ppermute | solution.py:180
  13.0 6.7 %collective-permute-start.5 = (f32[4,72,128]{2,1,0:T(8,128)S(1)}, f32[4,72,128]{2,1,0:T(8,128)S(1)}, u32[]{:S(2)}, u32[]{:S(2)}) collective-permute-start(f32[4,72,128]{2,1,0:T(8,128)S(1)} %pad_maximum_fusion.refs_0_), channel_id=1, source_target_pairs={{0,17},{1,16},{2,19},{3,18},{4,21},{5,20},{6,23},{7,22},{8,25},{9,... | collective-permute-start | bytes 442376 | tf_op jit(solution)/shard_map/ppermute | solution.py:180
  15.5 5.9 %collective-permute-start.4 = (f32[4,72,128]{2,1,0:T(8,128)S(1)}, f32[4,72,128]{2,1,0:T(8,128)S(1)}, u32[]{:S(2)}, u32[]{:S(2)}) collective-permute-start(f32[4,72,128]{2,1,0:T(8,128)S(1)} %pad_maximum_fusion.refs_0_), channel_id=1, source_target_pairs={{0,16},{1,17},{2,18},{3,19},{4,20},{5,21},{6,22},{7,23},{8,24},{9,... | collective-permute-start | bytes 442376 | tf_op jit(solution)/shard_map/ppermute | solution.py:180
  16.0 5.3 %collective-permute-start.3 = (f32[4,72,128]{2,1,0:T(8,128)S(1)}, f32[4,72,128]{2,1,0:T(8,128)S(1)}, u32[]{:S(2)}, u32[]{:S(2)}) collective-permute-start(f32[4,72,128]{2,1,0:T(8,128)S(1)} %pad_maximum_fusion.refs_0_), channel_id=1, source_target_pairs={{0,1},{1,0},{2,3},{3,2},{4,5},{5,4},{6,7},{7,6},{8,9},{9,8},{10,11... | collective-permute-start | bytes 442376 | tf_op jit(solution)/shard_map/ppermute | solution.py:180
  16.5 5.3 %collective-permute-start.6 = (f32[4,72,128]{2,1,0:T(8,128)S(1)}, f32[4,72,128]{2,1,0:T(8,128)S(1)}, u32[]{:S(2)}, u32[]{:S(2)}) collective-permute-start(f32[4,72,128]{2,1,0:T(8,128)S(1)} %pad_maximum_fusion.refs_0_), channel_id=1, source_target_pairs={{0,8},{1,9},{2,10},{3,11},{4,12},{5,13},{6,14},{7,15},{8,0},{9,1},... | collective-permute-start | bytes 442376 | tf_op jit(solution)/shard_map/ppermute | solution.py:180
  19.7 2.2 %collective-permute-start.9 = (f32[4,72,128]{2,1,0:T(8,128)S(1)}, f32[4,72,128]{2,1,0:T(8,128)S(1)}, u32[]{:S(2)}, u32[]{:S(2)}) collective-permute-start(f32[4,72,128]{2,1,0:T(8,128)S(1)} %collective-permute-done.5.refs_3_), channel_id=1, source_target_pairs={{0,8},{1,9},{2,10},{3,11},{4,12},{5,13},{6,14},{7,15},{8,0},{9,1},... | collective-permute-start | bytes 442376 | tf_op jit(solution)/shard_map/ppermute | solution.py:180
  21.3 1.4 %collective-permute-start.8 = (f32[4,72,128]{2,1,0:T(8,128)S(1)}, f32[4,72,128]{2,1,0:T(8,128)S(1)}, u32[]{:S(2)}, u32[]{:S(2)}) collective-permute-start(f32[4,72,128]{2,1,0:T(8,128)S(1)} %collective-permute-done.4.refs_2_), channel_id=1, source_target_pairs={{0,8},{1,9},{2,10},{3,11},{4,12},{5,13},{6,14},{7,15},{8,0},{9,1},... | collective-permute-start | bytes 442376 | tf_op jit(solution)/shard_map/ppermute | solution.py:180
  21.4 1.6 %collective-permute-start.7 = (f32[4,72,128]{2,1,0:T(8,128)S(1)}, f32[4,72,128]{2,1,0:T(8,128)S(1)}, u32[]{:S(2)}, u32[]{:S(2)}) collective-permute-start(f32[4,72,128]{2,1,0:T(8,128)S(1)} %collective-permute-done.3.refs_1_), channel_id=1, source_target_pairs={{0,8},{1,9},{2,10},{3,11},{4,12},{5,13},{6,14},{7,15},{8,0},{9,1},... | collective-permute-start | bytes 442376 | tf_op jit(solution)/shard_map/ppermute | solution.py:180

commit v3 on v2

--- a/solution.py
+++ b/solution.py
@@ -96,8 +96,11 @@
 
     for t in range(tiles):
         ivec[t] = codes(me_r * cols + t * plan.fold) * slots
-    copy = pltpu.make_async_copy(ivec, idx, sem)
-    copy.start()
+    copies = []
+    for n in range(tiles * 2 * slots):
+        spot = idx.at[pl.ds(n * LANES, LANES)]
+        copies.append(pltpu.make_async_copy(ivec.at[n // (2 * slots), n % (2 * slots)], spot, sem.at[n]))
+        copies[-1].start()
     jcode = codes(me_c * rows + chunk * plan.fold)
 
     depth_iota = lax.broadcasted_iota(I32, (depth, LANES), 0)
@@ -150,15 +153,16 @@
                 put(j, i, v)
                 put(i, j, v.T)
     select(slots, zj)
-    copy.wait()
-
-    def eight(n, _):
-        tile_at, base = n // (LANES // 8), (n % (LANES // 8)) * 8
+    for copy in copies:
+        copy.wait()
+
+    def eight(tile_at, n):
+        base = n * 8
         for s in range(8):
             total = None
             for k in range(slots):
-                q = pl.multiple_of(idx[tile_at, slots + k, base + s], slots)
-                p = pl.multiple_of(idx[tile_at, k, base + s], slots)
+                q = pl.multiple_of(idx[base + ((tile_at * 2 * slots + slots + k) * LANES + s)], slots)
+                p = pl.multiple_of(idx[base + (tile_at * 2 * slots + k) * LANES + s], slots)
                 term = xj[pl.ds(q, slots), :] * zj[pl.ds(p, slots), :]
                 total = term if total is None else total + term
             acc[s * slots : (s + 1) * slots, :] = total
@@ -166,10 +170,11 @@
         for l in range(slots):
             v = acc[pl.ds(l, 8, stride=slots), :]
             out = v if out is None else out + v
-        out_ref[pl.ds(pl.multiple_of(n * 8, 8), 8), :] = out
-        return 0
-
-    lax.fori_loop(0, plan.ni // 8, eight, 0)
+        out_ref[tile_at * LANES + base : tile_at * LANES + base + 8, :] = out
+
+    for t in range(tiles):
+        for n in range(LANES // 8):
+            eight(t, n)
 
 
 def send(plan, v, row_xor, col_xor):
@@ -204,8 +209,8 @@
             pltpu.VMEM((plan.depth, plan.slots * LANES), BF16),
             pltpu.VMEM((plan.ni // LANES, 2 * plan.slots, LANES), I32),
             pltpu.VMEM((8 * plan.slots, LANES), F32),
-            pltpu.SMEM((plan.ni // LANES, 2 * plan.slots, LANES), I32),
-            pltpu.SemaphoreType.DMA,
+            pltpu.SMEM((plan.ni * 2 * plan.slots,), I32),
+            pltpu.SemaphoreType.DMA((plan.ni // LANES * 2 * plan.slots,)),
         ],
         compiler_params=pltpu.CompilerParams(vmem_limit_bytes=24 << 20),
         name="schur",

time: 35.2 us -> 30.6 us (0.87)
  Pallas kernels: 12.1 us -> 7.47 us
    pallas_call x1, Pallas kernels: 12 us -> 7.38 us  [schur_call(): pl.pallas_call(functools.partial(main_kernel, plan, len(stacks)), grid=(p...]
where the time goes in v3:
time: 30.6 us; the launch traced here: 30.3 us
  waiting for transfers between devices  10.1 us (33%)
  starting transfers between devices  9.83 us (32%)
  Pallas kernels  7.47 us (24%)
  local copies, waits for them, and re-layouts  2.87 us (9%)
    ppermute x10, waiting for transfers between devices, send(): return lax.ppermute(v, ('row', 'col'), pairs)  10.1 us
    ppermute x10, starting transfers between devices, send(): return lax.ppermute(v, ('row', 'col'), pairs)  9.83 us
    pallas_call x1, Pallas kernels, schur_call(): pl.pallas_call(functools.partial(main_kernel, plan, len(stacks)), grid=(p...  7.38 us
    unnamed x8, local copies, waits for them, and re-layouts  2.87 us
  transfers between devices with their start and end apart: 10, of which 6 were waited for; matrix products, arithmetic and copies ran while one was open for 0% of the time, Pallas kernels for 0%

profile of v3, /device:TPU:0, one launch (start us, length us, event | category | flops | bytes accessed | tf_op | source)
XLA Modules:
  0.0 30.3 jit_solution(13217966666553473161)
XLA Ops:
  0.0 0.0 copy-start.3
  0.0 0.7 %copy-done.3 = s32[32]{0:T(128)S(1)} copy-done((s32[32]{0:T(128)S(1)}, s32[32]{0:T(128)}, u32[]{:S(2)}) %copy-start.3) | copy-done | bytes 152
  0.7 0.0 copy-start
  0.7 0.8 %copy-done = f32[124,62]{0,1:T(8,128)S(1)} copy-done((f32[124,62]{0,1:T(8,128)S(1)}, f32[124,62]{0,1:T(8,128)}, u32[]{:S(2)}) %copy-start) | copy-done | bytes 30776
  1.4 0.0 copy-start.1
  1.4 0.8 %copy-done.1 = f32[124,62]{0,1:T(8,128)S(1)} copy-done((f32[124,62]{0,1:T(8,128)S(1)}, f32[124,62]{0,1:T(8,128)}, u32[]{:S(2)}) %copy-start.1) | copy-done | bytes 30776
  2.2 0.0 copy-start.2
  2.2 0.7 %copy-done.2 = s32[32,16]{0,1:T(8,128)S(1)} copy-done((s32[32,16]{0,1:T(8,128)S(1)}, s32[32,16]{0,1:T(8,128)}, u32[]{:S(2)}) %copy-start.2) | copy-done | bytes 2072
  2.9 0.1 pack.1
  3.0 5.1 %collective-permute-start.2 = (f32[72,128]{1,0:T(8,128)S(1)}, f32[72,128]{1,0:T(8,128)S(1)}, u32[]{:S(2)}, u32[]{:S(2)}) collective-permute-start(f32[72,128]{1,0:T(8,128)S(1)} %pack.1), channel_id=1, source_target_pairs={{0,6},{1,7},{2,4},{3,5},{4,2},{5,3},{6,0},{7,1},{8,14},{9,15},{10,... | collective-permute-start | bytes 110600 | tf_op jit(solution)/shard_map/ppermute | solution.py:185
  8.1 0.0 collective-permute-start.1
  8.1 0.6 %collective-permute-start = (f32[72,128]{1,0:T(8,128)S(1)}, f32[72,128]{1,0:T(8,128)S(1)}, u32[]{:S(2)}, u32[]{:S(2)}) collective-permute-start(f32[72,128]{1,0:T(8,128)S(1)} %pack.1), channel_id=1, source_target_pairs={{0,2},{1,3},{2,0},{3,1},{4,6},{5,7},{6,4},{7,5},{8,10},{9,11},{10,... | collective-permute-start | bytes 110600 | tf_op jit(solution)/shard_map/ppermute | solution.py:185
  8.7 1.3 %collective-permute-done.2 = f32[72,128]{1,0:T(8,128)S(1)} collective-permute-done((f32[72,128]{1,0:T(8,128)S(1)}, f32[72,128]{1,0:T(8,128)S(1)}, u32[]{:S(2)}, u32[]{:S(2)}) %collective-permute-start.2) | collective-permute-done | bytes 36896 | tf_op jit(solution)/shard_map/ppermute | solution.py:185
  10.0 2.9 %collective-permute-done.1 = f32[72,128]{1,0:T(8,128)S(1)} collective-permute-done((f32[72,128]{1,0:T(8,128)S(1)}, f32[72,128]{1,0:T(8,128)S(1)}, u32[]{:S(2)}, u32[]{:S(2)}) %collective-permute-start.1) | collective-permute-done | bytes 36896 | tf_op jit(solution)/shard_map/ppermute | solution.py:185
  12.9 0.0 collective-permute-done
  13.0 2.5 %collective-permute-start.5 = (f32[4,72,128]{2,1,0:T(8,128)S(1)}, f32[4,72,128]{2,1,0:T(8,128)S(1)}, u32[]{:S(2)}, u32[]{:S(2)}) collective-permute-start(f32[4,72,128]{2,1,0:T(8,128)S(1)} %pad_maximum_fusion.refs_0_), channel_id=1, source_target_pairs={{0,17},{1,16},{2,19},{3,18},{4,21},{5,20},{6,23},{7,22},{8,25},{9,... | collective-permute-start | bytes 442376 | tf_op jit(solution)/shard_map/ppermute | solution.py:185
  15.5 0.5 %collective-permute-start.4 = (f32[4,72,128]{2,1,0:T(8,128)S(1)}, f32[4,72,128]{2,1,0:T(8,128)S(1)}, u32[]{:S(2)}, u32[]{:S(2)}) collective-permute-start(f32[4,72,128]{2,1,0:T(8,128)S(1)} %pad_maximum_fusion.refs_0_), channel_id=1, source_target_pairs={{0,16},{1,17},{2,18},{3,19},{4,20},{5,21},{6,22},{7,23},{8,24},{9,... | collective-permute-start | bytes 442376 | tf_op jit(solution)/shard_map/ppermute | solution.py:185
  16.0 0.5 %collective-permute-start.3 = (f32[4,72,128]{2,1,0:T(8,128)S(1)}, f32[4,72,128]{2,1,0:T(8,128)S(1)}, u32[]{:S(2)}, u32[]{:S(2)}) collective-permute-start(f32[4,72,128]{2,1,0:T(8,128)S(1)} %pad_maximum_fusion.refs_0_), channel_id=1, source_target_pairs={{0,1},{1,0},{2,3},{3,2},{4,5},{5,4},{6,7},{7,6},{8,9},{9,8},{10,11... | collective-permute-start | bytes 442376 | tf_op jit(solution)/shard_map/ppermute | solution.py:185
  16.5 0.0 collective-permute-start.6
  16.5 3.1 %collective-permute-done.5.refs_3_ = f32[4,72,128]{2,1,0:T(8,128)S(1)} collective-permute-done((f32[4,72,128]{2,1,0:T(8,128)S(1)}, f32[4,72,128]{2,1,0:T(8,128)S(1)}, u32[]{:S(2)}, u32[]{:S(2)}) %collective-permute-start.5) | collective-permute-done | bytes 147488 | tf_op jit(solution)/shard_map/ppermute | solution.py:185
  19.7 0.0 collective-permute-start.9
  19.7 1.7 %collective-permute-done.4.refs_2_ = f32[4,72,128]{2,1,0:T(8,128)S(1)} collective-permute-done((f32[4,72,128]{2,1,0:T(8,128)S(1)}, f32[4,72,128]{2,1,0:T(8,128)S(1)}, u32[]{:S(2)}, u32[]{:S(2)}) %collective-permute-start.4) | collective-permute-done | bytes 147488 | tf_op jit(solution)/shard_map/ppermute | solution.py:185
  21.3 0.0 collective-permute-start.8
  21.3 0.0 collective-permute-done.3.refs_1_
  21.4 0.5 %collective-permute-start.7 = (f32[4,72,128]{2,1,0:T(8,128)S(1)}, f32[4,72,128]{2,1,0:T(8,128)S(1)}, u32[]{:S(2)}, u32[]{:S(2)}) collective-permute-start(f32[4,72,128]{2,1,0:T(8,128)S(1)} %collective-permute-done.3.refs_1_), channel_id=1, source_target_pairs={{0,8},{1,9},{2,10},{3,11},{4,12},{5,13},{6,14},{7,15},{8,0},{9,1},... | collective-permute-start | bytes 442376 | tf_op jit(solution)/shard_map/ppermute | solution.py:185
  21.9 0.0 collective-permute-done.6.refs_4_
  21.9 0.0 collective-permute-done.9.refs_7_
  21.9 0.9 %collective-permute-done.8.refs_6_ = f32[4,72,128]{2,1,0:T(8,128)S(1)} collective-permute-done((f32[4,72,128]{2,1,0:T(8,128)S(1)}, f32[4,72,128]{2,1,0:T(8,128)S(1)}, u32[]{:S(2)}, u32[]{:S(2)}) %collective-permute-start.8) | collective-permute-done | bytes 147488 | tf_op jit(solution)/shard_map/ppermute | solution.py:185
  22.7 0.2 collective-permute-done.7.refs_5_
  22.9 7.4 %schur.1 = f32[256,128]{1,0:T(8,128)} custom-call(f32[4,72,128]{2,1,0:T(8,128)S(1)} %pad_maximum_fusion.refs_0_, f32[4,72,128]{2,1,0:T(8,128)S(1)} %collective-permute-done.3.refs_1_, f32[4,72,128]{2,1,0:T(8,128)S(1)} %collective-permute-done.4.refs_2_, f32[4,72,128]{2,1,0:T(8,128)S(1)} %collective-permute-done.5.refs_3_, ...), custom_call_target="tpu_custom_call" | custom-call | tf_op jit(solution)/shard_map/schur/pallas_call | solution.py:197
  (1 shorter events, 0.0 us)
Async XLA Ops:
  0.0 0.7 %copy-start.3 = (s32[32]{0:T(128)S(1)}, s32[32]{0:T(128)}, u32[]{:S(2)}) copy-start(s32[32]{0:T(128)} %param.7) | copy-start | bytes 388
  0.7 0.8 %copy-start = (f32[124,62]{0,1:T(8,128)S(1)}, f32[124,62]{0,1:T(8,128)}, u32[]{:S(2)}) copy-start(f32[124,62]{0,1:T(8,128)} %param.4) | copy-start | bytes 92260
  1.4 0.8 %copy-start.1 = (f32[124,62]{0,1:T(8,128)S(1)}, f32[124,62]{0,1:T(8,128)}, u32[]{:S(2)}) copy-start(f32[124,62]{0,1:T(8,128)} %param.5) | copy-start | bytes 92260
  2.2 0.7 %copy-start.2 = (s32[32,16]{0,1:T(8,128)S(1)}, s32[32,16]{0,1:T(8,128)}, u32[]{:S(2)}) copy-start(s32[32,16]{0,1:T(8,128)} %param.6) | copy-start | bytes 6148
  3.0 7.1 %collective-permute-start.2 = (f32[72,128]{1,0:T(8,128)S(1)}, f32[72,128]{1,0:T(8,128)S(1)}, u32[]{:S(2)}, u32[]{:S(2)}) collective-permute-start(f32[72,128]{1,0:T(8,128)S(1)} %pack.1), channel_id=1, source_target_pairs={{0,6},{1,7},{2,4},{3,5},{4,2},{5,3},{6,0},{7,1},{8,14},{9,15},{10,... | collective-permute-start | bytes 110600 | tf_op jit(solution)/shard_map/ppermute | solution.py:185
  8.1 4.9 %collective-permute-start.1 = (f32[72,128]{1,0:T(8,128)S(1)}, f32[72,128]{1,0:T(8,128)S(1)}, u32[]{:S(2)}, u32[]{:S(2)}) collective-permute-start(f32[72,128]{1,0:T(8,128)S(1)} %pack.1), channel_id=1, source_target_pairs={{0,4},{1,5},{2,6},{3,7},{4,0},{5,1},{6,2},{7,3},{8,12},{9,13},{10,... | collective-permute-start | bytes 110600 | tf_op jit(solution)/shard_map/ppermute | solution.py:185
  8.1 4.9 %collective-permute-start = (f32[72,128]{1,0:T(8,128)S(1)}, f32[72,128]{1,0:T(8,128)S(1)}, u32[]{:S(2)}, u32[]{:S(2)}) collective-permute-start(f32[72,128]{1,0:T(8,128)S(1)} %pack.1), channel_id=1, source_target_pairs={{0,2},{1,3},{2,0},{3,1},{4,6},{5,7},{6,4},{7,5},{8,10},{9,11},{10,... | collective-permute-start | bytes 110600 | tf_op jit(solution)/shard_map/ppermute | solution.py:185
  13.0 6.7 %collective-permute-start.5 = (f32[4,72,128]{2,1,0:T(8,128)S(1)}, f32[4,72,128]{2,1,0:T(8,128)S(1)}, u32[]{:S(2)}, u32[]{:S(2)}) collective-permute-start(f32[4,72,128]{2,1,0:T(8,128)S(1)} %pad_maximum_fusion.refs_0_), channel_id=1, source_target_pairs={{0,17},{1,16},{2,19},{3,18},{4,21},{5,20},{6,23},{7,22},{8,25},{9,... | collective-permute-start | bytes 442376 | tf_op jit(solution)/shard_map/ppermute | solution.py:185
  15.5 5.9 %collective-permute-start.4 = (f32[4,72,128]{2,1,0:T(8,128)S(1)}, f32[4,72,128]{2,1,0:T(8,128)S(1)}, u32[]{:S(2)}, u32[]{:S(2)}) collective-permute-start(f32[4,72,128]{2,1,0:T(8,128)S(1)} %pad_maximum_fusion.refs_0_), channel_id=1, source_target_pairs={{0,16},{1,17},{2,18},{3,19},{4,20},{5,21},{6,22},{7,23},{8,24},{9,... | collective-permute-start | bytes 442376 | tf_op jit(solution)/shard_map/ppermute | solution.py:185
  16.0 5.3 %collective-permute-start.3 = (f32[4,72,128]{2,1,0:T(8,128)S(1)}, f32[4,72,128]{2,1,0:T(8,128)S(1)}, u32[]{:S(2)}, u32[]{:S(2)}) collective-permute-start(f32[4,72,128]{2,1,0:T(8,128)S(1)} %pad_maximum_fusion.refs_0_), channel_id=1, source_target_pairs={{0,1},{1,0},{2,3},{3,2},{4,5},{5,4},{6,7},{7,6},{8,9},{9,8},{10,11... | collective-permute-start | bytes 442376 | tf_op jit(solution)/shard_map/ppermute | solution.py:185
  16.5 5.3 %collective-permute-start.6 = (f32[4,72,128]{2,1,0:T(8,128)S(1)}, f32[4,72,128]{2,1,0:T(8,128)S(1)}, u32[]{:S(2)}, u32[]{:S(2)}) collective-permute-start(f32[4,72,128]{2,1,0:T(8,128)S(1)} %pad_maximum_fusion.refs_0_), channel_id=1, source_target_pairs={{0,8},{1,9},{2,10},{3,11},{4,12},{5,13},{6,14},{7,15},{8,0},{9,1},... | collective-permute-start | bytes 442376 | tf_op jit(solution)/shard_map/ppermute | solution.py:185
  19.7 2.2 %collective-permute-start.9 = (f32[4,72,128]{2,1,0:T(8,128)S(1)}, f32[4,72,128]{2,1,0:T(8,128)S(1)}, u32[]{:S(2)}, u32[]{:S(2)}) collective-permute-start(f32[4,72,128]{2,1,0:T(8,128)S(1)} %collective-permute-done.5.refs_3_), channel_id=1, source_target_pairs={{0,8},{1,9},{2,10},{3,11},{4,12},{5,13},{6,14},{7,15},{8,0},{9,1},... | collective-permute-start | bytes 442376 | tf_op jit(solution)/shard_map/ppermute | solution.py:185
  21.3 1.4 %collective-permute-start.8 = (f32[4,72,128]{2,1,0:T(8,128)S(1)}, f32[4,72,128]{2,1,0:T(8,128)S(1)}, u32[]{:S(2)}, u32[]{:S(2)}) collective-permute-start(f32[4,72,128]{2,1,0:T(8,128)S(1)} %collective-permute-done.4.refs_2_), channel_id=1, source_target_pairs={{0,8},{1,9},{2,10},{3,11},{4,12},{5,13},{6,14},{7,15},{8,0},{9,1},... | collective-permute-start | bytes 442376 | tf_op jit(solution)/shard_map/ppermute | solution.py:185
  21.4 1.6 %collective-permute-start.7 = (f32[4,72,128]{2,1,0:T(8,128)S(1)}, f32[4,72,128]{2,1,0:T(8,128)S(1)}, u32[]{:S(2)}, u32[]{:S(2)}) collective-permute-start(f32[4,72,128]{2,1,0:T(8,128)S(1)} %collective-permute-done.3.refs_1_), channel_id=1, source_target_pairs={{0,8},{1,9},{2,10},{3,11},{4,12},{5,13},{6,14},{7,15},{8,0},{9,1},... | collective-permute-start | bytes 442376 | tf_op jit(solution)/shard_map/ppermute | solution.py:185

commit v4 on v3

--- a/solution.py
+++ b/solution.py
@@ -33,10 +33,16 @@
         self.near = [(i << 1, k) for i in range(1 << (row_bits - 1)) for k in range(1 << y_bits)]
 
 
-def pack_kernel(plan, x_ref, z_ref, pos_ref, cnt_ref, out_ref):
+def pack_kernel(plan, x_in, z_in, pos_in, cnt_in, out_ref, x_ref, z_ref, pos_ref, cnt_ref, sem):
     nb, slot, wide = plan.nb, plan.slot, plan.wide
     me_r, me_c = lax.axis_index("row"), lax.axis_index("col")
+    copies = []
+    for n, (src, dst) in enumerate(((x_in, x_ref), (z_in, z_ref), (pos_in, pos_ref), (cnt_in, cnt_ref))):
+        copies.append(pltpu.make_async_copy(src, dst, sem.at[n]))
+        copies[-1].start()
     out_ref[...] = jnp.zeros_like(out_ref)
+    for copy in copies:
+        copy.wait()
     a = lax.broadcasted_iota(I32, (nb, plan.mb), 0) + me_c * nb
     b = lax.broadcasted_iota(I32, (nb, plan.mb), 1) + me_r * plan.mb
     z = z_ref[...]
@@ -219,12 +225,21 @@
 
 def shards(rows, cols, moment_x, zinv, positions, entry_count):
     plan = Plan(rows, cols, moment_x.shape, positions.shape)
+    args = (moment_x.T, zinv.T, positions.T, entry_count.reshape(1, -1))
     packed = pl.pallas_call(
         functools.partial(pack_kernel, plan),
+        in_specs=[pl.BlockSpec(memory_space=pltpu.HBM)] * 4,
         out_shape=jax.ShapeDtypeStruct((plan.payload, LANES), F32),
+        scratch_shapes=[
+            pltpu.VMEM((plan.nb, plan.mb), F32),
+            pltpu.VMEM((plan.nb, plan.mb), F32),
+            pltpu.VMEM((2 * plan.slots, plan.local), I32),
+            pltpu.VMEM((1, plan.local), I32),
+            pltpu.SemaphoreType.DMA((4,)),
+        ],
         compiler_params=pltpu.CompilerParams(vmem_limit_bytes=4 << 20),
         name="pack",
-    )(moment_x.T, zinv.T, positions.T, entry_count.reshape(1, -1))
+    )(*[pltpu.with_memory_space_constraint(v, pltpu.HBM) for v in args])
     return schur_call(plan, gather(plan, packed))
 
 

time: 30.6 us -> 28.5 us (0.931)
  local copies, waits for them, and re-layouts: 2.87 us -> 0 us
  Pallas kernels: 7.47 us -> 8.29 us
    unnamed x8 -> x0, local copies, waits for them, and re-layouts: 2.87 us -> none
    pallas_call x1, Pallas kernels: 0.1 us -> 0.9 us  [shards(): pl.pallas_call(functools.partial(pack_kernel, plan), in_specs=[pl.BlockSp...]
where the time goes in v4:
time: 28.5 us; the launch traced here: 28.3 us
  waiting for transfers between devices  10.1 us (35%)
  starting transfers between devices  9.85 us (35%)
  Pallas kernels  8.29 us (29%)
    ppermute x10, waiting for transfers between devices, send(): return lax.ppermute(v, ('row', 'col'), pairs)  10.1 us
    ppermute x10, starting transfers between devices, send(): return lax.ppermute(v, ('row', 'col'), pairs)  9.85 us
    pallas_call x1, Pallas kernels, schur_call(): pl.pallas_call(functools.partial(main_kernel, plan, len(stacks)), grid=(p...  7.38 us
    pallas_call x1, Pallas kernels, shards(): pl.pallas_call(functools.partial(pack_kernel, plan), in_specs=[pl.BlockSp...  0.9 us
  transfers between devices with their start and end apart: 10, of which 6 were waited for; matrix products, arithmetic and copies ran while one was open for 0% of the time, Pallas kernels for 0%

profile of v4, /device:TPU:0, one launch (start us, length us, event | category | flops | bytes accessed | tf_op | source)
XLA Modules:
  0.0 28.3 jit_solution(4922112421764865736)
XLA Ops:
  0.0 0.9 %pack.1 = f32[72,128]{1,0:T(8,128)S(1)} custom-call(f32[62,124]{1,0:T(8,128)} %bitcast.12, f32[62,124]{1,0:T(8,128)} %bitcast.13, s32[16,32]{1,0:T(8,128)} %bitcast.14, s32[1,32]{1,0:T(1,128)} %bitcast.15), custom_call_target="tpu_custom_call" | custom-call | tf_op jit(solution)/shard_map/pack/pallas_call | solution.py:229
  0.9 5.1 %collective-permute-start.2 = (f32[72,128]{1,0:T(8,128)S(1)}, f32[72,128]{1,0:T(8,128)S(1)}, u32[]{:S(2)}, u32[]{:S(2)}) collective-permute-start(f32[72,128]{1,0:T(8,128)S(1)} %pack.1), channel_id=1, source_target_pairs={{0,6},{1,7},{2,4},{3,5},{4,2},{5,3},{6,0},{7,1},{8,14},{9,15},{10,... | collective-permute-start | bytes 110600 | tf_op jit(solution)/shard_map/ppermute | solution.py:191
  6.1 0.0 collective-permute-start.1
  6.1 0.6 %collective-permute-start = (f32[72,128]{1,0:T(8,128)S(1)}, f32[72,128]{1,0:T(8,128)S(1)}, u32[]{:S(2)}, u32[]{:S(2)}) collective-permute-start(f32[72,128]{1,0:T(8,128)S(1)} %pack.1), channel_id=1, source_target_pairs={{0,2},{1,3},{2,0},{3,1},{4,6},{5,7},{6,4},{7,5},{8,10},{9,11},{10,... | collective-permute-start | bytes 110600 | tf_op jit(solution)/shard_map/ppermute | solution.py:191
  6.7 1.3 %collective-permute-done.2 = f32[72,128]{1,0:T(8,128)S(1)} collective-permute-done((f32[72,128]{1,0:T(8,128)S(1)}, f32[72,128]{1,0:T(8,128)S(1)}, u32[]{:S(2)}, u32[]{:S(2)}) %collective-permute-start.2) | collective-permute-done | bytes 36896 | tf_op jit(solution)/shard_map/ppermute | solution.py:191
  8.0 2.9 %collective-permute-done.1 = f32[72,128]{1,0:T(8,128)S(1)} collective-permute-done((f32[72,128]{1,0:T(8,128)S(1)}, f32[72,128]{1,0:T(8,128)S(1)}, u32[]{:S(2)}, u32[]{:S(2)}) %collective-permute-start.1) | collective-permute-done | bytes 36896 | tf_op jit(solution)/shard_map/ppermute | solution.py:191
  10.9 0.0 collective-permute-done
  10.9 2.5 %collective-permute-start.5 = (f32[4,72,128]{2,1,0:T(8,128)S(1)}, f32[4,72,128]{2,1,0:T(8,128)S(1)}, u32[]{:S(2)}, u32[]{:S(2)}) collective-permute-start(f32[4,72,128]{2,1,0:T(8,128)S(1)} %pad_maximum_fusion.refs_0_), channel_id=1, source_target_pairs={{0,17},{1,16},{2,19},{3,18},{4,21},{5,20},{6,23},{7,22},{8,25},{9,... | collective-permute-start | bytes 442376 | tf_op jit(solution)/shard_map/ppermute | solution.py:191
  13.4 0.5 %collective-permute-start.4 = (f32[4,72,128]{2,1,0:T(8,128)S(1)}, f32[4,72,128]{2,1,0:T(8,128)S(1)}, u32[]{:S(2)}, u32[]{:S(2)}) collective-permute-start(f32[4,72,128]{2,1,0:T(8,128)S(1)} %pad_maximum_fusion.refs_0_), channel_id=1, source_target_pairs={{0,16},{1,17},{2,18},{3,19},{4,20},{5,21},{6,22},{7,23},{8,24},{9,... | collective-permute-start | bytes 442376 | tf_op jit(solution)/shard_map/ppermute | solution.py:191
  14.0 0.5 %collective-permute-start.3 = (f32[4,72,128]{2,1,0:T(8,128)S(1)}, f32[4,72,128]{2,1,0:T(8,128)S(1)}, u32[]{:S(2)}, u32[]{:S(2)}) collective-permute-start(f32[4,72,128]{2,1,0:T(8,128)S(1)} %pad_maximum_fusion.refs_0_), channel_id=1, source_target_pairs={{0,1},{1,0},{2,3},{3,2},{4,5},{5,4},{6,7},{7,6},{8,9},{9,8},{10,11... | collective-permute-start | bytes 442376 | tf_op jit(solution)/shard_map/ppermute | solution.py:191
  14.5 0.0 collective-permute-start.6
  14.5 3.1 %collective-permute-done.5.refs_3_ = f32[4,72,128]{2,1,0:T(8,128)S(1)} collective-permute-done((f32[4,72,128]{2,1,0:T(8,128)S(1)}, f32[4,72,128]{2,1,0:T(8,128)S(1)}, u32[]{:S(2)}, u32[]{:S(2)}) %collective-permute-start.5) | collective-permute-done | bytes 147488 | tf_op jit(solution)/shard_map/ppermute | solution.py:191
  17.6 0.0 collective-permute-start.9
  17.6 1.7 %collective-permute-done.4.refs_2_ = f32[4,72,128]{2,1,0:T(8,128)S(1)} collective-permute-done((f32[4,72,128]{2,1,0:T(8,128)S(1)}, f32[4,72,128]{2,1,0:T(8,128)S(1)}, u32[]{:S(2)}, u32[]{:S(2)}) %collective-permute-start.4) | collective-permute-done | bytes 147488 | tf_op jit(solution)/shard_map/ppermute | solution.py:191
  19.3 0.0 collective-permute-start.8
  19.3 0.0 collective-permute-done.3.refs_1_
  19.3 0.5 %collective-permute-start.7 = (f32[4,72,128]{2,1,0:T(8,128)S(1)}, f32[4,72,128]{2,1,0:T(8,128)S(1)}, u32[]{:S(2)}, u32[]{:S(2)}) collective-permute-start(f32[4,72,128]{2,1,0:T(8,128)S(1)} %collective-permute-done.3.refs_1_), channel_id=1, source_target_pairs={{0,8},{1,9},{2,10},{3,11},{4,12},{5,13},{6,14},{7,15},{8,0},{9,1},... | collective-permute-start | bytes 442376 | tf_op jit(solution)/shard_map/ppermute | solution.py:191
  19.8 0.0 collective-permute-done.6.refs_4_
  19.8 0.0 collective-permute-done.9.refs_7_
  19.8 0.9 %collective-permute-done.8.refs_6_ = f32[4,72,128]{2,1,0:T(8,128)S(1)} collective-permute-done((f32[4,72,128]{2,1,0:T(8,128)S(1)}, f32[4,72,128]{2,1,0:T(8,128)S(1)}, u32[]{:S(2)}, u32[]{:S(2)}) %collective-permute-start.8) | collective-permute-done | bytes 147488 | tf_op jit(solution)/shard_map/ppermute | solution.py:191
  20.7 0.2 collective-permute-done.7.refs_5_
  20.9 7.4 %schur.1 = f32[256,128]{1,0:T(8,128)} custom-call(f32[4,72,128]{2,1,0:T(8,128)S(1)} %pad_maximum_fusion.refs_0_, f32[4,72,128]{2,1,0:T(8,128)S(1)} %collective-permute-done.3.refs_1_, f32[4,72,128]{2,1,0:T(8,128)S(1)} %collective-permute-done.4.refs_2_, f32[4,72,128]{2,1,0:T(8,128)S(1)} %collective-permute-done.5.refs_3_, ...), custom_call_target="tpu_custom_call" | custom-call | tf_op jit(solution)/shard_map/schur/pallas_call | solution.py:203
  (1 shorter events, 0.0 us)
Async XLA Ops:
  0.9 7.1 %collective-permute-start.2 = (f32[72,128]{1,0:T(8,128)S(1)}, f32[72,128]{1,0:T(8,128)S(1)}, u32[]{:S(2)}, u32[]{:S(2)}) collective-permute-start(f32[72,128]{1,0:T(8,128)S(1)} %pack.1), channel_id=1, source_target_pairs={{0,6},{1,7},{2,4},{3,5},{4,2},{5,3},{6,0},{7,1},{8,14},{9,15},{10,... | collective-permute-start | bytes 110600 | tf_op jit(solution)/shard_map/ppermute | solution.py:191
  6.1 4.9 %collective-permute-start.1 = (f32[72,128]{1,0:T(8,128)S(1)}, f32[72,128]{1,0:T(8,128)S(1)}, u32[]{:S(2)}, u32[]{:S(2)}) collective-permute-start(f32[72,128]{1,0:T(8,128)S(1)} %pack.1), channel_id=1, source_target_pairs={{0,4},{1,5},{2,6},{3,7},{4,0},{5,1},{6,2},{7,3},{8,12},{9,13},{10,... | collective-permute-start | bytes 110600 | tf_op jit(solution)/shard_map/ppermute | solution.py:191
  6.1 4.9 %collective-permute-start = (f32[72,128]{1,0:T(8,128)S(1)}, f32[72,128]{1,0:T(8,128)S(1)}, u32[]{:S(2)}, u32[]{:S(2)}) collective-permute-start(f32[72,128]{1,0:T(8,128)S(1)} %pack.1), channel_id=1, source_target_pairs={{0,2},{1,3},{2,0},{3,1},{4,6},{5,7},{6,4},{7,5},{8,10},{9,11},{10,... | collective-permute-start | bytes 110600 | tf_op jit(solution)/shard_map/ppermute | solution.py:191
  10.9 6.7 %collective-permute-start.5 = (f32[4,72,128]{2,1,0:T(8,128)S(1)}, f32[4,72,128]{2,1,0:T(8,128)S(1)}, u32[]{:S(2)}, u32[]{:S(2)}) collective-permute-start(f32[4,72,128]{2,1,0:T(8,128)S(1)} %pad_maximum_fusion.refs_0_), channel_id=1, source_target_pairs={{0,17},{1,16},{2,19},{3,18},{4,21},{5,20},{6,23},{7,22},{8,25},{9,... | collective-permute-start | bytes 442376 | tf_op jit(solution)/shard_map/ppermute | solution.py:191
  13.4 5.9 %collective-permute-start.4 = (f32[4,72,128]{2,1,0:T(8,128)S(1)}, f32[4,72,128]{2,1,0:T(8,128)S(1)}, u32[]{:S(2)}, u32[]{:S(2)}) collective-permute-start(f32[4,72,128]{2,1,0:T(8,128)S(1)} %pad_maximum_fusion.refs_0_), channel_id=1, source_target_pairs={{0,16},{1,17},{2,18},{3,19},{4,20},{5,21},{6,22},{7,23},{8,24},{9,... | collective-permute-start | bytes 442376 | tf_op jit(solution)/shard_map/ppermute | solution.py:191
  14.0 5.3 %collective-permute-start.3 = (f32[4,72,128]{2,1,0:T(8,128)S(1)}, f32[4,72,128]{2,1,0:T(8,128)S(1)}, u32[]{:S(2)}, u32[]{:S(2)}) collective-permute-start(f32[4,72,128]{2,1,0:T(8,128)S(1)} %pad_maximum_fusion.refs_0_), channel_id=1, source_target_pairs={{0,1},{1,0},{2,3},{3,2},{4,5},{5,4},{6,7},{7,6},{8,9},{9,8},{10,11... | collective-permute-start | bytes 442376 | tf_op jit(solution)/shard_map/ppermute | solution.py:191
  14.5 5.3 %collective-permute-start.6 = (f32[4,72,128]{2,1,0:T(8,128)S(1)}, f32[4,72,128]{2,1,0:T(8,128)S(1)}, u32[]{:S(2)}, u32[]{:S(2)}) collective-permute-start(f32[4,72,128]{2,1,0:T(8,128)S(1)} %pad_maximum_fusion.refs_0_), channel_id=1, source_target_pairs={{0,8},{1,9},{2,10},{3,11},{4,12},{5,13},{6,14},{7,15},{8,0},{9,1},... | collective-permute-start | bytes 442376 | tf_op jit(solution)/shard_map/ppermute | solution.py:191
  17.6 2.2 %collective-permute-start.9 = (f32[4,72,128]{2,1,0:T(8,128)S(1)}, f32[4,72,128]{2,1,0:T(8,128)S(1)}, u32[]{:S(2)}, u32[]{:S(2)}) collective-permute-start(f32[4,72,128]{2,1,0:T(8,128)S(1)} %collective-permute-done.5.refs_3_), channel_id=1, source_target_pairs={{0,8},{1,9},{2,10},{3,11},{4,12},{5,13},{6,14},{7,15},{8,0},{9,1},... | collective-permute-start | bytes 442376 | tf_op jit(solution)/shard_map/ppermute | solution.py:191
  19.3 1.4 %collective-permute-start.8 = (f32[4,72,128]{2,1,0:T(8,128)S(1)}, f32[4,72,128]{2,1,0:T(8,128)S(1)}, u32[]{:S(2)}, u32[]{:S(2)}) collective-permute-start(f32[4,72,128]{2,1,0:T(8,128)S(1)} %collective-permute-done.4.refs_2_), channel_id=1, source_target_pairs={{0,8},{1,9},{2,10},{3,11},{4,12},{5,13},{6,14},{7,15},{8,0},{9,1},... | collective-permute-start | bytes 442376 | tf_op jit(solution)/shard_map/ppermute | solution.py:191
  19.3 1.6 %collective-permute-start.7 = (f32[4,72,128]{2,1,0:T(8,128)S(1)}, f32[4,72,128]{2,1,0:T(8,128)S(1)}, u32[]{:S(2)}, u32[]{:S(2)}) collective-permute-start(f32[4,72,128]{2,1,0:T(8,128)S(1)} %collective-permute-done.3.refs_1_), channel_id=1, source_target_pairs={{0,8},{1,9},{2,10},{3,11},{4,12},{5,13},{6,14},{7,15},{8,0},{9,1},... | collective-permute-start | bytes 442376 | tf_op jit(solution)/shard_map/ppermute | solution.py:191

commit v5 on v4

--- a/solution.py
+++ b/solution.py
@@ -65,7 +65,7 @@
 
 def main_kernel(plan, n_in, *refs):
     ins, out_ref = refs[:n_in], refs[n_in]
-    misc, mat, left, xj, zj, pick, ivec, acc, idx, sem = refs[n_in + 1 :]
+    misc, mat, xleft, zleft, xj, zj, xpick, zpick, ivec, acc, idx, sem = refs[n_in + 1 :]
     slot, cols, rows = plan.slot, plan.cols, plan.rows
     slots, tiles, depth = plan.slots, plan.ni // LANES, plan.depth
     me_r, me_c = lax.axis_index("row"), lax.axis_index("col")
@@ -117,31 +117,35 @@
     def tile(i, j):
         return mat[j, i * LANES : (i + 1) * LANES, :]
 
-    def put(i, j, v):
+    def put(left, i, j, v):
         hi = v.astype(BF16)
         lo = (v - hi.astype(F32)).astype(BF16)
         left[i * LANES : (i + 1) * LANES, j * LANES : (j + 1) * LANES] = hi
         left[depth + i * LANES : depth + (i + 1) * LANES, j * LANES : (j + 1) * LANES] = lo
 
-    def select(base, out):
+    def mark(base, pick):
         for l in range(slots):
             at = jcode[base + l : base + l + 1, :]
             pick[:, l * LANES : (l + 1) * LANES] = jnp.where(depth_iota == at, 1.0, 0.0).astype(BF16)
+
+    def select(left, pick, out):
         for m in range(slots // 2):
             res = jnp.dot(left[...], pick[:, m * 256 : (m + 1) * 256], preferred_element_type=F32)
             res = res[:depth] + res[depth:]
             for l in range(2):
                 out[pl.ds(2 * m + l, depth, stride=slots), :] = res[:, l * LANES : (l + 1) * LANES]
 
+    mark(0, xpick)
     for i in range(n_tile):
         for j in range(i, n_tile):
             v = tile(i, j)
             if i == j:
-                put(i, i, jnp.where(ra <= rb, v, v.T))
+                put(xleft, i, i, jnp.where(ra <= rb, v, v.T))
             else:
-                put(i, j, v)
-                put(j, i, v.T)
-    select(0, xj)
+                put(xleft, i, j, v)
+                put(xleft, j, i, v.T)
+    select(xleft, xpick, xj)
+    mark(slots, zpick)
     per_tile = LANES // slot
     for i in range(n_tile):
         for j in range(i, n_tile):
@@ -154,11 +158,11 @@
                     if per > 1 and r % per:
                         row = pltpu.roll(row, (r % per) * plan.wide, 1)
                     diag = row if diag is None else diag + row
-                put(i, i, jnp.where(ra > rb, v, jnp.where(ra == rb, diag, v.T)))
+                put(zleft, i, i, jnp.where(ra > rb, v, jnp.where(ra == rb, diag, v.T)))
             else:
-                put(j, i, v)
-                put(i, j, v.T)
-    select(slots, zj)
+                put(zleft, j, i, v)
+                put(zleft, i, j, v.T)
+    select(zleft, zpick, zj)
     for copy in copies:
         copy.wait()
 
@@ -210,8 +214,10 @@
             pltpu.VMEM((plan.rows * plan.cols, EXTRA, LANES), F32),
             pltpu.VMEM((n_tile, plan.depth, LANES), F32),
             pltpu.VMEM((2 * plan.depth, plan.depth), BF16),
+            pltpu.VMEM((2 * plan.depth, plan.depth), BF16),
             pltpu.VMEM((plan.depth * plan.slots, LANES), F32),
             pltpu.VMEM((plan.depth * plan.slots, LANES), F32),
+            pltpu.VMEM((plan.depth, plan.slots * LANES), BF16),
             pltpu.VMEM((plan.depth, plan.slots * LANES), BF16),
             pltpu.VMEM((plan.ni // LANES, 2 * plan.slots, LANES), I32),
             pltpu.VMEM((8 * plan.slots, LANES), F32),

time: 28.5 us -> 28 us (0.982)
  Pallas kernels: 8.29 us -> 7.85 us
    pallas_call x1, Pallas kernels: 7.38 us -> 6.94 us  [schur_call(): pl.pallas_call(functools.partial(main_kernel, plan, len(stacks)), grid=(p...]
where the time goes in v5:
time: 28 us; the launch traced here: 27.8 us
  waiting for transfers between devices  10.1 us (36%)
  starting transfers between devices  9.85 us (35%)
  Pallas kernels  7.85 us (28%)
    ppermute x10, waiting for transfers between devices, send(): return lax.ppermute(v, ('row', 'col'), pairs)  10.1 us
    ppermute x10, starting transfers between devices, send(): return lax.ppermute(v, ('row', 'col'), pairs)  9.85 us
    pallas_call x1, Pallas kernels, schur_call(): pl.pallas_call(functools.partial(main_kernel, plan, len(stacks)), grid=(p...  6.94 us
    pallas_call x1, Pallas kernels, shards(): pl.pallas_call(functools.partial(pack_kernel, plan), in_specs=[pl.BlockSp...  0.9 us
  transfers between devices with their start and end apart: 10, of which 6 were waited for; matrix products, arithmetic and copies ran while one was open for 0% of the time, Pallas kernels for 0%

profile of v5, /device:TPU:0, one launch (start us, length us, event | category | flops | bytes accessed | tf_op | source)
XLA Modules:
  0.0 27.8 jit_solution(16790253473932026549)
XLA Ops:
  0.0 0.9 %pack.1 = f32[72,128]{1,0:T(8,128)S(1)} custom-call(f32[62,124]{1,0:T(8,128)} %bitcast.12, f32[62,124]{1,0:T(8,128)} %bitcast.13, s32[16,32]{1,0:T(8,128)} %bitcast.14, s32[1,32]{1,0:T(1,128)} %bitcast.15), custom_call_target="tpu_custom_call" | custom-call | tf_op jit(solution)/shard_map/pack/pallas_call | solution.py:235
  0.9 5.1 %collective-permute-start.2 = (f32[72,128]{1,0:T(8,128)S(1)}, f32[72,128]{1,0:T(8,128)S(1)}, u32[]{:S(2)}, u32[]{:S(2)}) collective-permute-start(f32[72,128]{1,0:T(8,128)S(1)} %pack.1), channel_id=1, source_target_pairs={{0,6},{1,7},{2,4},{3,5},{4,2},{5,3},{6,0},{7,1},{8,14},{9,15},{10,... | collective-permute-start | bytes 110600 | tf_op jit(solution)/shard_map/ppermute | solution.py:195
  6.1 0.0 collective-permute-start.1
  6.1 0.6 %collective-permute-start = (f32[72,128]{1,0:T(8,128)S(1)}, f32[72,128]{1,0:T(8,128)S(1)}, u32[]{:S(2)}, u32[]{:S(2)}) collective-permute-start(f32[72,128]{1,0:T(8,128)S(1)} %pack.1), channel_id=1, source_target_pairs={{0,2},{1,3},{2,0},{3,1},{4,6},{5,7},{6,4},{7,5},{8,10},{9,11},{10,... | collective-permute-start | bytes 110600 | tf_op jit(solution)/shard_map/ppermute | solution.py:195
  6.7 1.3 %collective-permute-done.2 = f32[72,128]{1,0:T(8,128)S(1)} collective-permute-done((f32[72,128]{1,0:T(8,128)S(1)}, f32[72,128]{1,0:T(8,128)S(1)}, u32[]{:S(2)}, u32[]{:S(2)}) %collective-permute-start.2) | collective-permute-done | bytes 36896 | tf_op jit(solution)/shard_map/ppermute | solution.py:195
  8.0 2.9 %collective-permute-done.1 = f32[72,128]{1,0:T(8,128)S(1)} collective-permute-done((f32[72,128]{1,0:T(8,128)S(1)}, f32[72,128]{1,0:T(8,128)S(1)}, u32[]{:S(2)}, u32[]{:S(2)}) %collective-permute-start.1) | collective-permute-done | bytes 36896 | tf_op jit(solution)/shard_map/ppermute | solution.py:195
  10.9 0.0 collective-permute-done
  10.9 2.5 %collective-permute-start.5 = (f32[4,72,128]{2,1,0:T(8,128)S(1)}, f32[4,72,128]{2,1,0:T(8,128)S(1)}, u32[]{:S(2)}, u32[]{:S(2)}) collective-permute-start(f32[4,72,128]{2,1,0:T(8,128)S(1)} %pad_maximum_fusion.refs_0_), channel_id=1, source_target_pairs={{0,17},{1,16},{2,19},{3,18},{4,21},{5,20},{6,23},{7,22},{8,25},{9,... | collective-permute-start | bytes 442376 | tf_op jit(solution)/shard_map/ppermute | solution.py:195
  13.4 0.5 %collective-permute-start.4 = (f32[4,72,128]{2,1,0:T(8,128)S(1)}, f32[4,72,128]{2,1,0:T(8,128)S(1)}, u32[]{:S(2)}, u32[]{:S(2)}) collective-permute-start(f32[4,72,128]{2,1,0:T(8,128)S(1)} %pad_maximum_fusion.refs_0_), channel_id=1, source_target_pairs={{0,16},{1,17},{2,18},{3,19},{4,20},{5,21},{6,22},{7,23},{8,24},{9,... | collective-permute-start | bytes 442376 | tf_op jit(solution)/shard_map/ppermute | solution.py:195
  14.0 0.5 %collective-permute-start.3 = (f32[4,72,128]{2,1,0:T(8,128)S(1)}, f32[4,72,128]{2,1,0:T(8,128)S(1)}, u32[]{:S(2)}, u32[]{:S(2)}) collective-permute-start(f32[4,72,128]{2,1,0:T(8,128)S(1)} %pad_maximum_fusion.refs_0_), channel_id=1, source_target_pairs={{0,1},{1,0},{2,3},{3,2},{4,5},{5,4},{6,7},{7,6},{8,9},{9,8},{10,11... | collective-permute-start | bytes 442376 | tf_op jit(solution)/shard_map/ppermute | solution.py:195
  14.5 0.0 collective-permute-start.6
  14.5 3.1 %collective-permute-done.5.refs_3_ = f32[4,72,128]{2,1,0:T(8,128)S(1)} collective-permute-done((f32[4,72,128]{2,1,0:T(8,128)S(1)}, f32[4,72,128]{2,1,0:T(8,128)S(1)}, u32[]{:S(2)}, u32[]{:S(2)}) %collective-permute-start.5) | collective-permute-done | bytes 147488 | tf_op jit(solution)/shard_map/ppermute | solution.py:195
  17.6 0.0 collective-permute-start.9
  17.6 1.7 %collective-permute-done.4.refs_2_ = f32[4,72,128]{2,1,0:T(8,128)S(1)} collective-permute-done((f32[4,72,128]{2,1,0:T(8,128)S(1)}, f32[4,72,128]{2,1,0:T(8,128)S(1)}, u32[]{:S(2)}, u32[]{:S(2)}) %collective-permute-start.4) | collective-permute-done | bytes 147488 | tf_op jit(solution)/shard_map/ppermute | solution.py:195
  19.3 0.0 collective-permute-start.8
  19.3 0.0 collective-permute-done.3.refs_1_
  19.3 0.5 %collective-permute-start.7 = (f32[4,72,128]{2,1,0:T(8,128)S(1)}, f32[4,72,128]{2,1,0:T(8,128)S(1)}, u32[]{:S(2)}, u32[]{:S(2)}) collective-permute-start(f32[4,72,128]{2,1,0:T(8,128)S(1)} %collective-permute-done.3.refs_1_), channel_id=1, source_target_pairs={{0,8},{1,9},{2,10},{3,11},{4,12},{5,13},{6,14},{7,15},{8,0},{9,1},... | collective-permute-start | bytes 442376 | tf_op jit(solution)/shard_map/ppermute | solution.py:195
  19.8 0.0 collective-permute-done.6.refs_4_
  19.8 0.0 collective-permute-done.9.refs_7_
  19.8 0.9 %collective-permute-done.8.refs_6_ = f32[4,72,128]{2,1,0:T(8,128)S(1)} collective-permute-done((f32[4,72,128]{2,1,0:T(8,128)S(1)}, f32[4,72,128]{2,1,0:T(8,128)S(1)}, u32[]{:S(2)}, u32[]{:S(2)}) %collective-permute-start.8) | collective-permute-done | bytes 147488 | tf_op jit(solution)/shard_map/ppermute | solution.py:195
  20.7 0.2 collective-permute-done.7.refs_5_
  20.9 6.9 %schur.1 = f32[256,128]{1,0:T(8,128)} custom-call(f32[4,72,128]{2,1,0:T(8,128)S(1)} %pad_maximum_fusion.refs_0_, f32[4,72,128]{2,1,0:T(8,128)S(1)} %collective-permute-done.3.refs_1_, f32[4,72,128]{2,1,0:T(8,128)S(1)} %collective-permute-done.4.refs_2_, f32[4,72,128]{2,1,0:T(8,128)S(1)} %collective-permute-done.5.refs_3_, ...), custom_call_target="tpu_custom_call" | custom-call | tf_op jit(solution)/shard_map/schur/pallas_call | solution.py:207
  (1 shorter events, 0.0 us)
Async XLA Ops:
  0.9 7.1 %collective-permute-start.2 = (f32[72,128]{1,0:T(8,128)S(1)}, f32[72,128]{1,0:T(8,128)S(1)}, u32[]{:S(2)}, u32[]{:S(2)}) collective-permute-start(f32[72,128]{1,0:T(8,128)S(1)} %pack.1), channel_id=1, source_target_pairs={{0,6},{1,7},{2,4},{3,5},{4,2},{5,3},{6,0},{7,1},{8,14},{9,15},{10,... | collective-permute-start | bytes 110600 | tf_op jit(solution)/shard_map/ppermute | solution.py:195
  6.1 4.9 %collective-permute-start.1 = (f32[72,128]{1,0:T(8,128)S(1)}, f32[72,128]{1,0:T(8,128)S(1)}, u32[]{:S(2)}, u32[]{:S(2)}) collective-permute-start(f32[72,128]{1,0:T(8,128)S(1)} %pack.1), channel_id=1, source_target_pairs={{0,4},{1,5},{2,6},{3,7},{4,0},{5,1},{6,2},{7,3},{8,12},{9,13},{10,... | collective-permute-start | bytes 110600 | tf_op jit(solution)/shard_map/ppermute | solution.py:195
  6.1 4.9 %collective-permute-start = (f32[72,128]{1,0:T(8,128)S(1)}, f32[72,128]{1,0:T(8,128)S(1)}, u32[]{:S(2)}, u32[]{:S(2)}) collective-permute-start(f32[72,128]{1,0:T(8,128)S(1)} %pack.1), channel_id=1, source_target_pairs={{0,2},{1,3},{2,0},{3,1},{4,6},{5,7},{6,4},{7,5},{8,10},{9,11},{10,... | collective-permute-start | bytes 110600 | tf_op jit(solution)/shard_map/ppermute | solution.py:195
  10.9 6.7 %collective-permute-start.5 = (f32[4,72,128]{2,1,0:T(8,128)S(1)}, f32[4,72,128]{2,1,0:T(8,128)S(1)}, u32[]{:S(2)}, u32[]{:S(2)}) collective-permute-start(f32[4,72,128]{2,1,0:T(8,128)S(1)} %pad_maximum_fusion.refs_0_), channel_id=1, source_target_pairs={{0,17},{1,16},{2,19},{3,18},{4,21},{5,20},{6,23},{7,22},{8,25},{9,... | collective-permute-start | bytes 442376 | tf_op jit(solution)/shard_map/ppermute | solution.py:195
  13.4 5.9 %collective-permute-start.4 = (f32[4,72,128]{2,1,0:T(8,128)S(1)}, f32[4,72,128]{2,1,0:T(8,128)S(1)}, u32[]{:S(2)}, u32[]{:S(2)}) collective-permute-start(f32[4,72,128]{2,1,0:T(8,128)S(1)} %pad_maximum_fusion.refs_0_), channel_id=1, source_target_pairs={{0,16},{1,17},{2,18},{3,19},{4,20},{5,21},{6,22},{7,23},{8,24},{9,... | collective-permute-start | bytes 442376 | tf_op jit(solution)/shard_map/ppermute | solution.py:195
  14.0 5.3 %collective-permute-start.3 = (f32[4,72,128]{2,1,0:T(8,128)S(1)}, f32[4,72,128]{2,1,0:T(8,128)S(1)}, u32[]{:S(2)}, u32[]{:S(2)}) collective-permute-start(f32[4,72,128]{2,1,0:T(8,128)S(1)} %pad_maximum_fusion.refs_0_), channel_id=1, source_target_pairs={{0,1},{1,0},{2,3},{3,2},{4,5},{5,4},{6,7},{7,6},{8,9},{9,8},{10,11... | collective-permute-start | bytes 442376 | tf_op jit(solution)/shard_map/ppermute | solution.py:195
  14.5 5.3 %collective-permute-start.6 = (f32[4,72,128]{2,1,0:T(8,128)S(1)}, f32[4,72,128]{2,1,0:T(8,128)S(1)}, u32[]{:S(2)}, u32[]{:S(2)}) collective-permute-start(f32[4,72,128]{2,1,0:T(8,128)S(1)} %pad_maximum_fusion.refs_0_), channel_id=1, source_target_pairs={{0,8},{1,9},{2,10},{3,11},{4,12},{5,13},{6,14},{7,15},{8,0},{9,1},... | collective-permute-start | bytes 442376 | tf_op jit(solution)/shard_map/ppermute | solution.py:195
  17.6 2.2 %collective-permute-start.9 = (f32[4,72,128]{2,1,0:T(8,128)S(1)}, f32[4,72,128]{2,1,0:T(8,128)S(1)}, u32[]{:S(2)}, u32[]{:S(2)}) collective-permute-start(f32[4,72,128]{2,1,0:T(8,128)S(1)} %collective-permute-done.5.refs_3_), channel_id=1, source_target_pairs={{0,8},{1,9},{2,10},{3,11},{4,12},{5,13},{6,14},{7,15},{8,0},{9,1},... | collective-permute-start | bytes 442376 | tf_op jit(solution)/shard_map/ppermute | solution.py:195
  19.3 1.4 %collective-permute-start.8 = (f32[4,72,128]{2,1,0:T(8,128)S(1)}, f32[4,72,128]{2,1,0:T(8,128)S(1)}, u32[]{:S(2)}, u32[]{:S(2)}) collective-permute-start(f32[4,72,128]{2,1,0:T(8,128)S(1)} %collective-permute-done.4.refs_2_), channel_id=1, source_target_pairs={{0,8},{1,9},{2,10},{3,11},{4,12},{5,13},{6,14},{7,15},{8,0},{9,1},... | collective-permute-start | bytes 442376 | tf_op jit(solution)/shard_map/ppermute | solution.py:195
  19.3 1.6 %collective-permute-start.7 = (f32[4,72,128]{2,1,0:T(8,128)S(1)}, f32[4,72,128]{2,1,0:T(8,128)S(1)}, u32[]{:S(2)}, u32[]{:S(2)}) collective-permute-start(f32[4,72,128]{2,1,0:T(8,128)S(1)} %collective-permute-done.3.refs_1_), channel_id=1, source_target_pairs={{0,8},{1,9},{2,10},{3,11},{4,12},{5,13},{6,14},{7,15},{8,0},{9,1},... | collective-permute-start | bytes 442376 | tf_op jit(solution)/shard_map/ppermute | solution.py:195

commit v6 on v5

--- a/solution.py
+++ b/solution.py
@@ -64,8 +64,8 @@
 
 
 def main_kernel(plan, n_in, *refs):
-    ins, out_ref = refs[:n_in], refs[n_in]
-    misc, mat, xleft, zleft, xj, zj, xpick, zpick, ivec, acc, idx, sem = refs[n_in + 1 :]
+    ins, out_hbm = refs[:n_in], refs[n_in]
+    out_ref, osem, misc, mat, xleft, zleft, xj, zj, xpick, zpick, ivec, acc, idx, sem = refs[n_in + 1 :]
     slot, cols, rows = plan.slot, plan.cols, plan.rows
     slots, tiles, depth = plan.slots, plan.ni // LANES, plan.depth
     me_r, me_c = lax.axis_index("row"), lax.axis_index("col")
@@ -100,13 +100,14 @@
             quads.append(quad)
         return jnp.concatenate(quads, axis=0).astype(I32)
 
-    for t in range(tiles):
-        ivec[t] = codes(me_r * cols + t * plan.fold) * slots
-    copies = []
-    for n in range(tiles * 2 * slots):
-        spot = idx.at[pl.ds(n * LANES, LANES)]
-        copies.append(pltpu.make_async_copy(ivec.at[n // (2 * slots), n % (2 * slots)], spot, sem.at[n]))
-        copies[-1].start()
+    copy = pltpu.make_async_copy(ivec, idx, sem)
+
+    @pl.when(me_r >= 0)
+    def _():
+        for t in range(tiles):
+            ivec[t] = codes(me_r * cols + t * plan.fold) * slots
+        copy.start()
+
     jcode = codes(me_c * rows + chunk * plan.fold)
 
     depth_iota = lax.broadcasted_iota(I32, (depth, LANES), 0)
@@ -163,16 +164,15 @@
                 put(zleft, j, i, v)
                 put(zleft, i, j, v.T)
     select(zleft, zpick, zj)
-    for copy in copies:
-        copy.wait()
+    copy.wait()
 
     def eight(tile_at, n):
         base = n * 8
         for s in range(8):
             total = None
             for k in range(slots):
-                q = pl.multiple_of(idx[base + ((tile_at * 2 * slots + slots + k) * LANES + s)], slots)
-                p = pl.multiple_of(idx[base + (tile_at * 2 * slots + k) * LANES + s], slots)
+                q = pl.multiple_of(idx[tile_at, slots + k, base + s], slots)
+                p = pl.multiple_of(idx[tile_at, k, base + s], slots)
                 term = xj[pl.ds(q, slots), :] * zj[pl.ds(p, slots), :]
                 total = term if total is None else total + term
             acc[s * slots : (s + 1) * slots, :] = total
@@ -182,9 +182,16 @@
             out = v if out is None else out + v
         out_ref[tile_at * LANES + base : tile_at * LANES + base + 8, :] = out
 
+    outs = []
     for t in range(tiles):
         for n in range(LANES // 8):
             eight(t, n)
+        span = pl.ds(t * LANES, LANES)
+        there = out_hbm.at[span, pl.ds(pl.multiple_of(chunk * LANES, LANES), LANES)]
+        outs.append(pltpu.make_async_copy(out_ref.at[span], there, osem.at[t]))
+        outs[-1].start()
+    for copy in outs:
+        copy.wait()
 
 
 def send(plan, v, row_xor, col_xor):
@@ -208,9 +215,11 @@
         functools.partial(main_kernel, plan, len(stacks)),
         grid=(plan.nj // LANES,),
         in_specs=[pl.BlockSpec(memory_space=pltpu.VMEM)] * len(stacks),
-        out_specs=pl.BlockSpec((plan.ni, LANES), lambda c: (0, c)),
+        out_specs=pl.BlockSpec(memory_space=pltpu.HBM),
         out_shape=jax.ShapeDtypeStruct((plan.ni, plan.nj), F32),
         scratch_shapes=[
+            pltpu.VMEM((plan.ni, LANES), F32),
+            pltpu.SemaphoreType.DMA((plan.ni // LANES,)),
             pltpu.VMEM((plan.rows * plan.cols, EXTRA, LANES), F32),
             pltpu.VMEM((n_tile, plan.depth, LANES), F32),
             pltpu.VMEM((2 * plan.depth, plan.depth), BF16),
@@ -221,8 +230,8 @@
             pltpu.VMEM((plan.depth, plan.slots * LANES), BF16),
             pltpu.VMEM((plan.ni // LANES, 2 * plan.slots, LANES), I32),
             pltpu.VMEM((8 * plan.slots, LANES), F32),
-            pltpu.SMEM((plan.ni * 2 * plan.slots,), I32),
-            pltpu.SemaphoreType.DMA((plan.ni // LANES * 2 * plan.slots,)),
+            pltpu.SMEM((plan.ni // LANES, 2 * plan.slots, LANES), I32),
+            pltpu.SemaphoreType.DMA,
         ],
         compiler_params=pltpu.CompilerParams(vmem_limit_bytes=24 << 20),
         name="schur",

time: 28 us -> 27.2 us (0.971)
  Pallas kernels: 7.85 us -> 7.06 us
    pallas_call x1, Pallas kernels: 6.94 us -> 6.16 us  [schur_call(): pl.pallas_call(functools.partial(main_kernel, plan, len(stacks)), grid=(p...]
where the time goes in v6:
time: 27.2 us; the launch traced here: 27.1 us
  waiting for transfers between devices  10.1 us (37%)
  starting transfers between devices  9.85 us (36%)
  Pallas kernels  7.06 us (26%)
    ppermute x10, waiting for transfers between devices, send(): return lax.ppermute(v, ('row', 'col'), pairs)  10.1 us
    ppermute x10, starting transfers between devices, send(): return lax.ppermute(v, ('row', 'col'), pairs)  9.85 us
    pallas_call x1, Pallas kernels, schur_call(): pl.pallas_call(functools.partial(main_kernel, plan, len(stacks)), grid=(p...  6.16 us
    pallas_call x1, Pallas kernels, shards(): pl.pallas_call(functools.partial(pack_kernel, plan), in_specs=[pl.BlockSp...  0.9 us
  transfers between devices with their start and end apart: 10, of which 6 were waited for; matrix products, arithmetic and copies ran while one was open for 0% of the time, Pallas kernels for 0%

profile of v6, /device:TPU:0, one launch (start us, length us, event | category | flops | bytes accessed | tf_op | source)
XLA Modules:
  0.0 27.1 jit_solution(10095101518218235317)
XLA Ops:
  0.0 0.9 %pack.1 = f32[72,128]{1,0:T(8,128)S(1)} custom-call(f32[62,124]{1,0:T(8,128)} %bitcast.12, f32[62,124]{1,0:T(8,128)} %bitcast.13, s32[16,32]{1,0:T(8,128)} %bitcast.14, s32[1,32]{1,0:T(1,128)} %bitcast.15), custom_call_target="tpu_custom_call" | custom-call | tf_op jit(solution)/shard_map/pack/pallas_call | solution.py:244
  0.9 5.1 %collective-permute-start.2 = (f32[72,128]{1,0:T(8,128)S(1)}, f32[72,128]{1,0:T(8,128)S(1)}, u32[]{:S(2)}, u32[]{:S(2)}) collective-permute-start(f32[72,128]{1,0:T(8,128)S(1)} %pack.1), channel_id=1, source_target_pairs={{0,6},{1,7},{2,4},{3,5},{4,2},{5,3},{6,0},{7,1},{8,14},{9,15},{10,... | collective-permute-start | bytes 110600 | tf_op jit(solution)/shard_map/ppermute | solution.py:202
  6.1 0.0 collective-permute-start.1
  6.1 0.6 %collective-permute-start = (f32[72,128]{1,0:T(8,128)S(1)}, f32[72,128]{1,0:T(8,128)S(1)}, u32[]{:S(2)}, u32[]{:S(2)}) collective-permute-start(f32[72,128]{1,0:T(8,128)S(1)} %pack.1), channel_id=1, source_target_pairs={{0,2},{1,3},{2,0},{3,1},{4,6},{5,7},{6,4},{7,5},{8,10},{9,11},{10,... | collective-permute-start | bytes 110600 | tf_op jit(solution)/shard_map/ppermute | solution.py:202
  6.7 1.3 %collective-permute-done.2 = f32[72,128]{1,0:T(8,128)S(1)} collective-permute-done((f32[72,128]{1,0:T(8,128)S(1)}, f32[72,128]{1,0:T(8,128)S(1)}, u32[]{:S(2)}, u32[]{:S(2)}) %collective-permute-start.2) | collective-permute-done | bytes 36896 | tf_op jit(solution)/shard_map/ppermute | solution.py:202
  8.0 2.9 %collective-permute-done.1 = f32[72,128]{1,0:T(8,128)S(1)} collective-permute-done((f32[72,128]{1,0:T(8,128)S(1)}, f32[72,128]{1,0:T(8,128)S(1)}, u32[]{:S(2)}, u32[]{:S(2)}) %collective-permute-start.1) | collective-permute-done | bytes 36896 | tf_op jit(solution)/shard_map/ppermute | solution.py:202
  10.9 0.0 collective-permute-done
  10.9 2.5 %collective-permute-start.5 = (f32[4,72,128]{2,1,0:T(8,128)S(1)}, f32[4,72,128]{2,1,0:T(8,128)S(1)}, u32[]{:S(2)}, u32[]{:S(2)}) collective-permute-start(f32[4,72,128]{2,1,0:T(8,128)S(1)} %pad_maximum_fusion.refs_0_), channel_id=1, source_target_pairs={{0,17},{1,16},{2,19},{3,18},{4,21},{5,20},{6,23},{7,22},{8,25},{9,... | collective-permute-start | bytes 442376 | tf_op jit(solution)/shard_map/ppermute | solution.py:202
  13.4 0.5 %collective-permute-start.4 = (f32[4,72,128]{2,1,0:T(8,128)S(1)}, f32[4,72,128]{2,1,0:T(8,128)S(1)}, u32[]{:S(2)}, u32[]{:S(2)}) collective-permute-start(f32[4,72,128]{2,1,0:T(8,128)S(1)} %pad_maximum_fusion.refs_0_), channel_id=1, source_target_pairs={{0,16},{1,17},{2,18},{3,19},{4,20},{5,21},{6,22},{7,23},{8,24},{9,... | collective-permute-start | bytes 442376 | tf_op jit(solution)/shard_map/ppermute | solution.py:202
  14.0 0.5 %collective-permute-start.3 = (f32[4,72,128]{2,1,0:T(8,128)S(1)}, f32[4,72,128]{2,1,0:T(8,128)S(1)}, u32[]{:S(2)}, u32[]{:S(2)}) collective-permute-start(f32[4,72,128]{2,1,0:T(8,128)S(1)} %pad_maximum_fusion.refs_0_), channel_id=1, source_target_pairs={{0,1},{1,0},{2,3},{3,2},{4,5},{5,4},{6,7},{7,6},{8,9},{9,8},{10,11... | collective-permute-start | bytes 442376 | tf_op jit(solution)/shard_map/ppermute | solution.py:202
  14.5 0.0 collective-permute-start.6
  14.5 3.1 %collective-permute-done.5.refs_3_ = f32[4,72,128]{2,1,0:T(8,128)S(1)} collective-permute-done((f32[4,72,128]{2,1,0:T(8,128)S(1)}, f32[4,72,128]{2,1,0:T(8,128)S(1)}, u32[]{:S(2)}, u32[]{:S(2)}) %collective-permute-start.5) | collective-permute-done | bytes 147488 | tf_op jit(solution)/shard_map/ppermute | solution.py:202
  17.6 0.0 collective-permute-start.9
  17.6 1.7 %collective-permute-done.4.refs_2_ = f32[4,72,128]{2,1,0:T(8,128)S(1)} collective-permute-done((f32[4,72,128]{2,1,0:T(8,128)S(1)}, f32[4,72,128]{2,1,0:T(8,128)S(1)}, u32[]{:S(2)}, u32[]{:S(2)}) %collective-permute-start.4) | collective-permute-done | bytes 147488 | tf_op jit(solution)/shard_map/ppermute | solution.py:202
  19.3 0.0 collective-permute-start.8
  19.3 0.0 collective-permute-done.3.refs_1_
  19.3 0.5 %collective-permute-start.7 = (f32[4,72,128]{2,1,0:T(8,128)S(1)}, f32[4,72,128]{2,1,0:T(8,128)S(1)}, u32[]{:S(2)}, u32[]{:S(2)}) collective-permute-start(f32[4,72,128]{2,1,0:T(8,128)S(1)} %collective-permute-done.3.refs_1_), channel_id=1, source_target_pairs={{0,8},{1,9},{2,10},{3,11},{4,12},{5,13},{6,14},{7,15},{8,0},{9,1},... | collective-permute-start | bytes 442376 | tf_op jit(solution)/shard_map/ppermute | solution.py:202
  19.8 0.0 collective-permute-done.6.refs_4_
  19.8 0.0 collective-permute-done.9.refs_7_
  19.8 0.9 %collective-permute-done.8.refs_6_ = f32[4,72,128]{2,1,0:T(8,128)S(1)} collective-permute-done((f32[4,72,128]{2,1,0:T(8,128)S(1)}, f32[4,72,128]{2,1,0:T(8,128)S(1)}, u32[]{:S(2)}, u32[]{:S(2)}) %collective-permute-start.8) | collective-permute-done | bytes 147488 | tf_op jit(solution)/shard_map/ppermute | solution.py:202
  20.7 0.2 collective-permute-done.7.refs_5_
  20.9 6.2 %schur.1 = f32[256,128]{1,0:T(8,128)} custom-call(f32[4,72,128]{2,1,0:T(8,128)S(1)} %pad_maximum_fusion.refs_0_, f32[4,72,128]{2,1,0:T(8,128)S(1)} %collective-permute-done.3.refs_1_, f32[4,72,128]{2,1,0:T(8,128)S(1)} %collective-permute-done.4.refs_2_, f32[4,72,128]{2,1,0:T(8,128)S(1)} %collective-permute-done.5.refs_3_, ...), custom_call_target="tpu_custom_call" | custom-call | tf_op jit(solution)/shard_map/schur/pallas_call | solution.py:214
  (1 shorter events, 0.0 us)
Async XLA Ops:
  0.9 7.1 %collective-permute-start.2 = (f32[72,128]{1,0:T(8,128)S(1)}, f32[72,128]{1,0:T(8,128)S(1)}, u32[]{:S(2)}, u32[]{:S(2)}) collective-permute-start(f32[72,128]{1,0:T(8,128)S(1)} %pack.1), channel_id=1, source_target_pairs={{0,6},{1,7},{2,4},{3,5},{4,2},{5,3},{6,0},{7,1},{8,14},{9,15},{10,... | collective-permute-start | bytes 110600 | tf_op jit(solution)/shard_map/ppermute | solution.py:202
  6.1 4.9 %collective-permute-start.1 = (f32[72,128]{1,0:T(8,128)S(1)}, f32[72,128]{1,0:T(8,128)S(1)}, u32[]{:S(2)}, u32[]{:S(2)}) collective-permute-start(f32[72,128]{1,0:T(8,128)S(1)} %pack.1), channel_id=1, source_target_pairs={{0,4},{1,5},{2,6},{3,7},{4,0},{5,1},{6,2},{7,3},{8,12},{9,13},{10,... | collective-permute-start | bytes 110600 | tf_op jit(solution)/shard_map/ppermute | solution.py:202
  6.1 4.9 %collective-permute-start = (f32[72,128]{1,0:T(8,128)S(1)}, f32[72,128]{1,0:T(8,128)S(1)}, u32[]{:S(2)}, u32[]{:S(2)}) collective-permute-start(f32[72,128]{1,0:T(8,128)S(1)} %pack.1), channel_id=1, source_target_pairs={{0,2},{1,3},{2,0},{3,1},{4,6},{5,7},{6,4},{7,5},{8,10},{9,11},{10,... | collective-permute-start | bytes 110600 | tf_op jit(solution)/shard_map/ppermute | solution.py:202
  10.9 6.7 %collective-permute-start.5 = (f32[4,72,128]{2,1,0:T(8,128)S(1)}, f32[4,72,128]{2,1,0:T(8,128)S(1)}, u32[]{:S(2)}, u32[]{:S(2)}) collective-permute-start(f32[4,72,128]{2,1,0:T(8,128)S(1)} %pad_maximum_fusion.refs_0_), channel_id=1, source_target_pairs={{0,17},{1,16},{2,19},{3,18},{4,21},{5,20},{6,23},{7,22},{8,25},{9,... | collective-permute-start | bytes 442376 | tf_op jit(solution)/shard_map/ppermute | solution.py:202
  13.4 5.9 %collective-permute-start.4 = (f32[4,72,128]{2,1,0:T(8,128)S(1)}, f32[4,72,128]{2,1,0:T(8,128)S(1)}, u32[]{:S(2)}, u32[]{:S(2)}) collective-permute-start(f32[4,72,128]{2,1,0:T(8,128)S(1)} %pad_maximum_fusion.refs_0_), channel_id=1, source_target_pairs={{0,16},{1,17},{2,18},{3,19},{4,20},{5,21},{6,22},{7,23},{8,24},{9,... | collective-permute-start | bytes 442376 | tf_op jit(solution)/shard_map/ppermute | solution.py:202
  14.0 5.3 %collective-permute-start.3 = (f32[4,72,128]{2,1,0:T(8,128)S(1)}, f32[4,72,128]{2,1,0:T(8,128)S(1)}, u32[]{:S(2)}, u32[]{:S(2)}) collective-permute-start(f32[4,72,128]{2,1,0:T(8,128)S(1)} %pad_maximum_fusion.refs_0_), channel_id=1, source_target_pairs={{0,1},{1,0},{2,3},{3,2},{4,5},{5,4},{6,7},{7,6},{8,9},{9,8},{10,11... | collective-permute-start | bytes 442376 | tf_op jit(solution)/shard_map/ppermute | solution.py:202
  14.5 5.3 %collective-permute-start.6 = (f32[4,72,128]{2,1,0:T(8,128)S(1)}, f32[4,72,128]{2,1,0:T(8,128)S(1)}, u32[]{:S(2)}, u32[]{:S(2)}) collective-permute-start(f32[4,72,128]{2,1,0:T(8,128)S(1)} %pad_maximum_fusion.refs_0_), channel_id=1, source_target_pairs={{0,8},{1,9},{2,10},{3,11},{4,12},{5,13},{6,14},{7,15},{8,0},{9,1},... | collective-permute-start | bytes 442376 | tf_op jit(solution)/shard_map/ppermute | solution.py:202
  17.6 2.2 %collective-permute-start.9 = (f32[4,72,128]{2,1,0:T(8,128)S(1)}, f32[4,72,128]{2,1,0:T(8,128)S(1)}, u32[]{:S(2)}, u32[]{:S(2)}) collective-permute-start(f32[4,72,128]{2,1,0:T(8,128)S(1)} %collective-permute-done.5.refs_3_), channel_id=1, source_target_pairs={{0,8},{1,9},{2,10},{3,11},{4,12},{5,13},{6,14},{7,15},{8,0},{9,1},... | collective-permute-start | bytes 442376 | tf_op jit(solution)/shard_map/ppermute | solution.py:202
  19.3 1.4 %collective-permute-start.8 = (f32[4,72,128]{2,1,0:T(8,128)S(1)}, f32[4,72,128]{2,1,0:T(8,128)S(1)}, u32[]{:S(2)}, u32[]{:S(2)}) collective-permute-start(f32[4,72,128]{2,1,0:T(8,128)S(1)} %collective-permute-done.4.refs_2_), channel_id=1, source_target_pairs={{0,8},{1,9},{2,10},{3,11},{4,12},{5,13},{6,14},{7,15},{8,0},{9,1},... | collective-permute-start | bytes 442376 | tf_op jit(solution)/shard_map/ppermute | solution.py:202
  19.3 1.6 %collective-permute-start.7 = (f32[4,72,128]{2,1,0:T(8,128)S(1)}, f32[4,72,128]{2,1,0:T(8,128)S(1)}, u32[]{:S(2)}, u32[]{:S(2)}) collective-permute-start(f32[4,72,128]{2,1,0:T(8,128)S(1)} %collective-permute-done.3.refs_1_), channel_id=1, source_target_pairs={{0,8},{1,9},{2,10},{3,11},{4,12},{5,13},{6,14},{7,15},{8,0},{9,1},... | collective-permute-start | bytes 442376 | tf_op jit(solution)/shard_map/ppermute | solution.py:202

commit v7 on v6

--- a/solution.py
+++ b/solution.py
@@ -65,7 +65,7 @@
 
 def main_kernel(plan, n_in, *refs):
     ins, out_hbm = refs[:n_in], refs[n_in]
-    out_ref, osem, misc, mat, xleft, zleft, xj, zj, xpick, zpick, ivec, acc, idx, sem = refs[n_in + 1 :]
+    out_ref, osem, misc, mat, left, zrow, zgot, xj, zj, pick, ivec, jvec, acc, idx, jdx, sem = refs[n_in + 1 :]
     slot, cols, rows = plan.slot, plan.cols, plan.rows
     slots, tiles, depth = plan.slots, plan.ni // LANES, plan.depth
     me_r, me_c = lax.axis_index("row"), lax.axis_index("col")
@@ -100,53 +100,35 @@
             quads.append(quad)
         return jnp.concatenate(quads, axis=0).astype(I32)
 
-    copy = pltpu.make_async_copy(ivec, idx, sem)
+    n_tile = depth // LANES
+    jcode = codes(me_c * rows + chunk * plan.fold)
+    icopy = pltpu.make_async_copy(ivec, idx, sem.at[0])
+    jcopy = pltpu.make_async_copy(jvec, jdx, sem.at[1])
 
     @pl.when(me_r >= 0)
     def _():
+        jvec[...] = codes(me_c * rows + chunk * plan.fold)[slots:] * n_tile
+        jcopy.start()
         for t in range(tiles):
             ivec[t] = codes(me_r * cols + t * plan.fold) * slots
-        copy.start()
-
-    jcode = codes(me_c * rows + chunk * plan.fold)
+        icopy.start()
 
     depth_iota = lax.broadcasted_iota(I32, (depth, LANES), 0)
-    n_tile = depth // LANES
     ra = lax.broadcasted_iota(I32, (LANES, LANES), 0)
     rb = lax.broadcasted_iota(I32, (LANES, LANES), 1)
 
     def tile(i, j):
         return mat[j, i * LANES : (i + 1) * LANES, :]
 
-    def put(left, i, j, v):
+    def put_x(i, j, v):
         hi = v.astype(BF16)
         lo = (v - hi.astype(F32)).astype(BF16)
         left[i * LANES : (i + 1) * LANES, j * LANES : (j + 1) * LANES] = hi
         left[depth + i * LANES : depth + (i + 1) * LANES, j * LANES : (j + 1) * LANES] = lo
 
-    def mark(base, pick):
-        for l in range(slots):
-            at = jcode[base + l : base + l + 1, :]
-            pick[:, l * LANES : (l + 1) * LANES] = jnp.where(depth_iota == at, 1.0, 0.0).astype(BF16)
-
-    def select(left, pick, out):
-        for m in range(slots // 2):
-            res = jnp.dot(left[...], pick[:, m * 256 : (m + 1) * 256], preferred_element_type=F32)
-            res = res[:depth] + res[depth:]
-            for l in range(2):
-                out[pl.ds(2 * m + l, depth, stride=slots), :] = res[:, l * LANES : (l + 1) * LANES]
-
-    mark(0, xpick)
-    for i in range(n_tile):
-        for j in range(i, n_tile):
-            v = tile(i, j)
-            if i == j:
-                put(xleft, i, i, jnp.where(ra <= rb, v, v.T))
-            else:
-                put(xleft, i, j, v)
-                put(xleft, j, i, v.T)
-    select(xleft, xpick, xj)
-    mark(slots, zpick)
+    def put_z(i, j, v):
+        zrow[pl.ds(8 + i * LANES * n_tile + j, LANES, stride=n_tile), :] = v
+
     per_tile = LANES // slot
     for i in range(n_tile):
         for j in range(i, n_tile):
@@ -159,12 +141,46 @@
                     if per > 1 and r % per:
                         row = pltpu.roll(row, (r % per) * plan.wide, 1)
                     diag = row if diag is None else diag + row
-                put(zleft, i, i, jnp.where(ra > rb, v, jnp.where(ra == rb, diag, v.T)))
+                put_z(i, i, jnp.where(ra > rb, v, jnp.where(ra == rb, diag, v.T)))
             else:
-                put(zleft, j, i, v)
-                put(zleft, i, j, v.T)
-    select(zleft, zpick, zj)
-    copy.wait()
+                put_z(j, i, v)
+                put_z(i, j, v.T)
+    for l in range(slots):
+        at = jcode[l : l + 1, :]
+        pick[:, l * LANES : (l + 1) * LANES] = jnp.where(depth_iota == at, 1.0, 0.0).astype(BF16)
+    for i in range(n_tile):
+        for j in range(i, n_tile):
+            v = tile(i, j)
+            if i == j:
+                put_x(i, i, jnp.where(ra <= rb, v, v.T))
+            else:
+                put_x(i, j, v)
+                put_x(j, i, v.T)
+
+    group = lax.broadcasted_iota(I32, (8, LANES), 0) // n_tile
+    jcopy.wait()
+
+    def gather_rows(l):
+        for j in range(0, LANES, 8 // n_tile):
+            both = None
+            for e in range(8 // n_tile):
+                at = pl.multiple_of(jdx[l, j + e], n_tile)
+                v = zrow[pl.ds(at + (8 - e * n_tile), 8), :]
+                both = v if both is None else jnp.where(group == e, v, both)
+            base = (l * LANES + j) * n_tile
+            zgot[base : base + 8, :] = both
+        for s in range(n_tile):
+            v = zgot[pl.ds(l * LANES * n_tile + s, LANES, stride=n_tile), :]
+            zj[pl.ds(s * LANES * slots + l, LANES, stride=slots), :] = v.T
+
+    for m in range(slots // 2):
+        res = jnp.dot(left[...], pick[:, m * 256 : (m + 1) * 256], preferred_element_type=F32)
+        res = res[:depth] + res[depth:]
+        for l in range(2):
+            xj[pl.ds(2 * m + l, depth, stride=slots), :] = res[:, l * LANES : (l + 1) * LANES]
+    for l in range(slots):
+        gather_rows(l)
+    icopy.wait()
 
     def eight(tile_at, n):
         base = n * 8
@@ -223,15 +239,17 @@
             pltpu.VMEM((plan.rows * plan.cols, EXTRA, LANES), F32),
             pltpu.VMEM((n_tile, plan.depth, LANES), F32),
             pltpu.VMEM((2 * plan.depth, plan.depth), BF16),
-            pltpu.VMEM((2 * plan.depth, plan.depth), BF16),
+            pltpu.VMEM((plan.depth * n_tile + 16, LANES), F32),
+            pltpu.VMEM((plan.slots * LANES * n_tile, LANES), F32),
             pltpu.VMEM((plan.depth * plan.slots, LANES), F32),
             pltpu.VMEM((plan.depth * plan.slots, LANES), F32),
             pltpu.VMEM((plan.depth, plan.slots * LANES), BF16),
-            pltpu.VMEM((plan.depth, plan.slots * LANES), BF16),
             pltpu.VMEM((plan.ni // LANES, 2 * plan.slots, LANES), I32),
+            pltpu.VMEM((plan.slots, LANES), I32),
             pltpu.VMEM((8 * plan.slots, LANES), F32),
             pltpu.SMEM((plan.ni // LANES, 2 * plan.slots, LANES), I32),
-            pltpu.SemaphoreType.DMA,
+            pltpu.SMEM((plan.slots, LANES), I32),
+            pltpu.SemaphoreType.DMA((2,)),
         ],
         compiler_params=pltpu.CompilerParams(vmem_limit_bytes=24 << 20),
         name="schur",

time: 27.2 us -> 26.9 us (0.989)
  Pallas kernels: 7.06 us -> 6.69 us
    pallas_call x1, Pallas kernels: 6.16 us -> 5.79 us  [schur_call(): pl.pallas_call(functools.partial(main_kernel, plan, len(stacks)), grid=(p...]
where the time goes in v7:
time: 26.9 us; the launch traced here: 26.7 us
  waiting for transfers between devices  10.1 us (38%)
  starting transfers between devices  9.85 us (37%)
  Pallas kernels  6.69 us (25%)
    ppermute x10, waiting for transfers between devices, send(): return lax.ppermute(v, ('row', 'col'), pairs)  10.1 us
    ppermute x10, starting transfers between devices, send(): return lax.ppermute(v, ('row', 'col'), pairs)  9.85 us
    pallas_call x1, Pallas kernels, schur_call(): pl.pallas_call(functools.partial(main_kernel, plan, len(stacks)), grid=(p...  5.79 us
    pallas_call x1, Pallas kernels, shards(): pl.pallas_call(functools.partial(pack_kernel, plan), in_specs=[pl.BlockSp...  0.9 us
  transfers between devices with their start and end apart: 10, of which 6 were waited for; matrix products, arithmetic and copies ran while one was open for 0% of the time, Pallas kernels for 0%

profile of v7, /device:TPU:0, one launch (start us, length us, event | category | flops | bytes accessed | tf_op | source)
XLA Modules:
  0.0 26.7 jit_solution(4270242220711974847)
XLA Ops:
  0.0 0.9 %pack.1 = f32[72,128]{1,0:T(8,128)S(1)} custom-call(f32[62,124]{1,0:T(8,128)} %bitcast.12, f32[62,124]{1,0:T(8,128)} %bitcast.13, s32[16,32]{1,0:T(8,128)} %bitcast.14, s32[1,32]{1,0:T(1,128)} %bitcast.15), custom_call_target="tpu_custom_call" | custom-call | tf_op jit(solution)/shard_map/pack/pallas_call | solution.py:262
  0.9 5.1 %collective-permute-start.2 = (f32[72,128]{1,0:T(8,128)S(1)}, f32[72,128]{1,0:T(8,128)S(1)}, u32[]{:S(2)}, u32[]{:S(2)}) collective-permute-start(f32[72,128]{1,0:T(8,128)S(1)} %pack.1), channel_id=1, source_target_pairs={{0,6},{1,7},{2,4},{3,5},{4,2},{5,3},{6,0},{7,1},{8,14},{9,15},{10,... | collective-permute-start | bytes 110600 | tf_op jit(solution)/shard_map/ppermute | solution.py:218
  6.1 0.0 collective-permute-start.1
  6.1 0.6 %collective-permute-start = (f32[72,128]{1,0:T(8,128)S(1)}, f32[72,128]{1,0:T(8,128)S(1)}, u32[]{:S(2)}, u32[]{:S(2)}) collective-permute-start(f32[72,128]{1,0:T(8,128)S(1)} %pack.1), channel_id=1, source_target_pairs={{0,2},{1,3},{2,0},{3,1},{4,6},{5,7},{6,4},{7,5},{8,10},{9,11},{10,... | collective-permute-start | bytes 110600 | tf_op jit(solution)/shard_map/ppermute | solution.py:218
  6.7 1.3 %collective-permute-done.2 = f32[72,128]{1,0:T(8,128)S(1)} collective-permute-done((f32[72,128]{1,0:T(8,128)S(1)}, f32[72,128]{1,0:T(8,128)S(1)}, u32[]{:S(2)}, u32[]{:S(2)}) %collective-permute-start.2) | collective-permute-done | bytes 36896 | tf_op jit(solution)/shard_map/ppermute | solution.py:218
  8.0 2.9 %collective-permute-done.1 = f32[72,128]{1,0:T(8,128)S(1)} collective-permute-done((f32[72,128]{1,0:T(8,128)S(1)}, f32[72,128]{1,0:T(8,128)S(1)}, u32[]{:S(2)}, u32[]{:S(2)}) %collective-permute-start.1) | collective-permute-done | bytes 36896 | tf_op jit(solution)/shard_map/ppermute | solution.py:218
  10.9 0.0 collective-permute-done
  10.9 2.5 %collective-permute-start.5 = (f32[4,72,128]{2,1,0:T(8,128)S(1)}, f32[4,72,128]{2,1,0:T(8,128)S(1)}, u32[]{:S(2)}, u32[]{:S(2)}) collective-permute-start(f32[4,72,128]{2,1,0:T(8,128)S(1)} %pad_maximum_fusion.refs_0_), channel_id=1, source_target_pairs={{0,17},{1,16},{2,19},{3,18},{4,21},{5,20},{6,23},{7,22},{8,25},{9,... | collective-permute-start | bytes 442376 | tf_op jit(solution)/shard_map/ppermute | solution.py:218
  13.4 0.5 %collective-permute-start.4 = (f32[4,72,128]{2,1,0:T(8,128)S(1)}, f32[4,72,128]{2,1,0:T(8,128)S(1)}, u32[]{:S(2)}, u32[]{:S(2)}) collective-permute-start(f32[4,72,128]{2,1,0:T(8,128)S(1)} %pad_maximum_fusion.refs_0_), channel_id=1, source_target_pairs={{0,16},{1,17},{2,18},{3,19},{4,20},{5,21},{6,22},{7,23},{8,24},{9,... | collective-permute-start | bytes 442376 | tf_op jit(solution)/shard_map/ppermute | solution.py:218
  14.0 0.5 %collective-permute-start.3 = (f32[4,72,128]{2,1,0:T(8,128)S(1)}, f32[4,72,128]{2,1,0:T(8,128)S(1)}, u32[]{:S(2)}, u32[]{:S(2)}) collective-permute-start(f32[4,72,128]{2,1,0:T(8,128)S(1)} %pad_maximum_fusion.refs_0_), channel_id=1, source_target_pairs={{0,1},{1,0},{2,3},{3,2},{4,5},{5,4},{6,7},{7,6},{8,9},{9,8},{10,11... | collective-permute-start | bytes 442376 | tf_op jit(solution)/shard_map/ppermute | solution.py:218
  14.5 0.0 collective-permute-start.6
  14.5 3.1 %collective-permute-done.5.refs_3_ = f32[4,72,128]{2,1,0:T(8,128)S(1)} collective-permute-done((f32[4,72,128]{2,1,0:T(8,128)S(1)}, f32[4,72,128]{2,1,0:T(8,128)S(1)}, u32[]{:S(2)}, u32[]{:S(2)}) %collective-permute-start.5) | collective-permute-done | bytes 147488 | tf_op jit(solution)/shard_map/ppermute | solution.py:218
  17.6 0.0 collective-permute-start.9
  17.6 1.7 %collective-permute-done.4.refs_2_ = f32[4,72,128]{2,1,0:T(8,128)S(1)} collective-permute-done((f32[4,72,128]{2,1,0:T(8,128)S(1)}, f32[4,72,128]{2,1,0:T(8,128)S(1)}, u32[]{:S(2)}, u32[]{:S(2)}) %collective-permute-start.4) | collective-permute-done | bytes 147488 | tf_op jit(solution)/shard_map/ppermute | solution.py:218
  19.3 0.0 collective-permute-start.8
  19.3 0.0 collective-permute-done.3.refs_1_
  19.3 0.5 %collective-permute-start.7 = (f32[4,72,128]{2,1,0:T(8,128)S(1)}, f32[4,72,128]{2,1,0:T(8,128)S(1)}, u32[]{:S(2)}, u32[]{:S(2)}) collective-permute-start(f32[4,72,128]{2,1,0:T(8,128)S(1)} %collective-permute-done.3.refs_1_), channel_id=1, source_target_pairs={{0,8},{1,9},{2,10},{3,11},{4,12},{5,13},{6,14},{7,15},{8,0},{9,1},... | collective-permute-start | bytes 442376 | tf_op jit(solution)/shard_map/ppermute | solution.py:218
  19.8 0.0 collective-permute-done.6.refs_4_
  19.8 0.0 collective-permute-done.9.refs_7_
  19.8 0.9 %collective-permute-done.8.refs_6_ = f32[4,72,128]{2,1,0:T(8,128)S(1)} collective-permute-done((f32[4,72,128]{2,1,0:T(8,128)S(1)}, f32[4,72,128]{2,1,0:T(8,128)S(1)}, u32[]{:S(2)}, u32[]{:S(2)}) %collective-permute-start.8) | collective-permute-done | bytes 147488 | tf_op jit(solution)/shard_map/ppermute | solution.py:218
  20.7 0.2 collective-permute-done.7.refs_5_
  20.9 5.8 %schur.1 = f32[256,128]{1,0:T(8,128)} custom-call(f32[4,72,128]{2,1,0:T(8,128)S(1)} %pad_maximum_fusion.refs_0_, f32[4,72,128]{2,1,0:T(8,128)S(1)} %collective-permute-done.3.refs_1_, f32[4,72,128]{2,1,0:T(8,128)S(1)} %collective-permute-done.4.refs_2_, f32[4,72,128]{2,1,0:T(8,128)S(1)} %collective-permute-done.5.refs_3_, ...), custom_call_target="tpu_custom_call" | custom-call | tf_op jit(solution)/shard_map/schur/pallas_call | solution.py:230
  (1 shorter events, 0.0 us)
Async XLA Ops:
  0.9 7.1 %collective-permute-start.2 = (f32[72,128]{1,0:T(8,128)S(1)}, f32[72,128]{1,0:T(8,128)S(1)}, u32[]{:S(2)}, u32[]{:S(2)}) collective-permute-start(f32[72,128]{1,0:T(8,128)S(1)} %pack.1), channel_id=1, source_target_pairs={{0,6},{1,7},{2,4},{3,5},{4,2},{5,3},{6,0},{7,1},{8,14},{9,15},{10,... | collective-permute-start | bytes 110600 | tf_op jit(solution)/shard_map/ppermute | solution.py:218
  6.1 4.9 %collective-permute-start.1 = (f32[72,128]{1,0:T(8,128)S(1)}, f32[72,128]{1,0:T(8,128)S(1)}, u32[]{:S(2)}, u32[]{:S(2)}) collective-permute-start(f32[72,128]{1,0:T(8,128)S(1)} %pack.1), channel_id=1, source_target_pairs={{0,4},{1,5},{2,6},{3,7},{4,0},{5,1},{6,2},{7,3},{8,12},{9,13},{10,... | collective-permute-start | bytes 110600 | tf_op jit(solution)/shard_map/ppermute | solution.py:218
  6.1 4.9 %collective-permute-start = (f32[72,128]{1,0:T(8,128)S(1)}, f32[72,128]{1,0:T(8,128)S(1)}, u32[]{:S(2)}, u32[]{:S(2)}) collective-permute-start(f32[72,128]{1,0:T(8,128)S(1)} %pack.1), channel_id=1, source_target_pairs={{0,2},{1,3},{2,0},{3,1},{4,6},{5,7},{6,4},{7,5},{8,10},{9,11},{10,... | collective-permute-start | bytes 110600 | tf_op jit(solution)/shard_map/ppermute | solution.py:218
  10.9 6.7 %collective-permute-start.5 = (f32[4,72,128]{2,1,0:T(8,128)S(1)}, f32[4,72,128]{2,1,0:T(8,128)S(1)}, u32[]{:S(2)}, u32[]{:S(2)}) collective-permute-start(f32[4,72,128]{2,1,0:T(8,128)S(1)} %pad_maximum_fusion.refs_0_), channel_id=1, source_target_pairs={{0,17},{1,16},{2,19},{3,18},{4,21},{5,20},{6,23},{7,22},{8,25},{9,... | collective-permute-start | bytes 442376 | tf_op jit(solution)/shard_map/ppermute | solution.py:218
  13.4 5.9 %collective-permute-start.4 = (f32[4,72,128]{2,1,0:T(8,128)S(1)}, f32[4,72,128]{2,1,0:T(8,128)S(1)}, u32[]{:S(2)}, u32[]{:S(2)}) collective-permute-start(f32[4,72,128]{2,1,0:T(8,128)S(1)} %pad_maximum_fusion.refs_0_), channel_id=1, source_target_pairs={{0,16},{1,17},{2,18},{3,19},{4,20},{5,21},{6,22},{7,23},{8,24},{9,... | collective-permute-start | bytes 442376 | tf_op jit(solution)/shard_map/ppermute | solution.py:218
  14.0 5.3 %collective-permute-start.3 = (f32[4,72,128]{2,1,0:T(8,128)S(1)}, f32[4,72,128]{2,1,0:T(8,128)S(1)}, u32[]{:S(2)}, u32[]{:S(2)}) collective-permute-start(f32[4,72,128]{2,1,0:T(8,128)S(1)} %pad_maximum_fusion.refs_0_), channel_id=1, source_target_pairs={{0,1},{1,0},{2,3},{3,2},{4,5},{5,4},{6,7},{7,6},{8,9},{9,8},{10,11... | collective-permute-start | bytes 442376 | tf_op jit(solution)/shard_map/ppermute | solution.py:218
  14.5 5.3 %collective-permute-start.6 = (f32[4,72,128]{2,1,0:T(8,128)S(1)}, f32[4,72,128]{2,1,0:T(8,128)S(1)}, u32[]{:S(2)}, u32[]{:S(2)}) collective-permute-start(f32[4,72,128]{2,1,0:T(8,128)S(1)} %pad_maximum_fusion.refs_0_), channel_id=1, source_target_pairs={{0,8},{1,9},{2,10},{3,11},{4,12},{5,13},{6,14},{7,15},{8,0},{9,1},... | collective-permute-start | bytes 442376 | tf_op jit(solution)/shard_map/ppermute | solution.py:218
  17.6 2.2 %collective-permute-start.9 = (f32[4,72,128]{2,1,0:T(8,128)S(1)}, f32[4,72,128]{2,1,0:T(8,128)S(1)}, u32[]{:S(2)}, u32[]{:S(2)}) collective-permute-start(f32[4,72,128]{2,1,0:T(8,128)S(1)} %collective-permute-done.5.refs_3_), channel_id=1, source_target_pairs={{0,8},{1,9},{2,10},{3,11},{4,12},{5,13},{6,14},{7,15},{8,0},{9,1},... | collective-permute-start | bytes 442376 | tf_op jit(solution)/shard_map/ppermute | solution.py:218
  19.3 1.4 %collective-permute-start.8 = (f32[4,72,128]{2,1,0:T(8,128)S(1)}, f32[4,72,128]{2,1,0:T(8,128)S(1)}, u32[]{:S(2)}, u32[]{:S(2)}) collective-permute-start(f32[4,72,128]{2,1,0:T(8,128)S(1)} %collective-permute-done.4.refs_2_), channel_id=1, source_target_pairs={{0,8},{1,9},{2,10},{3,11},{4,12},{5,13},{6,14},{7,15},{8,0},{9,1},... | collective-permute-start | bytes 442376 | tf_op jit(solution)/shard_map/ppermute | solution.py:218
  19.3 1.6 %collective-permute-start.7 = (f32[4,72,128]{2,1,0:T(8,128)S(1)}, f32[4,72,128]{2,1,0:T(8,128)S(1)}, u32[]{:S(2)}, u32[]{:S(2)}) collective-permute-start(f32[4,72,128]{2,1,0:T(8,128)S(1)} %collective-permute-done.3.refs_1_), channel_id=1, source_target_pairs={{0,8},{1,9},{2,10},{3,11},{4,12},{5,13},{6,14},{7,15},{8,0},{9,1},... | collective-permute-start | bytes 442376 | tf_op jit(solution)/shard_map/ppermute | solution.py:218

commit v8 on v7

--- a/solution.py
+++ b/solution.py
@@ -26,7 +26,8 @@
         self.folded = 2 * self.slots // self.fold
         self.ni = self.local * cols
         self.nj = self.local * rows
-        self.payload = self.slot + EXTRA
+        self.used = self.nb + self.folded
+        self.payload = -(-max(self.slot, self.used) // 8) * 8
         row_bits, col_bits = rows.bit_length() - 1, cols.bit_length() - 1
         y_bits = col_bits // 2
         self.far = [(0, k << y_bits) for k in range(1 << (col_bits - y_bits))]
@@ -47,11 +48,10 @@
     b = lax.broadcasted_iota(I32, (nb, plan.mb), 1) + me_r * plan.mb
     z = z_ref[...]
     mixed = jnp.where(a <= b, x_ref[...], z)
-    diag = jnp.sum(jnp.where(a == b, z, 0.0), axis=0, keepdims=True)
-    at = slot + plan.folded
+    diag = jnp.sum(jnp.where(a == b, z, 0.0), axis=1, keepdims=True)
     for h in range(plan.halves):
         out_ref[0:nb, h * slot : h * slot + nb] = mixed[:, h * nb : (h + 1) * nb]
-        out_ref[at : at + 1, h * slot : h * slot + nb] = diag[:, h * nb : (h + 1) * nb]
+    out_ref[0:nb, nb : nb + 1] = diag
     spots = pos_ref[...].astype(F32)
     code = spots
     for t in range(1, plan.cols):
@@ -60,7 +60,7 @@
     code = jnp.where(k < cnt_ref[...], code, float(plan.dead))
     for g in range(plan.fold):
         piece = code[g * plan.folded : (g + 1) * plan.folded, :]
-        out_ref[slot : slot + plan.folded, g * plan.local : (g + 1) * plan.local] = piece
+        out_ref[nb : nb + plan.folded, g * plan.local : (g + 1) * plan.local] = piece
 
 
 def main_kernel(plan, n_in, *refs):
@@ -73,12 +73,14 @@
     per = LANES // plan.wide
     if per > 1:
         mat[...] = jnp.zeros_like(mat)
+    live_row = lax.broadcasted_iota(I32, (slot, LANES), 0) < plan.nb
     near = [(core ^ i, k) for core in (0, 1) for i, k in plan.near]
     for ref, (ri, ci) in zip(ins, near):
         for n, (rf, cf) in enumerate(plan.far):
             r, c = me_r ^ (ri ^ rf), me_c ^ (ci ^ cf)
-            misc[r * cols + c] = ref[n, slot:, :]
-            v = ref[n, 0:slot, :]
+            base = n * plan.used
+            misc[r * cols + c, 0 : plan.folded, :] = ref[base + plan.nb : base + plan.used, :]
+            v = jnp.where(live_row, ref[base : base + slot, :], 0.0)
             span = pl.ds(pl.multiple_of(c * slot, slot), slot)
             if per == 1:
                 mat[r, span, :] = v
@@ -129,18 +131,15 @@
     def put_z(i, j, v):
         zrow[pl.ds(8 + i * LANES * n_tile + j, LANES, stride=n_tile), :] = v
 
-    per_tile = LANES // slot
     for i in range(n_tile):
         for j in range(i, n_tile):
             v = tile(j, i)
             if i == j:
                 diag = None
-                for c in range(i * per_tile, (i + 1) * per_tile):
-                    r = c // plan.halves
-                    row = misc[r * cols + c][plan.folded : plan.folded + 1]
-                    if per > 1 and r % per:
-                        row = pltpu.roll(row, (r % per) * plan.wide, 1)
-                    diag = row if diag is None else diag + row
+                for g in range(per):
+                    spot = g * plan.wide + plan.nb
+                    col = jnp.broadcast_to(v[:, spot : spot + 1], v.shape)
+                    diag = col if diag is None else jnp.where(ra // plan.wide == g, col, diag)
                 put_z(i, i, jnp.where(ra > rb, v, jnp.where(ra == rb, diag, v.T)))
             else:
                 put_z(j, i, v)
@@ -218,9 +217,19 @@
     return lax.ppermute(v, ("row", "col"), pairs)
 
 
+def stack_kernel(plan, *refs):
+    for n, ref in enumerate(refs[:-1]):
+        refs[-1][n * plan.used : (n + 1) * plan.used, :] = ref[0 : plan.used, :]
+
+
 def gather(plan, v):
     line = [v if k == (0, 0) else send(plan, v, *k) for k in plan.far]
-    stack = jnp.stack(line)
+    stack = pl.pallas_call(
+        functools.partial(stack_kernel, plan),
+        out_shape=jax.ShapeDtypeStruct((len(line) * plan.used, LANES), F32),
+        compiler_params=pltpu.CompilerParams(vmem_limit_bytes=4 << 20),
+        name="stack",
+    )(*line)
     stacks = [stack if k == (0, 0) else send(plan, stack, *k) for k in plan.near]
     return stacks + [send(plan, s, 1, 0) for s in stacks]
 

time: 26.9 us -> 26.4 us (0.981)
  waiting for transfers between devices: 10.1 us -> 9.79 us
    ppermute x10, waiting for transfers between devices: 10.1 us -> 9.79 us  [send(): return lax.ppermute(v, ('row', 'col'), pairs)]
  transfers between devices with their start and end apart: 10 -> 10, of which waited for: 6 -> 7; matrix products, arithmetic and copies ran while one was open for 0% -> 0% of each run, Pallas kernels for 0% -> 0%
where the time goes in v8:
time: 26.4 us; the launch traced here: 26.2 us
  waiting for transfers between devices  9.79 us (37%)
  starting transfers between devices  9.61 us (36%)
  Pallas kernels  6.8 us (26%)
    ppermute x10, waiting for transfers between devices, send(): return lax.ppermute(v, ('row', 'col'), pairs)  9.79 us
    ppermute x10, starting transfers between devices, send(): return lax.ppermute(v, ('row', 'col'), pairs)  9.61 us
    pallas_call x1, Pallas kernels, schur_call(): pl.pallas_call(functools.partial(main_kernel, plan, len(stacks)), grid=(p...  5.88 us
    pallas_call x1, Pallas kernels, shards(): pl.pallas_call(functools.partial(pack_kernel, plan), in_specs=[pl.BlockSp...  0.91 us
  transfers between devices with their start and end apart: 10, of which 7 were waited for; matrix products, arithmetic and copies ran while one was open for 0% of the time, Pallas kernels for 0%

profile of v8, /device:TPU:0, one launch (start us, length us, event | category | flops | bytes accessed | tf_op | source)
XLA Modules:
  0.0 26.2 jit_solution(4297193522038480225)
XLA Ops:
  0.0 0.9 %pack.1.refs_0_ = f32[72,128]{1,0:T(8,128)S(1)} custom-call(f32[62,124]{1,0:T(8,128)} %bitcast.4, f32[62,124]{1,0:T(8,128)} %bitcast.5, s32[16,32]{1,0:T(8,128)} %bitcast.6, s32[1,32]{1,0:T(1,128)} %bitcast.7), custom_call_target="tpu_custom_call" | custom-call | tf_op jit(solution)/shard_map/pack/pallas_call | solution.py:271
  0.9 5.1 %collective-permute-start.2 = (f32[72,128]{1,0:T(8,128)S(1)}, f32[72,128]{1,0:T(8,128)S(1)}, u32[]{:S(2)}, u32[]{:S(2)}) collective-permute-start(f32[72,128]{1,0:T(8,128)S(1)} %pack.1.refs_0_), channel_id=1, source_target_pairs={{0,6},{1,7},{2,4},{3,5},{4,2},{5,3},{6,0},{7,1},{8,14},{9,15},{10,... | collective-permute-start | bytes 110600 | tf_op jit(solution)/shard_map/ppermute | solution.py:217
  6.1 0.0 collective-permute-start.1
  6.1 0.6 %collective-permute-start = (f32[72,128]{1,0:T(8,128)S(1)}, f32[72,128]{1,0:T(8,128)S(1)}, u32[]{:S(2)}, u32[]{:S(2)}) collective-permute-start(f32[72,128]{1,0:T(8,128)S(1)} %pack.1.refs_0_), channel_id=1, source_target_pairs={{0,2},{1,3},{2,0},{3,1},{4,6},{5,7},{6,4},{7,5},{8,10},{9,11},{10,... | collective-permute-start | bytes 110600 | tf_op jit(solution)/shard_map/ppermute | solution.py:217
  6.7 1.3 %collective-permute-done.2.refs_3_ = f32[72,128]{1,0:T(8,128)S(1)} collective-permute-done((f32[72,128]{1,0:T(8,128)S(1)}, f32[72,128]{1,0:T(8,128)S(1)}, u32[]{:S(2)}, u32[]{:S(2)}) %collective-permute-start.2) | collective-permute-done | bytes 36896 | tf_op jit(solution)/shard_map/ppermute | solution.py:217
  8.0 2.9 %collective-permute-done.1.refs_2_ = f32[72,128]{1,0:T(8,128)S(1)} collective-permute-done((f32[72,128]{1,0:T(8,128)S(1)}, f32[72,128]{1,0:T(8,128)S(1)}, u32[]{:S(2)}, u32[]{:S(2)}) %collective-permute-start.1) | collective-permute-done | bytes 36896 | tf_op jit(solution)/shard_map/ppermute | solution.py:217
  10.9 0.0 collective-permute-done.refs_1_
  10.9 2.5 %collective-permute-start.5 = (f32[264,128]{1,0:T(8,128)S(1)}, f32[264,128]{1,0:T(8,128)S(1)}, u32[]{:S(2)}, u32[]{:S(2)}) collective-permute-start(f32[264,128]{1,0:T(8,128)S(1)} %stack.1.refs_0_), channel_id=1, source_target_pairs={{0,17},{1,16},{2,19},{3,18},{4,21},{5,20},{6,23},{7,22},{8,25},{9,... | collective-permute-start | bytes 405512 | tf_op jit(solution)/shard_map/ppermute | solution.py:217
  13.5 0.5 %collective-permute-start.4 = (f32[264,128]{1,0:T(8,128)S(1)}, f32[264,128]{1,0:T(8,128)S(1)}, u32[]{:S(2)}, u32[]{:S(2)}) collective-permute-start(f32[264,128]{1,0:T(8,128)S(1)} %stack.1.refs_0_), channel_id=1, source_target_pairs={{0,16},{1,17},{2,18},{3,19},{4,20},{5,21},{6,22},{7,23},{8,24},{9,... | collective-permute-start | bytes 405512 | tf_op jit(solution)/shard_map/ppermute | solution.py:217
  14.0 0.5 %collective-permute-start.3 = (f32[264,128]{1,0:T(8,128)S(1)}, f32[264,128]{1,0:T(8,128)S(1)}, u32[]{:S(2)}, u32[]{:S(2)}) collective-permute-start(f32[264,128]{1,0:T(8,128)S(1)} %stack.1.refs_0_), channel_id=1, source_target_pairs={{0,1},{1,0},{2,3},{3,2},{4,5},{5,4},{6,7},{7,6},{8,9},{9,8},{10,11... | collective-permute-start | bytes 405512 | tf_op jit(solution)/shard_map/ppermute | solution.py:217
  14.5 0.0 collective-permute-start.6
  14.5 2.8 %collective-permute-done.5.refs_3_ = f32[264,128]{1,0:T(8,128)S(1)} collective-permute-done((f32[264,128]{1,0:T(8,128)S(1)}, f32[264,128]{1,0:T(8,128)S(1)}, u32[]{:S(2)}, u32[]{:S(2)}) %collective-permute-start.5) | collective-permute-done | bytes 135200 | tf_op jit(solution)/shard_map/ppermute | solution.py:217
  17.3 0.0 collective-permute-start.9
  17.3 1.4 %collective-permute-done.4.refs_2_ = f32[264,128]{1,0:T(8,128)S(1)} collective-permute-done((f32[264,128]{1,0:T(8,128)S(1)}, f32[264,128]{1,0:T(8,128)S(1)}, u32[]{:S(2)}, u32[]{:S(2)}) %collective-permute-start.4) | collective-permute-done | bytes 135200 | tf_op jit(solution)/shard_map/ppermute | solution.py:217
  18.8 0.0 collective-permute-start.8
  18.8 0.2 collective-permute-done.3.refs_1_
  19.0 0.3 %collective-permute-start.7 = (f32[264,128]{1,0:T(8,128)S(1)}, f32[264,128]{1,0:T(8,128)S(1)}, u32[]{:S(2)}, u32[]{:S(2)}) collective-permute-start(f32[264,128]{1,0:T(8,128)S(1)} %collective-permute-done.3.refs_1_), channel_id=1, source_target_pairs={{0,8},{1,9},{2,10},{3,11},{4,12},{5,13},{6,14},{7,15},{8,0},{9,1},... | collective-permute-start | bytes 405512 | tf_op jit(solution)/shard_map/ppermute | solution.py:217
  19.3 0.0 collective-permute-done.6.refs_4_
  19.3 0.0 collective-permute-done.9.refs_7_
  19.3 0.8 %collective-permute-done.8.refs_6_ = f32[264,128]{1,0:T(8,128)S(1)} collective-permute-done((f32[264,128]{1,0:T(8,128)S(1)}, f32[264,128]{1,0:T(8,128)S(1)}, u32[]{:S(2)}, u32[]{:S(2)}) %collective-permute-start.8) | collective-permute-done | bytes 135200 | tf_op jit(solution)/shard_map/ppermute | solution.py:217
  20.1 0.2 collective-permute-done.7.refs_5_
  20.4 5.9 %schur.1 = f32[256,128]{1,0:T(8,128)} custom-call(f32[264,128]{1,0:T(8,128)S(1)} %stack.1.refs_0_, f32[264,128]{1,0:T(8,128)S(1)} %collective-permute-done.3.refs_1_, f32[264,128]{1,0:T(8,128)S(1)} %collective-permute-done.4.refs_2_, f32[264,128]{1,0:T(8,128)S(1)} %collective-permute-done.5.refs_3_, f32[264,128]{1,0:T(8,128)S(1)} %collective-permute-done.6.refs_4_, ...), custom_call_target="tpu_custom_call" | custom-call | tf_op jit(solution)/shard_map/schur/pallas_call | solution.py:239
  (1 shorter events, 0.0 us)
Async XLA Ops:
  0.9 7.1 %collective-permute-start.2 = (f32[72,128]{1,0:T(8,128)S(1)}, f32[72,128]{1,0:T(8,128)S(1)}, u32[]{:S(2)}, u32[]{:S(2)}) collective-permute-start(f32[72,128]{1,0:T(8,128)S(1)} %pack.1.refs_0_), channel_id=1, source_target_pairs={{0,6},{1,7},{2,4},{3,5},{4,2},{5,3},{6,0},{7,1},{8,14},{9,15},{10,... | collective-permute-start | bytes 110600 | tf_op jit(solution)/shard_map/ppermute | solution.py:217
  6.1 4.9 %collective-permute-start.1 = (f32[72,128]{1,0:T(8,128)S(1)}, f32[72,128]{1,0:T(8,128)S(1)}, u32[]{:S(2)}, u32[]{:S(2)}) collective-permute-start(f32[72,128]{1,0:T(8,128)S(1)} %pack.1.refs_0_), channel_id=1, source_target_pairs={{0,4},{1,5},{2,6},{3,7},{4,0},{5,1},{6,2},{7,3},{8,12},{9,13},{10,... | collective-permute-start | bytes 110600 | tf_op jit(solution)/shard_map/ppermute | solution.py:217
  6.1 4.9 %collective-permute-start = (f32[72,128]{1,0:T(8,128)S(1)}, f32[72,128]{1,0:T(8,128)S(1)}, u32[]{:S(2)}, u32[]{:S(2)}) collective-permute-start(f32[72,128]{1,0:T(8,128)S(1)} %pack.1.refs_0_), channel_id=1, source_target_pairs={{0,2},{1,3},{2,0},{3,1},{4,6},{5,7},{6,4},{7,5},{8,10},{9,11},{10,... | collective-permute-start | bytes 110600 | tf_op jit(solution)/shard_map/ppermute | solution.py:217
  10.9 6.4 %collective-permute-start.5 = (f32[264,128]{1,0:T(8,128)S(1)}, f32[264,128]{1,0:T(8,128)S(1)}, u32[]{:S(2)}, u32[]{:S(2)}) collective-permute-start(f32[264,128]{1,0:T(8,128)S(1)} %stack.1.refs_0_), channel_id=1, source_target_pairs={{0,17},{1,16},{2,19},{3,18},{4,21},{5,20},{6,23},{7,22},{8,25},{9,... | collective-permute-start | bytes 405512 | tf_op jit(solution)/shard_map/ppermute | solution.py:217
  13.5 5.3 %collective-permute-start.4 = (f32[264,128]{1,0:T(8,128)S(1)}, f32[264,128]{1,0:T(8,128)S(1)}, u32[]{:S(2)}, u32[]{:S(2)}) collective-permute-start(f32[264,128]{1,0:T(8,128)S(1)} %stack.1.refs_0_), channel_id=1, source_target_pairs={{0,16},{1,17},{2,18},{3,19},{4,20},{5,21},{6,22},{7,23},{8,24},{9,... | collective-permute-start | bytes 405512 | tf_op jit(solution)/shard_map/ppermute | solution.py:217
  14.0 5.0 %collective-permute-start.3 = (f32[264,128]{1,0:T(8,128)S(1)}, f32[264,128]{1,0:T(8,128)S(1)}, u32[]{:S(2)}, u32[]{:S(2)}) collective-permute-start(f32[264,128]{1,0:T(8,128)S(1)} %stack.1.refs_0_), channel_id=1, source_target_pairs={{0,1},{1,0},{2,3},{3,2},{4,5},{5,4},{6,7},{7,6},{8,9},{9,8},{10,11... | collective-permute-start | bytes 405512 | tf_op jit(solution)/shard_map/ppermute | solution.py:217
  14.5 4.8 %collective-permute-start.6 = (f32[264,128]{1,0:T(8,128)S(1)}, f32[264,128]{1,0:T(8,128)S(1)}, u32[]{:S(2)}, u32[]{:S(2)}) collective-permute-start(f32[264,128]{1,0:T(8,128)S(1)} %stack.1.refs_0_), channel_id=1, source_target_pairs={{0,8},{1,9},{2,10},{3,11},{4,12},{5,13},{6,14},{7,15},{8,0},{9,1},... | collective-permute-start | bytes 405512 | tf_op jit(solution)/shard_map/ppermute | solution.py:217
  17.3 2.0 %collective-permute-start.9 = (f32[264,128]{1,0:T(8,128)S(1)}, f32[264,128]{1,0:T(8,128)S(1)}, u32[]{:S(2)}, u32[]{:S(2)}) collective-permute-start(f32[264,128]{1,0:T(8,128)S(1)} %collective-permute-done.5.refs_3_), channel_id=1, source_target_pairs={{0,8},{1,9},{2,10},{3,11},{4,12},{5,13},{6,14},{7,15},{8,0},{9,1},... | collective-permute-start | bytes 405512 | tf_op jit(solution)/shard_map/ppermute | solution.py:217
  18.8 1.4 %collective-permute-start.8 = (f32[264,128]{1,0:T(8,128)S(1)}, f32[264,128]{1,0:T(8,128)S(1)}, u32[]{:S(2)}, u32[]{:S(2)}) collective-permute-start(f32[264,128]{1,0:T(8,128)S(1)} %collective-permute-done.4.refs_2_), channel_id=1, source_target_pairs={{0,8},{1,9},{2,10},{3,11},{4,12},{5,13},{6,14},{7,15},{8,0},{9,1},... | collective-permute-start | bytes 405512 | tf_op jit(solution)/shard_map/ppermute | solution.py:217
  19.0 1.4 %collective-permute-start.7 = (f32[264,128]{1,0:T(8,128)S(1)}, f32[264,128]{1,0:T(8,128)S(1)}, u32[]{:S(2)}, u32[]{:S(2)}) collective-permute-start(f32[264,128]{1,0:T(8,128)S(1)} %collective-permute-done.3.refs_1_), channel_id=1, source_target_pairs={{0,8},{1,9},{2,10},{3,11},{4,12},{5,13},{6,14},{7,15},{8,0},{9,1},... | collective-permute-start | bytes 405512 | tf_op jit(solution)/shard_map/ppermute | solution.py:217

commit v9 on v8

--- a/solution.py
+++ b/solution.py
@@ -63,18 +63,11 @@
         out_ref[nb : nb + plan.folded, g * plan.local : (g + 1) * plan.local] = piece
 
 
-def main_kernel(plan, n_in, *refs):
-    ins, out_hbm = refs[:n_in], refs[n_in]
-    out_ref, osem, misc, mat, left, zrow, zgot, xj, zj, pick, ivec, jvec, acc, idx, jdx, sem = refs[n_in + 1 :]
-    slot, cols, rows = plan.slot, plan.cols, plan.rows
-    slots, tiles, depth = plan.slots, plan.ni // LANES, plan.depth
+def place(plan, near, ins, misc, mat):
+    slot, cols = plan.slot, plan.cols
     me_r, me_c = lax.axis_index("row"), lax.axis_index("col")
-    chunk = pl.program_id(0)
     per = LANES // plan.wide
-    if per > 1:
-        mat[...] = jnp.zeros_like(mat)
     live_row = lax.broadcasted_iota(I32, (slot, LANES), 0) < plan.nb
-    near = [(core ^ i, k) for core in (0, 1) for i, k in plan.near]
     for ref, (ri, ci) in zip(ins, near):
         for n, (rf, cf) in enumerate(plan.far):
             r, c = me_r ^ (ri ^ rf), me_c ^ (ci ^ cf)
@@ -86,6 +79,28 @@
                 mat[r, span, :] = v
             else:
                 mat[r // per, span, :] += pltpu.roll(v, (r % per) * plan.wide, 1)
+
+
+def early_kernel(plan, near, *refs):
+    misc, mat = refs[-2:]
+    if LANES // plan.wide > 1:
+        mat[...] = jnp.zeros_like(mat)
+    place(plan, near, refs[:-2], misc, mat)
+
+
+def main_kernel(plan, near, *refs):
+    n_in = len(near)
+    ins, (out_hbm, misc, mat) = refs[:n_in], refs[n_in + 2 : n_in + 5]
+    out_ref, osem, left, zrow, zgot, xj, zj, pick, ivec, jvec, acc, idx, jdx, sem = refs[n_in + 5 :]
+    slot, cols, rows = plan.slot, plan.cols, plan.rows
+    slots, tiles, depth = plan.slots, plan.ni // LANES, plan.depth
+    me_r, me_c = lax.axis_index("row"), lax.axis_index("col")
+    chunk = pl.program_id(0)
+    per = LANES // plan.wide
+
+    @pl.when(chunk == 0)
+    def _():
+        place(plan, near, ins, misc, mat)
 
     lane = lax.broadcasted_iota(I32, (plan.folded, LANES), 1) // plan.local
 
@@ -168,6 +183,8 @@
                 both = v if both is None else jnp.where(group == e, v, both)
             base = (l * LANES + j) * n_tile
             zgot[base : base + 8, :] = both
+
+    def turn(l):
         for s in range(n_tile):
             v = zgot[pl.ds(l * LANES * n_tile + s, LANES, stride=n_tile), :]
             zj[pl.ds(s * LANES * slots + l, LANES, stride=slots), :] = v.T
@@ -177,8 +194,11 @@
         res = res[:depth] + res[depth:]
         for l in range(2):
             xj[pl.ds(2 * m + l, depth, stride=slots), :] = res[:, l * LANES : (l + 1) * LANES]
+    gather_rows(0)
     for l in range(slots):
-        gather_rows(l)
+        if l + 1 < slots:
+            gather_rows(l + 1)
+        turn(l)
     icopy.wait()
 
     def eight(tile_at, n):
@@ -236,17 +256,33 @@
 
 def schur_call(plan, stacks):
     n_tile = plan.depth // LANES
+    vmem = pl.BlockSpec(memory_space=pltpu.VMEM)
+    near = [(core ^ i, k) for core in (0, 1) for i, k in plan.near]
+    first = len(plan.near) + 1
+    held = (
+        jax.ShapeDtypeStruct((plan.rows * plan.cols, EXTRA, LANES), F32),
+        jax.ShapeDtypeStruct((n_tile, plan.depth, LANES), F32),
+    )
+    misc, mat = pl.pallas_call(
+        functools.partial(early_kernel, plan, near[:first]),
+        in_specs=[vmem] * first,
+        out_specs=(vmem, vmem),
+        out_shape=held,
+        cost_estimate=pl.CostEstimate(flops=1 << 22, bytes_accessed=1 << 20, transcendentals=0),
+        compiler_params=pltpu.CompilerParams(vmem_limit_bytes=8 << 20),
+        name="early",
+    )(*stacks[:first])
+    late = near[first:]
     return pl.pallas_call(
-        functools.partial(main_kernel, plan, len(stacks)),
+        functools.partial(main_kernel, plan, late),
         grid=(plan.nj // LANES,),
-        in_specs=[pl.BlockSpec(memory_space=pltpu.VMEM)] * len(stacks),
-        out_specs=pl.BlockSpec(memory_space=pltpu.HBM),
-        out_shape=jax.ShapeDtypeStruct((plan.ni, plan.nj), F32),
+        in_specs=[vmem] * (len(late) + 2),
+        out_specs=(pl.BlockSpec(memory_space=pltpu.HBM), vmem, vmem),
+        out_shape=(jax.ShapeDtypeStruct((plan.ni, plan.nj), F32), *held),
+        input_output_aliases={len(late): 1, len(late) + 1: 2},
         scratch_shapes=[
             pltpu.VMEM((plan.ni, LANES), F32),
             pltpu.SemaphoreType.DMA((plan.ni // LANES,)),
-            pltpu.VMEM((plan.rows * plan.cols, EXTRA, LANES), F32),
-            pltpu.VMEM((n_tile, plan.depth, LANES), F32),
             pltpu.VMEM((2 * plan.depth, plan.depth), BF16),
             pltpu.VMEM((plan.depth * n_tile + 16, LANES), F32),
             pltpu.VMEM((plan.slots * LANES * n_tile, LANES), F32),
@@ -262,7 +298,7 @@
         ],
         compiler_params=pltpu.CompilerParams(vmem_limit_bytes=24 << 20),
         name="schur",
-    )(*stacks)
+    )(*stacks[first:], misc, mat)[0]
 
 
 def shards(rows, cols, moment_x, zinv, positions, entry_count):

time: 26.4 us -> 26.3 us (level)
    pallas_call x1 -> x2, Pallas kernels: 5.88 us -> 5.9 us  [the longest x1 5.82 us: schur_call(): pl.pallas_call(functools.partial(main_kernel, plan, late), grid=(plan.nj...]
where the time goes in v9:
time: 26.3 us; the launch traced here: 26.2 us
  waiting for transfers between devices  9.71 us (37%)
  starting transfers between devices  9.61 us (37%)
  Pallas kernels  6.82 us (26%)
    ppermute x10, waiting for transfers between devices, send(): return lax.ppermute(v, ('row', 'col'), pairs)  9.71 us
    ppermute x10, starting transfers between devices, send(): return lax.ppermute(v, ('row', 'col'), pairs)  9.61 us
    pallas_call x1, Pallas kernels, schur_call(): pl.pallas_call(functools.partial(main_kernel, plan, late), grid=(plan.nj...  5.82 us
    pallas_call x1, Pallas kernels, shards(): pl.pallas_call(functools.partial(pack_kernel, plan), in_specs=[pl.BlockSp...  0.91 us
  transfers between devices with their start and end apart: 10, of which 7 were waited for; matrix products, arithmetic and copies ran while one was open for 0% of the time, Pallas kernels for 0%

profile of v9, /device:TPU:0, one launch (start us, length us, event | category | flops | bytes accessed | tf_op | source)
XLA Modules:
  0.0 26.2 jit_solution(2658775326771517965)
XLA Ops:
  0.0 0.9 %pack.1.refs_0_ = f32[72,128]{1,0:T(8,128)S(1)} custom-call(f32[62,124]{1,0:T(8,128)} %bitcast.4, f32[62,124]{1,0:T(8,128)} %bitcast.5, s32[16,32]{1,0:T(8,128)} %bitcast.6, s32[1,32]{1,0:T(1,128)} %bitcast.7), custom_call_target="tpu_custom_call" | custom-call | tf_op jit(solution)/shard_map/pack/pallas_call | solution.py:307
  0.9 5.1 %collective-permute-start.2 = (f32[72,128]{1,0:T(8,128)S(1)}, f32[72,128]{1,0:T(8,128)S(1)}, u32[]{:S(2)}, u32[]{:S(2)}) collective-permute-start(f32[72,128]{1,0:T(8,128)S(1)} %pack.1.refs_0_), channel_id=1, source_target_pairs={{0,6},{1,7},{2,4},{3,5},{4,2},{5,3},{6,0},{7,1},{8,14},{9,15},{10,... | collective-permute-start | bytes 110600 | tf_op jit(solution)/shard_map/ppermute | solution.py:237
  6.1 0.0 collective-permute-start.1
  6.1 0.6 %collective-permute-start = (f32[72,128]{1,0:T(8,128)S(1)}, f32[72,128]{1,0:T(8,128)S(1)}, u32[]{:S(2)}, u32[]{:S(2)}) collective-permute-start(f32[72,128]{1,0:T(8,128)S(1)} %pack.1.refs_0_), channel_id=1, source_target_pairs={{0,2},{1,3},{2,0},{3,1},{4,6},{5,7},{6,4},{7,5},{8,10},{9,11},{10,... | collective-permute-start | bytes 110600 | tf_op jit(solution)/shard_map/ppermute | solution.py:237
  6.7 1.3 %collective-permute-done.2.refs_3_ = f32[72,128]{1,0:T(8,128)S(1)} collective-permute-done((f32[72,128]{1,0:T(8,128)S(1)}, f32[72,128]{1,0:T(8,128)S(1)}, u32[]{:S(2)}, u32[]{:S(2)}) %collective-permute-start.2) | collective-permute-done | bytes 36896 | tf_op jit(solution)/shard_map/ppermute | solution.py:237
  8.0 2.9 %collective-permute-done.1.refs_2_ = f32[72,128]{1,0:T(8,128)S(1)} collective-permute-done((f32[72,128]{1,0:T(8,128)S(1)}, f32[72,128]{1,0:T(8,128)S(1)}, u32[]{:S(2)}, u32[]{:S(2)}) %collective-permute-start.1) | collective-permute-done | bytes 36896 | tf_op jit(solution)/shard_map/ppermute | solution.py:237
  10.9 0.0 collective-permute-done.refs_1_
  10.9 2.5 %collective-permute-start.7 = (f32[264,128]{1,0:T(8,128)S(1)}, f32[264,128]{1,0:T(8,128)S(1)}, u32[]{:S(2)}, u32[]{:S(2)}) collective-permute-start(f32[264,128]{1,0:T(8,128)S(1)} %stack.1.refs_0_), channel_id=1, source_target_pairs={{0,17},{1,16},{2,19},{3,18},{4,21},{5,20},{6,23},{7,22},{8,25},{9,... | collective-permute-start | bytes 405512 | tf_op jit(solution)/shard_map/ppermute | solution.py:237
  13.5 0.5 %collective-permute-start.5 = (f32[264,128]{1,0:T(8,128)S(1)}, f32[264,128]{1,0:T(8,128)S(1)}, u32[]{:S(2)}, u32[]{:S(2)}) collective-permute-start(f32[264,128]{1,0:T(8,128)S(1)} %stack.1.refs_0_), channel_id=1, source_target_pairs={{0,16},{1,17},{2,18},{3,19},{4,20},{5,21},{6,22},{7,23},{8,24},{9,... | collective-permute-start | bytes 405512 | tf_op jit(solution)/shard_map/ppermute | solution.py:237
  14.0 0.5 %collective-permute-start.3 = (f32[264,128]{1,0:T(8,128)S(1)}, f32[264,128]{1,0:T(8,128)S(1)}, u32[]{:S(2)}, u32[]{:S(2)}) collective-permute-start(f32[264,128]{1,0:T(8,128)S(1)} %stack.1.refs_0_), channel_id=1, source_target_pairs={{0,1},{1,0},{2,3},{3,2},{4,5},{5,4},{6,7},{7,6},{8,9},{9,8},{10,11... | collective-permute-start | bytes 405512 | tf_op jit(solution)/shard_map/ppermute | solution.py:237
  14.5 0.0 collective-permute-start.9
  14.5 2.8 %collective-permute-done.7.refs_3_ = f32[264,128]{1,0:T(8,128)S(1)} collective-permute-done((f32[264,128]{1,0:T(8,128)S(1)}, f32[264,128]{1,0:T(8,128)S(1)}, u32[]{:S(2)}, u32[]{:S(2)}) %collective-permute-start.7) | collective-permute-done | bytes 135200 | tf_op jit(solution)/shard_map/ppermute | solution.py:237
  17.3 0.0 collective-permute-start.8
  17.3 1.4 %collective-permute-done.5.refs_2_ = f32[264,128]{1,0:T(8,128)S(1)} collective-permute-done((f32[264,128]{1,0:T(8,128)S(1)}, f32[264,128]{1,0:T(8,128)S(1)}, u32[]{:S(2)}, u32[]{:S(2)}) %collective-permute-start.5) | collective-permute-done | bytes 135200 | tf_op jit(solution)/shard_map/ppermute | solution.py:237
  18.8 0.0 collective-permute-start.6
  18.8 0.2 collective-permute-done.3.refs_1_
  19.0 0.3 %collective-permute-start.4 = (f32[264,128]{1,0:T(8,128)S(1)}, f32[264,128]{1,0:T(8,128)S(1)}, u32[]{:S(2)}, u32[]{:S(2)}) collective-permute-start(f32[264,128]{1,0:T(8,128)S(1)} %collective-permute-done.3.refs_1_), channel_id=1, source_target_pairs={{0,8},{1,9},{2,10},{3,11},{4,12},{5,13},{6,14},{7,15},{8,0},{9,1},... | collective-permute-start | bytes 405512 | tf_op jit(solution)/shard_map/ppermute | solution.py:237
  19.3 0.0 collective-permute-done.9.refs_4_
  19.3 0.1 early.1
  19.3 0.0 collective-permute-done.8.refs_2_
  19.4 0.7 %collective-permute-done.6.refs_1_ = f32[264,128]{1,0:T(8,128)S(1)} collective-permute-done((f32[264,128]{1,0:T(8,128)S(1)}, f32[264,128]{1,0:T(8,128)S(1)}, u32[]{:S(2)}, u32[]{:S(2)}) %collective-permute-start.6) | collective-permute-done | bytes 135200 | tf_op jit(solution)/shard_map/ppermute | solution.py:237
  20.1 0.2 collective-permute-done.4.refs_0_
  20.4 5.8 %schur.1 = (f32[256,128]{1,0:T(8,128)}, f32[32,8,128]{2,1,0:T(8,128)S(1)}, f32[4,512,128]{2,1,0:T(8,128)S(1)}) custom-call(f32[264,128]{1,0:T(8,128)S(1)} %collective-permute-done.4.refs_0_, f32[264,128]{1,0:T(8,128)S(1)} %collective-permute-done.6.refs_1_, ...), custom_call_target="tpu_custom_call", output_to_operand_aliasing={{1}: (3, {}), {2}: (4, {})} | custom-call | tf_op jit(solution)/shard_map/schur/pallas_call | solution.py:276
  (1 shorter events, 0.0 us)
Async XLA Ops:
  0.9 7.1 %collective-permute-start.2 = (f32[72,128]{1,0:T(8,128)S(1)}, f32[72,128]{1,0:T(8,128)S(1)}, u32[]{:S(2)}, u32[]{:S(2)}) collective-permute-start(f32[72,128]{1,0:T(8,128)S(1)} %pack.1.refs_0_), channel_id=1, source_target_pairs={{0,6},{1,7},{2,4},{3,5},{4,2},{5,3},{6,0},{7,1},{8,14},{9,15},{10,... | collective-permute-start | bytes 110600 | tf_op jit(solution)/shard_map/ppermute | solution.py:237
  6.1 4.9 %collective-permute-start.1 = (f32[72,128]{1,0:T(8,128)S(1)}, f32[72,128]{1,0:T(8,128)S(1)}, u32[]{:S(2)}, u32[]{:S(2)}) collective-permute-start(f32[72,128]{1,0:T(8,128)S(1)} %pack.1.refs_0_), channel_id=1, source_target_pairs={{0,4},{1,5},{2,6},{3,7},{4,0},{5,1},{6,2},{7,3},{8,12},{9,13},{10,... | collective-permute-start | bytes 110600 | tf_op jit(solution)/shard_map/ppermute | solution.py:237
  6.1 4.9 %collective-permute-start = (f32[72,128]{1,0:T(8,128)S(1)}, f32[72,128]{1,0:T(8,128)S(1)}, u32[]{:S(2)}, u32[]{:S(2)}) collective-permute-start(f32[72,128]{1,0:T(8,128)S(1)} %pack.1.refs_0_), channel_id=1, source_target_pairs={{0,2},{1,3},{2,0},{3,1},{4,6},{5,7},{6,4},{7,5},{8,10},{9,11},{10,... | collective-permute-start | bytes 110600 | tf_op jit(solution)/shard_map/ppermute | solution.py:237
  10.9 6.4 %collective-permute-start.7 = (f32[264,128]{1,0:T(8,128)S(1)}, f32[264,128]{1,0:T(8,128)S(1)}, u32[]{:S(2)}, u32[]{:S(2)}) collective-permute-start(f32[264,128]{1,0:T(8,128)S(1)} %stack.1.refs_0_), channel_id=1, source_target_pairs={{0,17},{1,16},{2,19},{3,18},{4,21},{5,20},{6,23},{7,22},{8,25},{9,... | collective-permute-start | bytes 405512 | tf_op jit(solution)/shard_map/ppermute | solution.py:237
  13.5 5.3 %collective-permute-start.5 = (f32[264,128]{1,0:T(8,128)S(1)}, f32[264,128]{1,0:T(8,128)S(1)}, u32[]{:S(2)}, u32[]{:S(2)}) collective-permute-start(f32[264,128]{1,0:T(8,128)S(1)} %stack.1.refs_0_), channel_id=1, source_target_pairs={{0,16},{1,17},{2,18},{3,19},{4,20},{5,21},{6,22},{7,23},{8,24},{9,... | collective-permute-start | bytes 405512 | tf_op jit(solution)/shard_map/ppermute | solution.py:237
  14.0 5.0 %collective-permute-start.3 = (f32[264,128]{1,0:T(8,128)S(1)}, f32[264,128]{1,0:T(8,128)S(1)}, u32[]{:S(2)}, u32[]{:S(2)}) collective-permute-start(f32[264,128]{1,0:T(8,128)S(1)} %stack.1.refs_0_), channel_id=1, source_target_pairs={{0,1},{1,0},{2,3},{3,2},{4,5},{5,4},{6,7},{7,6},{8,9},{9,8},{10,11... | collective-permute-start | bytes 405512 | tf_op jit(solution)/shard_map/ppermute | solution.py:237
  14.5 4.8 %collective-permute-start.9 = (f32[264,128]{1,0:T(8,128)S(1)}, f32[264,128]{1,0:T(8,128)S(1)}, u32[]{:S(2)}, u32[]{:S(2)}) collective-permute-start(f32[264,128]{1,0:T(8,128)S(1)} %stack.1.refs_0_), channel_id=1, source_target_pairs={{0,8},{1,9},{2,10},{3,11},{4,12},{5,13},{6,14},{7,15},{8,0},{9,1},... | collective-permute-start | bytes 405512 | tf_op jit(solution)/shard_map/ppermute | solution.py:237
  17.3 2.0 %collective-permute-start.8 = (f32[264,128]{1,0:T(8,128)S(1)}, f32[264,128]{1,0:T(8,128)S(1)}, u32[]{:S(2)}, u32[]{:S(2)}) collective-permute-start(f32[264,128]{1,0:T(8,128)S(1)} %collective-permute-done.7.refs_3_), channel_id=1, source_target_pairs={{0,8},{1,9},{2,10},{3,11},{4,12},{5,13},{6,14},{7,15},{8,0},{9,1},... | collective-permute-start | bytes 405512 | tf_op jit(solution)/shard_map/ppermute | solution.py:237
  18.8 1.4 %collective-permute-start.6 = (f32[264,128]{1,0:T(8,128)S(1)}, f32[264,128]{1,0:T(8,128)S(1)}, u32[]{:S(2)}, u32[]{:S(2)}) collective-permute-start(f32[264,128]{1,0:T(8,128)S(1)} %collective-permute-done.5.refs_2_), channel_id=1, source_target_pairs={{0,8},{1,9},{2,10},{3,11},{4,12},{5,13},{6,14},{7,15},{8,0},{9,1},... | collective-permute-start | bytes 405512 | tf_op jit(solution)/shard_map/ppermute | solution.py:237
  19.0 1.4 %collective-permute-start.4 = (f32[264,128]{1,0:T(8,128)S(1)}, f32[264,128]{1,0:T(8,128)S(1)}, u32[]{:S(2)}, u32[]{:S(2)}) collective-permute-start(f32[264,128]{1,0:T(8,128)S(1)} %collective-permute-done.3.refs_1_), channel_id=1, source_target_pairs={{0,8},{1,9},{2,10},{3,11},{4,12},{5,13},{6,14},{7,15},{8,0},{9,1},... | collective-permute-start | bytes 405512 | tf_op jit(solution)/shard_map/ppermute | solution.py:237
